TPU v7x, 64 devices: a 2x2x8 block of a 4x4x8 slice. The times are simulated.
64 devices in a mesh: part: 4 (over x, y), dp: 16 (over z, core).
Axes of the slice: x: 2, y: 2, z: 8, core: 2. Of those that a mesh axis runs over, the one named last changes fastest.
The devices are a block of a 4x4x8 slice.
Arguments:
- x: bfloat16 [512, 1024], P(('part', 'dp')), parts along dimension 0
- positions: int32 [512], P(('part', 'dp')), parts along dimension 0
- k_cache: bfloat16 [2, 512, 128, 8, 128], P(None, ('part', 'dp')), parts along dimension 1
- v_cache: bfloat16 [2, 512, 128, 8, 128], P(None, ('part', 'dp')), parts along dimension 1
- attn_norm: bfloat16 [2, 1024], replicated
- w_q: bfloat16 [2, 1024, 2048], P(None, 'dp')
- w_k: bfloat16 [2, 1024, 1024], P(None, 'dp')
- w_v: bfloat16 [2, 1024, 1024], P(None, 'dp')
- q_norm: bfloat16 [2, 128], replicated
- k_norm: bfloat16 [2, 128], replicated
- w_o: bfloat16 [2, 2048, 1024], P(None, 'dp')
- mlp_norm: bfloat16 [2, 1024], replicated
- w_gate: bfloat16 [2, 1024, 3072], P(None, 'dp')
- w_up: bfloat16 [2, 1024, 3072], P(None, 'dp')
- w_down: bfloat16 [2, 3072, 1024], P(None, 'dp')
Outputs:
- output 1: bfloat16 [512, 1024], P(('part', 'dp')), parts along dimension 0
- output 2: bfloat16 [2, 512, 128, 8, 128], P(None, ('part', 'dp')), parts along dimension 1
- output 3: bfloat16 [2, 512, 128, 8, 128], P(None, ('part', 'dp')), parts along dimension 1
There are 4 independent parts. A program takes and returns all parts, laid end to end along the dimension named above; an argument that names none is the same for every part.
All inputs are finite; a program needn't handle non-finite values.
Results may differ from a plain program's by a relative error of at most 0.0179508.
Values are sent between devices in bfloat16 or wider.
A program may use at most 768 MiB of HBM per device.

v0:
```python
import jax
import jax.numpy as jnp
from jax import lax
from jax.sharding import PartitionSpec as P

HEAD_DIM = 128
RMS_EPS = 1e-6
ROPE_THETA = 1000000.0


def rms_norm(values, gain_vec):
    values = values.astype(jnp.float32)
    inv_rms = lax.rsqrt(jnp.mean(values * values, axis=-1, keepdims=True) + RMS_EPS)
    return values * inv_rms * gain_vec.astype(jnp.float32)


def rope_tables(positions):
    inv_freq = ROPE_THETA ** (-jnp.arange(0, HEAD_DIM, 2).astype(jnp.float32) / HEAD_DIM)
    angles = positions.astype(jnp.float32)[:, None] * inv_freq[None, :]
    angles = jnp.concatenate([angles, angles], axis=-1)[:, None, :]
    return jnp.cos(angles), jnp.sin(angles)


def apply_rope(values, cos_tab, sin_tab):
    half_dim = HEAD_DIM // 2
    rotated = jnp.concatenate([-values[..., half_dim:], values[..., :half_dim]], axis=-1)
    return values * cos_tab + rotated * sin_tab


def attend_layer(q_proj, k_proj, v_proj, cos_tab, sin_tab, live_mask, k_layer, v_layer, q_gain, k_gain):
    tok_count = k_layer.shape[0]
    slot_count = k_layer.shape[1]
    kv_heads = k_layer.shape[2]
    q_heads = q_proj.shape[1] // HEAD_DIM
    q_rot = apply_rope(rms_norm(q_proj.reshape(tok_count, q_heads, HEAD_DIM), q_gain), cos_tab, sin_tab)
    q_grp = q_rot.astype(jnp.bfloat16).reshape(tok_count, kv_heads, q_heads // kv_heads, HEAD_DIM)
    k_rot = apply_rope(rms_norm(k_proj.reshape(tok_count, kv_heads, HEAD_DIM), k_gain), cos_tab, sin_tab).astype(jnp.bfloat16)
    v_new = v_proj.reshape(tok_count, kv_heads, HEAD_DIM)
    score_scale = HEAD_DIM ** -0.5
    old_scores = jnp.einsum("nkgd,ntkd->nkgt", q_grp, k_layer, preferred_element_type=jnp.float32) * score_scale
    old_scores = jnp.where(live_mask, old_scores, -jnp.inf)
    new_score = jnp.einsum("nkgd,nkd->nkg", q_grp, k_rot, preferred_element_type=jnp.float32) * score_scale
    scores = jnp.concatenate([old_scores, new_score[..., None]], axis=-1)
    attn_prob = jax.nn.softmax(scores, axis=-1).astype(jnp.bfloat16)
    attn_mix = jnp.einsum("nkgt,ntkd->nkgd", attn_prob[..., :slot_count], v_layer, preferred_element_type=jnp.float32)
    attn_mix = attn_mix + attn_prob[..., slot_count:].astype(jnp.float32) * v_new[:, :, None, :].astype(jnp.float32)
    attn_out = attn_mix.astype(jnp.bfloat16).reshape(tok_count, q_heads * HEAD_DIM)
    return attn_out, k_rot, v_new


def solution(mesh):
    batch_axes = ("part", "dp")
    act_spec = P(batch_axes, None)
    cache_spec = P(None, batch_axes, None, None, None)
    mat_spec = P(None, "dp", None)
    gain_spec = P(None, None)
    in_specs = (act_spec, P(batch_axes), cache_spec, cache_spec, gain_spec, mat_spec, mat_spec, mat_spec, gain_spec, gain_spec, mat_spec, gain_spec, mat_spec, mat_spec, mat_spec)
    out_specs = (act_spec, cache_spec, cache_spec)

    def gather_rows(shard):
        return lax.all_gather(shard, "dp", axis=0, tiled=True)

    def device_fn(x, positions, k_cache, v_cache, attn_norm, w_q, w_k, w_v, q_norm, k_norm, w_o, mlp_norm, w_gate, w_up, w_down):
        cos_tab, sin_tab = rope_tables(positions)
        slot_ids = jnp.arange(k_cache.shape[2])
        live_mask = (slot_ids[None, :] < positions[:, None])[:, None, None, :]
        hidden_x = x
        k_rows = []
        v_rows = []
        for layer_idx in range(k_cache.shape[0]):
            hidden = rms_norm(hidden_x, attn_norm[layer_idx]).astype(jnp.bfloat16)
            q_proj = jnp.dot(hidden, gather_rows(w_q[layer_idx]), preferred_element_type=jnp.float32).astype(jnp.bfloat16)
            k_proj = jnp.dot(hidden, gather_rows(w_k[layer_idx]), preferred_element_type=jnp.float32).astype(jnp.bfloat16)
            v_proj = jnp.dot(hidden, gather_rows(w_v[layer_idx]), preferred_element_type=jnp.float32).astype(jnp.bfloat16)
            attn_out, k_rot, v_new = attend_layer(q_proj, k_proj, v_proj, cos_tab, sin_tab, live_mask, k_cache[layer_idx], v_cache[layer_idx], q_norm[layer_idx], k_norm[layer_idx])
            x_mid = (hidden_x.astype(jnp.float32) + jnp.dot(attn_out, gather_rows(w_o[layer_idx]), preferred_element_type=jnp.float32)).astype(jnp.bfloat16)
            hidden2 = rms_norm(x_mid, mlp_norm[layer_idx]).astype(jnp.bfloat16)
            gate_val = jnp.dot(hidden2, gather_rows(w_gate[layer_idx]), preferred_element_type=jnp.float32)
            up_val = jnp.dot(hidden2, gather_rows(w_up[layer_idx]), preferred_element_type=jnp.float32)
            act_in = (jax.nn.silu(gate_val) * up_val).astype(jnp.bfloat16)
            hidden_x = (x_mid.astype(jnp.float32) + jnp.dot(act_in, gather_rows(w_down[layer_idx]), preferred_element_type=jnp.float32)).astype(jnp.bfloat16)
            k_rows.append(k_rot)
            v_rows.append(v_new)
        slot_hit = (slot_ids[None, :] == positions[:, None])[None, :, :, None, None]
        k_out = jnp.where(slot_hit, jnp.stack(k_rows)[:, :, None], k_cache)
        v_out = jnp.where(slot_hit, jnp.stack(v_rows)[:, :, None], v_cache)
        return hidden_x, k_out, v_out

    return jax.shard_map(device_fn, mesh=mesh, in_specs=in_specs, out_specs=out_specs, check_vma=False)
```

profile of v0, /device:TPU:21, one launch (start us, length us, event | category | flops | bytes accessed | tf_op | source)
XLA Modules:
  0.0 586.2 jit_solution(14022387416175398382)
XLA Ops:
  7.3 1.8 fusion.199
  9.2 1.7 fusion.198
  11.0 1.9 fusion.197
  13.1 0.8 fusion.196
  14.0 0.9 fusion.193
  15.1 0.9 fusion.194
  16.2 0.9 fusion.195
  17.3 0.7 all-gather.45.cloned.1.call-update
  18.1 0.7 all-gather.47.cloned.1.call-update
  18.9 0.6 all-gather.43.cloned.1.call-update
  19.6 0.7 all-gather.49.cloned.1.call-update
  20.3 0.6 all-gather.51.cloned.1.call-update
  21.0 0.7 all-gather.53.cloned.1.call-update
  22.9 4.1 fusion.192
  26.9 2.4 fusion.191
  29.4 21.6 %all-gather.31.cloned.1.call-done = bf16[1,1024,1024]{2,1,0:T(8,128)(2,1)} async-done(((bf16[1,64,1024]{2,1,0:T(8,128)(2,1)}), bf16[1,1024,1024]{2,1,0:T(8,128)(2,1)}) %all-gather.31.cloned.1.call-update) | async-done | bytes 2097168 | tf_op jit(solution)/shard_map/all_gather | solution.py:61
  50.9 2.1 fusion.160
  53.2 34.2 %all-gather.33.cloned.1.call-done = bf16[1,1024,1024]{2,1,0:T(8,128)(2,1)} async-done(((bf16[1,64,1024]{2,1,0:T(8,128)(2,1)}), bf16[1,1024,1024]{2,1,0:T(8,128)(2,1)}) %all-gather.33.cloned.1.call-update) | async-done | bytes 2097168 | tf_op jit(solution)/shard_map/all_gather | solution.py:61
  87.4 2.0 bitcast_convert_fusion.1
  89.5 36.8 %all-gather.29.cloned.1.call-done = bf16[1,1024,2048]{2,1,0:T(8,128)(2,1)} async-done(((bf16[1,64,2048]{2,1,0:T(8,128)(2,1)}), bf16[1,1024,2048]{2,1,0:T(8,128)(2,1)}) %all-gather.29.cloned.1.call-update) | async-done | bytes 4194320 | tf_op jit(solution)/shard_map/all_gather | solution.py:61
  126.3 2.9 fusion.135
  130.1 1.3 fusion.200
  132.1 0.7 copy.105
  133.6 2.2 fusion.63
  135.9 28.9 %all-gather.35.cloned.1.call-done = bf16[1,2048,1024]{2,1,0:T(8,128)(2,1)} async-done(((bf16[1,128,1024]{2,1,0:T(8,128)(2,1)}), bf16[1,2048,1024]{2,1,0:T(8,128)(2,1)}) %all-gather.35.cloned.1.call-update) | async-done | bytes 4194320 | tf_op jit(solution)/shard_map/all_gather | solution.py:61
  164.7 3.0 multiply_reduce_fusion.2
  167.7 39.7 %all-gather.37.cloned.1.call-done = bf16[1,1024,3072]{2,1,0:T(8,128)(2,1)} async-done(((bf16[1,64,3072]{2,1,0:T(8,128)(2,1)}), bf16[1,1024,3072]{2,1,0:T(8,128)(2,1)}) %all-gather.37.cloned.1.call-update) | async-done | bytes 6291472 | tf_op jit(solution)/shard_map/all_gather | solution.py:61
  207.3 3.7 fusion.10
  211.1 39.3 %all-gather.39.cloned.1.call-done = bf16[1,1024,3072]{2,1,0:T(8,128)(2,1)} async-done(((bf16[1,64,3072]{2,1,0:T(8,128)(2,1)}), bf16[1,1024,3072]{2,1,0:T(8,128)(2,1)}) %all-gather.39.cloned.1.call-update) | async-done | bytes 6291472 | tf_op jit(solution)/shard_map/all_gather | solution.py:61
  250.4 43.2 %all-gather.41.cloned.1.call-done = bf16[1,3072,1024]{2,1,0:T(8,128)(2,1)} async-done(((bf16[1,192,1024]{2,1,0:T(8,128)(2,1)}), bf16[1,3072,1024]{2,1,0:T(8,128)(2,1)}) %all-gather.41.cloned.1.call-update) | async-done | bytes 6291472 | tf_op jit(solution)/shard_map/all_gather | solution.py:61
  293.6 6.5 %multiply_reduce_fusion.1 = (f32[8]{0:T(128)S(1)}, f32[8,1024]{1,0:T(8,128)S(1)}) fusion(f32[8,1024]{1,0:T(8,128)S(1)} %get-tuple-element.62, bf16[1,3072,1024]{2,1,0:T(8,128)(2,1)} %all-gather.41.cloned.1.call-done, bf16[1,1024,3072]{2,1,0:T(8,128)(2,1)} %all-gather.39.cloned.1.call-done, f32[8,3072]{1,0:T(8,128)S(1)} %fusion.10, f32[1024]{0:T(1024)S(1)} %bitcast.285, ...), kind=kOutput, calls=%fused_computation.149 | convolution fusion | flops 100876280 | bytes 12750912 | tf_op jit(solution)/shard_map/dot_general | solution.py:81
  300.1 29.9 %all-gather.45.cloned.1.call-done = bf16[1,1024,1024]{2,1,0:T(8,128)(2,1)} async-done(((bf16[1,64,1024]{2,1,0:T(8,128)(2,1)}), bf16[1,1024,1024]{2,1,0:T(8,128)(2,1)}) %all-gather.45.cloned.1.call-update) | async-done | bytes 2097168 | tf_op jit(solution)/shard_map/all_gather | solution.py:61
  330.0 2.0 fusion.158
  332.4 34.1 %all-gather.47.cloned.1.call-done = bf16[1,1024,1024]{2,1,0:T(8,128)(2,1)} async-done(((bf16[1,64,1024]{2,1,0:T(8,128)(2,1)}), bf16[1,1024,1024]{2,1,0:T(8,128)(2,1)}) %all-gather.47.cloned.1.call-update) | async-done | bytes 2097168 | tf_op jit(solution)/shard_map/all_gather | solution.py:61
  366.5 2.0 bitcast_convert_fusion
  368.5 36.8 %all-gather.43.cloned.1.call-done = bf16[1,1024,2048]{2,1,0:T(8,128)(2,1)} async-done(((bf16[1,64,2048]{2,1,0:T(8,128)(2,1)}), bf16[1,1024,2048]{2,1,0:T(8,128)(2,1)}) %all-gather.43.cloned.1.call-update) | async-done | bytes 4194320 | tf_op jit(solution)/shard_map/all_gather | solution.py:61
  405.3 2.9 fusion.133
  409.1 1.3 fusion.203
  411.1 0.7 copy.120
  412.8 2.2 fusion.62
  415.0 28.8 %all-gather.49.cloned.1.call-done = bf16[1,2048,1024]{2,1,0:T(8,128)(2,1)} async-done(((bf16[1,128,1024]{2,1,0:T(8,128)(2,1)}), bf16[1,2048,1024]{2,1,0:T(8,128)(2,1)}) %all-gather.49.cloned.1.call-update) | async-done | bytes 4194320 | tf_op jit(solution)/shard_map/all_gather | solution.py:61
  443.8 3.0 multiply_reduce_fusion
  446.8 39.7 %all-gather.51.cloned.1.call-done = bf16[1,1024,3072]{2,1,0:T(8,128)(2,1)} async-done(((bf16[1,64,3072]{2,1,0:T(8,128)(2,1)}), bf16[1,1024,3072]{2,1,0:T(8,128)(2,1)}) %all-gather.51.cloned.1.call-update) | async-done | bytes 6291472 | tf_op jit(solution)/shard_map/all_gather | solution.py:61
  486.5 3.9 fusion.4
  490.5 6.4 %broadcast_select_fusion = (bf16[2,8,128,8,128]{4,3,2,1,0:T(8,128)(2,1)}, bf16[2,8,128,8,128]{4,3,2,1,0:T(8,128)(2,1)}) fusion(bf16[2,8,128,8,128]{4,3,2,1,0:T(8,128)(2,1)} %param.18, pred[8,128]{1,0:T(8,128)(4,1)S(1)} %get-tuple-element.47, bf16[2,8,8,128]{3,2,1,0:T(8,128)(2,1)S(1)} %copy.126, bf16[2,8,128,8,128]{4,3,2,1,0:T(8,128)(2,1)S(1)} %copy-done, ...), kind=kLoop, calls=%fused_computation.20 | loop fusion | flops 4194304 | bytes 16843776 | tf_op jit(solution)/shard_map/jit(_where)/select_n | solution.py:86
  496.8 32.8 %all-gather.53.cloned.1.call-done = bf16[1,1024,3072]{2,1,0:T(8,128)(2,1)} async-done(((bf16[1,64,3072]{2,1,0:T(8,128)(2,1)}), bf16[1,1024,3072]{2,1,0:T(8,128)(2,1)}) %all-gather.53.cloned.1.call-update) | async-done | bytes 6291472 | tf_op jit(solution)/shard_map/all_gather | solution.py:61
  529.6 43.0 %all-gather.55.cloned.1.call-done = bf16[1,3072,1024]{2,1,0:T(8,128)(2,1)} async-done(((bf16[1,192,1024]{2,1,0:T(8,128)(2,1)}), bf16[1,3072,1024]{2,1,0:T(8,128)(2,1)}) %all-gather.55.cloned.1.call-update) | async-done | bytes 6291472 | tf_op jit(solution)/shard_map/all_gather | solution.py:61
  572.7 7.0 %fusion.76 = bf16[8,1024]{1,0:T(8,128)(2,1)} fusion(f32[8,1024]{1,0:T(8,128)S(1)} %get-tuple-element.74, bf16[1,3072,1024]{2,1,0:T(8,128)(2,1)} %all-gather.55.cloned.1.call-done, bf16[1,1024,3072]{2,1,0:T(8,128)(2,1)} %all-gather.53.cloned.1.call-done, f32[8,3072]{1,0:T(8,128)S(1)} %fusion.4, f32[1024]{0:T(1024)S(1)} %bitcast.283, f32[8]{0:T(128)S(1)} %add_rsqrt_fusion.4), kind=kOutput, calls=%fused_computation.58 | convolution fusion | flops 100851712 | bytes 12734496 | tf_op jit(solution)/shard_map/dot_general | solution.py:81
  (118 shorter events, 7.9 us)
Async XLA Ops:
  7.2 5.9 %copy-start.6 = (bf16[2,128,1024]{2,1,0:T(8,128)(2,1)S(1)}, bf16[2,128,1024]{2,1,0:T(8,128)(2,1)}, u32[]{:S(2)}) copy-start(bf16[2,128,1024]{2,1,0:T(8,128)(2,1)} %param.25) | copy-start | bytes 1572868
  7.2 6.8 %copy-start.3 = (bf16[2,64,3072]{2,1,0:T(8,128)(2,1)S(1)}, bf16[2,64,3072]{2,1,0:T(8,128)(2,1)}, u32[]{:S(2)}) copy-start(bf16[2,64,3072]{2,1,0:T(8,128)(2,1)} %param.27) | copy-start | bytes 2359300
  7.2 43.8 %all-gather.31.cloned.1.call-start = ((), (), s32[]{:S(2)}) async-start(), calls=%async_computation.1 | async-start | bytes 2228224 | tf_op jit(solution)/shard_map/all_gather | solution.py:61
  9.1 78.3 %all-gather.33.cloned.1.call-start = ((), (), s32[]{:S(2)}) async-start(), calls=%async_computation.2 | async-start | bytes 2228224 | tf_op jit(solution)/shard_map/all_gather | solution.py:61
  10.9 4.2 copy-start.4
  10.9 115.4 %all-gather.29.cloned.1.call-start = ((), (), s32[]{:S(2)}) async-start(), calls=%async_computation | async-start | bytes 4456448 | tf_op jit(solution)/shard_map/all_gather | solution.py:61
  13.0 151.7 %all-gather.35.cloned.1.call-start = ((), (), s32[]{:S(2)}) async-start(), calls=%async_computation.3 | async-start | bytes 4456448 | tf_op jit(solution)/shard_map/all_gather | solution.py:61
  13.9 2.3 copy-start.5
  14.0 193.4 %all-gather.37.cloned.1.call-start = ((), (), s32[]{:S(2)}) async-start(), calls=%async_computation.4 | async-start | bytes 6684672 | tf_op jit(solution)/shard_map/all_gather | solution.py:61
  15.0 235.3 %all-gather.39.cloned.1.call-start = ((), (), s32[]{:S(2)}) async-start(), calls=%async_computation.5 | async-start | bytes 6684672 | tf_op jit(solution)/shard_map/all_gather | solution.py:61
  16.0 6.3 %copy-start.12 = (s32[8]{0:T(128)S(1)}, s32[8]{0:T(128)}, u32[]{:S(2)}) copy-start(s32[8]{0:T(128)} %param.16) | copy-start | bytes 100
  16.0 6.4 %copy-start.8 = (bf16[2,1024]{1,0:T(2,128)(2,1)S(1)}, bf16[2,1024]{1,0:T(2,128)(2,1)}, u32[]{:S(2)}) copy-start(bf16[2,1024]{1,0:T(2,128)(2,1)} %param.19) | copy-start | bytes 12292
  16.1 6.4 %copy-start.7 = (bf16[8,1024]{1,0:T(8,128)(2,1)S(1)}, bf16[8,1024]{1,0:T(8,128)(2,1)}, u32[]{:S(2)}) copy-start(bf16[8,1024]{1,0:T(8,128)(2,1)} %param.15) | copy-start | bytes 49156
  16.1 6.5 %copy-start.10 = (bf16[2,128]{1,0:T(2,128)(2,1)S(1)}, bf16[2,128]{1,0:T(2,128)(2,1)}, u32[]{:S(2)}) copy-start(bf16[2,128]{1,0:T(2,128)(2,1)} %param.24) | copy-start | bytes 1540
  16.1 6.7 %copy-start.11 = (bf16[2,128]{1,0:T(2,128)(2,1)S(1)}, bf16[2,128]{1,0:T(2,128)(2,1)}, u32[]{:S(2)}) copy-start(bf16[2,128]{1,0:T(2,128)(2,1)} %param.23) | copy-start | bytes 1540
  16.1 277.4 %all-gather.41.cloned.1.call-start = ((), (), s32[]{:S(2)}) async-start(), calls=%async_computation.6 | async-start | bytes 6684672 | tf_op jit(solution)/shard_map/all_gather | solution.py:61
  17.2 312.8 %all-gather.45.cloned.1.call-start = ((), (), s32[]{:S(2)}) async-start(), calls=%async_computation.8 | async-start | bytes 2228224 | tf_op jit(solution)/shard_map/all_gather | solution.py:61
  18.0 348.5 %all-gather.47.cloned.1.call-start = ((), (), s32[]{:S(2)}) async-start(), calls=%async_computation.9 | async-start | bytes 2228224 | tf_op jit(solution)/shard_map/all_gather | solution.py:61
  18.8 386.5 %all-gather.43.cloned.1.call-start = ((), (), s32[]{:S(2)}) async-start(), calls=%async_computation.7 | async-start | bytes 4456448 | tf_op jit(solution)/shard_map/all_gather | solution.py:61
  19.5 424.3 %all-gather.49.cloned.1.call-start = ((), (), s32[]{:S(2)}) async-start(), calls=%async_computation.10 | async-start | bytes 4456448 | tf_op jit(solution)/shard_map/all_gather | solution.py:61
  20.3 466.2 %all-gather.51.cloned.1.call-start = ((), (), s32[]{:S(2)}) async-start(), calls=%async_computation.11 | async-start | bytes 6684672 | tf_op jit(solution)/shard_map/all_gather | solution.py:61
  20.9 508.7 %all-gather.53.cloned.1.call-start = ((), (), s32[]{:S(2)}) async-start(), calls=%async_computation.12 | async-start | bytes 6684672 | tf_op jit(solution)/shard_map/all_gather | solution.py:61
  21.7 550.9 %all-gather.55.cloned.1.call-start = ((), (), s32[]{:S(2)}) async-start(), calls=%async_computation.13 | async-start | bytes 6684672 | tf_op jit(solution)/shard_map/all_gather | solution.py:61
  22.9 4.1 copy-start.1
  26.9 2.4 copy-start.9
  368.5 40.6 %copy-start.2 = (bf16[1,8,128,8,128]{4,3,2,1,0:T(8,128)(2,1)S(1)}, bf16[1,8,128,8,128]{4,3,2,1,0:T(8,128)(2,1)}, u32[]{:S(2)}) copy-start(bf16[1,8,128,8,128]{4,3,2,1,0:T(8,128)(2,1)} %get-tuple-element.5) | copy-start | bytes 6291460
  486.4 4.0 copy-start
Sparse Core Ops, SparseCore 0:
  9.7 41.2 all-gather.30
  52.6 34.8 all-gather.32
  89.1 37.2 all-gather.28
  127.8 36.8 all-gather.34
  166.2 41.1 all-gather.36
  208.8 41.5 all-gather.38
  252.0 41.5 all-gather.40
  295.2 34.8 all-gather.44
  331.7 34.8 all-gather.46
  368.0 37.2 all-gather.42
  406.9 36.8 all-gather.48
  445.3 41.1 all-gather.50
  488.1 41.5 all-gather.52
  531.1 41.5 all-gather.54
where the time goes:
time: 587 us; the launch traced here: 586 us
  waiting for transfers between devices  494 us (84%)
  matrix products  48.4 us (8%)
  local copies, waits for them, and re-layouts  19.8 us (3%)
  between operations  14.4 us (2%)
  other arithmetic  9.08 us (2%)
    all_gather x14, waiting for transfers between devices, gather_rows(): return lax.all_gather(shard, 'dp', axis=0, tiled=True)  489 us
    dot_general x2, matrix products, device_fn(): jnp.dot(act_in, gather_rows(w_down[layer_idx]), preferred_element_type=jn...  13.5 us
  transfers between devices with their start and end apart: 14, of which 14 were waited for; matrix products, arithmetic and copies ran while one was open for 12% of the time, Pallas kernels for 0%

commit v1 on v0

v1 whole, which is shorter than its diff:
```python
import functools
import math

import jax
import jax.numpy as jnp
from jax import lax
from jax.experimental import pallas as pl
from jax.experimental.pallas import tpu as pltpu
from jax.sharding import PartitionSpec as P

HEAD_DIM = 128
RMS_EPS = 1e-6
ROPE_THETA = 1000000.0
POOL_MAX = 2
MESH = pl.DeviceIdType.MESH
F32 = jnp.float32
BF16 = jnp.bfloat16
NEG = float("-inf")


def rms(values, width):
    return values * lax.rsqrt(jnp.sum(values * values, axis=-1, keepdims=True) * (1.0 / width) + RMS_EPS)


def decode_kernel(cfg, pos_ref, x_ref, an_ref, qn_ref, kn_ref, mn_ref, wq_hbm, wk_hbm, wv_hbm, wo_hbm, wg_hbm, wu_hbm, wd_hbm, kc_hbm, vc_hbm,
                  y_ref, krow_ref, vrow_ref,
                  wqkv, wo, wgu, wd, kc, vc, xg, qkvs, qkvi, og, x1g, pbuf, ybuf, x1f, qs, ks, vs, os_, kro, vro, cs, sn,
                  z_send, z_recv, d_send, d_recv, y_send, y_recv, a_send, a_recv, down_send, down_recv, loc_sem, down_loc):
    layers, zn, pool, tok = cfg["layers"], cfg["zn"], cfg["pool"], cfg["tok"]
    qh, kh = cfg["qh"], cfg["kh"]
    dm = x_ref.shape[1]
    nq = zn * tok
    ctile = dm // zn
    idx = lax.axis_index("dp")
    z, c = idx // 2, idx % 2
    part = lax.axis_index("part")
    yi = part % pool
    mate = part + 1 - 2 * yi
    sib = {"dp": 2 * z + (1 - c)}
    nei = {"part": mate}
    qmine = c * pool + yi
    qother = c * pool + (pool - 1 - yi)

    order = []
    for r in range(zn // 2, 0, -1):
        order.append(r)
        if r != zn - r:
            order.append(zn - r)

    def peer(r):
        return lax.rem(z + r, zn)

    def peer_id(zt):
        return {"dp": 2 * zt + c}

    barrier = pltpu.get_barrier_semaphore()
    for r in order:
        pl.semaphore_signal(barrier, inc=1, device_id=peer_id(peer(r)), device_id_type=MESH)
    pl.semaphore_signal(barrier, inc=1, device_id=sib, device_id_type=MESH)
    if pool == 2:
        pl.semaphore_signal(barrier, inc=1, device_id=nei, device_id_type=MESH)

    def rcopy(src, dst, ss, rs, dev):
        return pltpu.make_async_remote_copy(src_ref=src, dst_ref=dst, send_sem=ss, recv_sem=rs, device_id=dev, device_id_type=MESH)

    def wait_bytes(ref, sem):
        pltpu.make_async_copy(ref, ref, sem).wait()

    groups = {
        "qkv": (wqkv, 0, [(wq_hbm, 0), (wk_hbm, 2 * HEAD_DIM), (wv_hbm, 3 * HEAD_DIM)]),
        "o": (wo, 1, [(wo_hbm, 0)]),
        "gu": (wgu, 2, [(wg_hbm, 0), (wu_hbm, wgu.shape[-1] // 2)]),
    }

    def pieces(l, name, zt):
        buf, gi, srcs = groups[name]
        rows = buf.shape[3]
        out = []
        for src, off in srcs:
            width = src.shape[2] // zn
            s = src.at[l, pl.ds(pl.multiple_of(yi * rows, rows), rows), pl.ds(pl.multiple_of(zt * width, 128), width)]
            d = buf.at[l, z, qmine, :, pl.ds(off, width)]
            out.append((s, d))
        return out, gi

    def w_local(l, name):
        ps, gi = pieces(l, name, z)
        for s, d in ps:
            pltpu.make_async_copy(s, d, loc_sem.at[l, gi]).start()

    def w_send(l, name):
        for r in order:
            zt = peer(r)
            ps, gi = pieces(l, name, zt)
            for s, d in ps:
                rcopy(s, d, z_send.at[l, gi], z_recv.at[l, gi], peer_id(zt)).start()

    def w_fwd1(l, name):
        buf, gi, _ = groups[name]
        wait_bytes(buf.at[l, 0:zn - 1, 0], z_recv.at[l, gi])
        wait_bytes(buf.at[l, 0, 0], loc_sem.at[l, gi])
        q = buf.at[l, :, qmine]
        if pool == 2:
            rcopy(q, q, y_send.at[l, gi], y_recv.at[l, gi], nei).start()
        rcopy(q, q, d_send.at[l, gi, 0], d_recv.at[l, gi, 0], sib).start()

    def w_fwd2(l, name):
        if pool == 2:
            buf, gi, _ = groups[name]
            q = buf.at[l, :, qother]
            wait_bytes(q, y_recv.at[l, gi])
            rcopy(q, q, d_send.at[l, gi, 1], d_recv.at[l, gi, 1], sib).start()

    def w_fin(l, name):
        buf, gi, _ = groups[name]
        wait_bytes(buf.at[l, :, 0], d_recv.at[l, gi, 0])
        if pool == 2:
            wait_bytes(buf.at[l, :, 0], d_recv.at[l, gi, 1])

    def w_drain(l, name):
        buf, gi, _ = groups[name]
        wait_bytes(buf.at[l, 0:zn - 1, 0], z_send.at[l, gi])
        wait_bytes(buf.at[l, :, 0], d_send.at[l, gi, 0])
        if pool == 2:
            wait_bytes(buf.at[l, :, 0], y_send.at[l, gi])
            wait_bytes(buf.at[l, :, 0], d_send.at[l, gi, 1])

    def spread(src_of, dst, l, ph):
        for r in order:
            zt = peer(r)
            rcopy(src_of(zt), dst, a_send.at[l, ph], a_recv.at[l, ph], peer_id(zt)).start()

    def arrived(buf, l, ph):
        wait_bytes(buf.at[l, 0:zn - 1], a_recv.at[l, ph])

    for l in range(layers):
        pltpu.make_async_copy(wd_hbm.at[l], wd.at[l, c], down_loc.at[l, 0]).start()
        for name in ("qkv", "o", "gu"):
            w_local(l, name)
        pltpu.make_async_copy(kc_hbm.at[l], kc.at[l], down_loc.at[l, 1]).start()
        pltpu.make_async_copy(vc_hbm.at[l], vc.at[l], down_loc.at[l, 2]).start()

    xg[0, z] = x_ref[...]

    pl.semaphore_wait(barrier, zn + pool - 1)

    spread(lambda zt: x_ref, xg.at[0, z], 0, 0)
    w_send(0, "qkv")
    for l in range(layers):
        rcopy(wd_hbm.at[l], wd.at[l, c], down_send.at[l], down_recv.at[l], sib).start()

    row_id = lax.broadcasted_iota(jnp.int32, (tok, HEAD_DIM), 0)
    lane_id = lax.broadcasted_iota(jnp.int32, (tok, HEAD_DIM), 1)
    pos = jnp.zeros((tok, HEAD_DIM), jnp.int32)
    for n in range(tok):
        pos = jnp.where(row_id == n, pos_ref[n], pos)
    half = HEAD_DIM // 2
    pair = jnp.where(lane_id >= half, lane_id - half, lane_id).astype(F32)
    inv_freq = jnp.exp(pair * (-2.0 * math.log(ROPE_THETA) / HEAD_DIM))
    ang = pos.astype(F32) * inv_freq
    cs[...] = jnp.cos(ang)
    sin_tab = jnp.sin(ang)
    sn[...] = jnp.where(lane_id >= half, sin_tab, -sin_tab)

    w_send(0, "o")

    def head_norm(v, gain):
        v = rms(v, HEAD_DIM) * gain
        return (v * cs[...] + pltpu.roll(v, half, 1) * sn[...]).astype(BF16).astype(F32)

    def gathered_x(l):
        return xg[l].astype(F32).reshape(nq, dm)

    def attention(l):
        qg = qn_ref[l:l + 1, :].astype(F32)
        kg = kn_ref[l:l + 1, :].astype(F32)
        for h in range(qh):
            v = qkvi[l, h // 2, :, (h % 2) * HEAD_DIM:(h % 2 + 1) * HEAD_DIM].astype(F32)
            qs[pl.ds(h, tok, stride=qh), :] = head_norm(v, qg)
        for h in range(kh):
            k = head_norm(qkvi[l, h, :, 2 * HEAD_DIM:3 * HEAD_DIM].astype(F32), kg)
            v = qkvi[l, h, :, 3 * HEAD_DIM:4 * HEAD_DIM].astype(F32)
            for g in range(2):
                ks[pl.ds(2 * h + g, tok, stride=qh), :] = k
                vs[pl.ds(2 * h + g, tok, stride=qh), :] = v
            kro[pl.ds(h, tok, stride=kh), :] = k
            vro[pl.ds(h, tok, stride=kh), :] = v
        krow_ref[l] = kro[...].astype(BF16)
        vrow_ref[l] = vro[...].astype(BF16)
        cols = kc.shape[2]
        lane = lax.broadcasted_iota(jnp.int32, (qh, cols), 1)
        row = lax.broadcasted_iota(jnp.int32, (qh, cols), 0)
        mine = lax.rem(lane, kh) == lax.shift_right_logical(row, 1)
        slot = jnp.where(mine, lax.div(lane, kh), cols)
        scale = HEAD_DIM ** -0.5
        for n in range(tok):
            q = qs[n * qh:(n + 1) * qh, :]
            s_new = jnp.sum(q * ks[n * qh:(n + 1) * qh, :], axis=-1, keepdims=True) * scale
            s = lax.dot_general(q.astype(BF16), kc[l, n], (((1,), (1,)), ((), ())), preferred_element_type=F32) * scale
            s = jnp.where(slot < pos_ref[n], s, NEG)
            m = jnp.maximum(jnp.max(s, axis=-1, keepdims=True), s_new)
            e = jnp.exp(s - m)
            e_new = jnp.exp(s_new - m)
            den = jnp.sum(e, axis=-1, keepdims=True) + e_new
            p = (e / den).astype(BF16)
            p_new = (e_new / den).astype(BF16).astype(F32)
            o = jnp.dot(p, vc[l, n], preferred_element_type=F32) + p_new * vs[n * qh:(n + 1) * qh, :]
            os_[n * qh:(n + 1) * qh, :] = o
        for h in range(qh):
            og[l, z, :, h * HEAD_DIM:(h + 1) * HEAD_DIM] = os_[pl.ds(h, tok, stride=qh), :].astype(BF16)

    for l in range(layers):
        last = l == layers - 1
        if l == 0:
            w_send(0, "gu")
        arrived(xg, l, 0)
        h = (rms(gathered_x(l), dm) * an_ref[l:l + 1, :].astype(F32)).astype(BF16)
        if l == 0:
            w_fwd1(l, "qkv")
            w_fwd2(l, "qkv")
        w_fin(l, "qkv")
        r = jnp.dot(h, wqkv[l].reshape(dm, wqkv.shape[-1]), preferred_element_type=F32)
        qkvs[l] = r.reshape(zn, tok, wqkv.shape[-1]).astype(BF16)
        qkvi[l, z] = qkvs[l, z]
        spread(lambda zt: qkvs.at[l, zt], qkvi.at[l, z], l, 1)
        w_fwd1(l, "o")
        if l == 0:
            for k in range(layers):
                wait_bytes(kc.at[k], down_loc.at[k, 1])
                wait_bytes(vc.at[k], down_loc.at[k, 2])
        arrived(qkvi, l, 1)
        attention(l)
        spread(lambda zt: og.at[l, z], og.at[l, z], l, 2)
        if not last:
            w_send(l + 1, "qkv")
        w_fwd2(l, "o")
        w_fwd1(l, "gu")
        w_fin(l, "o")
        arrived(og, l, 2)
        o_all = og[l].astype(F32).reshape(nq, og.shape[-1]).astype(BF16)
        r = jnp.dot(o_all, wo[l].reshape(og.shape[-1], ctile), preferred_element_type=F32)
        xc = xg[l, :, :, pl.ds(pl.multiple_of(z * ctile, ctile), ctile)].astype(F32).reshape(nq, ctile)
        x1g[l, z] = (xc + r).astype(BF16)
        spread(lambda zt: x1g.at[l, z], x1g.at[l, z], l, 3)
        if not last:
            w_send(l + 1, "o")
        w_fwd2(l, "gu")
        wait_bytes(wd.at[l, 0], down_loc.at[l, 0])
        wait_bytes(wd.at[l, 0], down_recv.at[l])
        w_fin(l, "gu")
        arrived(x1g, l, 3)
        x1 = jnp.concatenate([x1g[l, zz].astype(F32) for zz in range(zn)], axis=-1)
        x1f[...] = x1
        h2 = (rms(x1, dm) * mn_ref[l:l + 1, :].astype(F32)).astype(BF16)
        gu = jnp.dot(h2, wgu[l].reshape(dm, wgu.shape[-1]), preferred_element_type=F32)
        ffc = wgu.shape[-1] // 2
        g = gu[:, :ffc]
        a = (g * jax.nn.sigmoid(g) * gu[:, ffc:]).astype(BF16)
        pr = jnp.dot(a, wd[l].reshape(ffc, dm), preferred_element_type=F32)
        pbuf[l] = pr.reshape(zn, tok, dm)
        ybuf[l, z] = pbuf[l, z]
        spread(lambda zt: pbuf.at[l, zt], ybuf.at[l, z], l, 4)
        if not last:
            w_send(l + 1, "gu")
            w_fwd1(l + 1, "qkv")
            w_fwd2(l + 1, "qkv")
        arrived(ybuf, l, 4)
        total = ybuf[l, 0]
        for zz in range(1, zn):
            total = total + ybuf[l, zz]
        y = (x1f[pl.ds(pl.multiple_of(z * tok, tok), tok), :] + total).astype(BF16)
        if last:
            y_ref[...] = y
        else:
            xg[l + 1, z] = y
            spread(lambda zt: xg.at[l + 1, z], xg.at[l + 1, z], l + 1, 0)

    for l in range(layers):
        for name in ("qkv", "o", "gu"):
            w_drain(l, name)
        wait_bytes(wd.at[l, 0], down_send.at[l])
        for ph, buf in enumerate((xg, qkvi, og, x1g, ybuf)):
            wait_bytes(buf.at[l, 0:zn - 1], a_send.at[l, ph])


def solution(mesh):
    batch_axes = ("part", "dp")
    act_spec = P(batch_axes, None)
    cache_spec = P(None, batch_axes, None, None, None)
    mat_spec = P(None, "dp", None)
    gain_spec = P(None, None)
    in_specs = (act_spec, P(batch_axes), cache_spec, cache_spec, gain_spec, mat_spec, mat_spec, mat_spec, gain_spec, gain_spec, mat_spec, gain_spec, mat_spec, mat_spec, mat_spec)
    out_specs = (act_spec, cache_spec, cache_spec)
    zn = mesh.shape["dp"] // 2
    pool = POOL_MAX if mesh.shape["part"] % POOL_MAX == 0 else 1

    def device_fn(x, positions, k_cache, v_cache, attn_norm, w_q, w_k, w_v, q_norm, k_norm, w_o, mlp_norm, w_gate, w_up, w_down):
        layers, tok, slots, kh, hd = k_cache.shape
        dm = x.shape[1]
        qw, kw, ff = w_q.shape[2], w_k.shape[2], w_gate.shape[2]
        qh = qw // hd
        nq = 2 * pool
        qkvc = (qw + 2 * kw) // zn
        cfg = dict(layers=layers, zn=zn, pool=pool, tok=tok, qh=qh, kh=kh)
        vm = pl.BlockSpec(memory_space=pltpu.VMEM)
        hb = pl.BlockSpec(memory_space=pl.ANY)
        sm = pl.BlockSpec(memory_space=pltpu.SMEM)
        dma = pltpu.SemaphoreType.DMA
        flat = (layers, tok, slots * kh, hd)
        scratch = [
            pltpu.VMEM((layers, zn, nq, w_q.shape[1] // pool, qkvc), BF16),
            pltpu.VMEM((layers, zn, nq, w_o.shape[1] // pool, dm // zn), BF16),
            pltpu.VMEM((layers, zn, nq, w_gate.shape[1] // pool, 2 * ff // zn), BF16),
            pltpu.VMEM((layers, 2, w_down.shape[1], dm), BF16),
            pltpu.VMEM(flat, BF16),
            pltpu.VMEM(flat, BF16),
            pltpu.VMEM((layers, zn, tok, dm), BF16),
            pltpu.VMEM((layers, zn, tok, qkvc), BF16),
            pltpu.VMEM((layers, zn, tok, qkvc), BF16),
            pltpu.VMEM((layers, zn, tok, qw), BF16),
            pltpu.VMEM((layers, zn, zn * tok, dm // zn), BF16),
            pltpu.VMEM((layers, zn, tok, dm), F32),
            pltpu.VMEM((layers, zn, tok, dm), F32),
            pltpu.VMEM((zn * tok, dm), F32),
            pltpu.VMEM((tok * qh, hd), F32),
            pltpu.VMEM((tok * qh, hd), F32),
            pltpu.VMEM((tok * qh, hd), F32),
            pltpu.VMEM((tok * qh, hd), F32),
            pltpu.VMEM((tok * kh, hd), F32),
            pltpu.VMEM((tok * kh, hd), F32),
            pltpu.VMEM((tok, hd), F32),
            pltpu.VMEM((tok, hd), F32),
            dma((layers, 3)), dma((layers, 3)), dma((layers, 3, 2)), dma((layers, 3, 2)), dma((layers, 3)), dma((layers, 3)),
            dma((layers, 5)), dma((layers, 5)), dma((layers,)), dma((layers,)), dma((layers, 3)), dma((layers, 3)),
        ]
        y, krow, vrow = pl.pallas_call(
            functools.partial(decode_kernel, cfg),
            name="decode",
            out_shape=(jax.ShapeDtypeStruct((tok, dm), BF16), jax.ShapeDtypeStruct((layers, tok * kh, hd), BF16), jax.ShapeDtypeStruct((layers, tok * kh, hd), BF16)),
            in_specs=[sm, vm, vm, vm, vm, vm] + [hb] * 9,
            out_specs=(vm, vm, vm),
            scratch_shapes=scratch,
            compiler_params=pltpu.CompilerParams(collective_id=0, has_side_effects=True, vmem_limit_bytes=48 * 1024 * 1024),
        )(positions, x, attn_norm, q_norm, k_norm, mlp_norm, w_q, w_k, w_v, w_o, w_gate, w_up, w_down, k_cache.reshape(flat), v_cache.reshape(flat))
        slot_hit = (jnp.arange(slots)[None, :] == positions[:, None])[None, :, :, None, None]
        k_out = jnp.where(slot_hit, krow.reshape(layers, tok, 1, kh, hd), k_cache)
        v_out = jnp.where(slot_hit, vrow.reshape(layers, tok, 1, kh, hd), v_cache)
        return y, k_out, v_out

    return jax.shard_map(device_fn, mesh=mesh, in_specs=in_specs, out_specs=out_specs, check_vma=False)
```

time: 587 us -> 122 us (0.21)
  the two profiles are of different devices: /device:TPU:21 before, /device:TPU:22 now
where the time goes in v1:
time: 122 us
  Pallas kernels  104 us (85%)
  local copies, waits for them, and re-layouts  12 us (10%)
  other arithmetic  4.73 us (4%)
    pallas_call x1, Pallas kernels, device_fn(): pl.pallas_call(functools.partial(decode_kernel, cfg), name='decode', out_...  104 us
    unnamed x31, local copies, waits for them, and re-layouts  12 us
    select_n x1, other arithmetic, device_fn(): v_out = jnp.where(slot_hit, vrow.reshape(layers, tok, 1, kh, hd), v_cache)  4 us

profile of v1, /device:TPU:22, one launch (start us, length us, event | category | flops | bytes accessed | tf_op | source)
XLA Modules:
  0.0 121.7 jit_solution(14695447411933777472)
XLA Ops:
  0.6 0.7 iota_compare_fusion
  1.4 0.0 copy-start
  1.4 1.1 copy-done
  2.5 0.0 copy-start.1
  2.5 1.1 copy-done.1
  3.6 0.0 copy-start.2
  3.6 1.1 copy-done.2
  4.8 0.0 copy-start.3
  4.8 1.0 copy-done.3
  5.8 0.0 copy-start.4
  5.8 1.0 copy-done.4
  6.8 0.0 copy-start.5
  6.8 0.9 copy-done.5
  7.8 0.0 copy-start.6
  7.8 0.9 copy-done.6
  8.7 0.0 copy-start.7
  8.7 0.7 copy-done.7
  9.5 0.0 copy-start.8
  9.5 0.7 copy-done.8
  10.2 0.0 copy-start.9
  10.2 0.7 copy-done.9
  10.8 0.0 copy-start.10
  10.8 0.7 copy-done.10
  11.5 0.0 copy-start.11
  11.5 0.7 copy-done.11
  12.1 0.0 copy-start.12
  12.2 0.7 copy-done.12
  12.8 0.0 copy-start.13
  12.8 0.0 copy-start.14
  12.8 104.2 %decode.1 = (bf16[8,1024]{1,0:T(8,128)(2,1)S(1)}, bf16[2,64,128]{2,1,0:T(8,128)(2,1)S(1)}, bf16[2,64,128]{2,1,0:T(8,128)(2,1)S(1)}) custom-call(s32[8]{0:T(128)S(1)} %copy-done.10, bf16[8,1024]{1,0:T(8,128)(2,1)S(1)} %copy-done.7, bf16[2,1024]{1,0:T(2,128)(2,1)S(1)} %copy-done.8, bf16[2,128]{1,0:T(2,128)(2,1)S(1)} %copy-done.11, ...), custom_call_target="tpu_custom_call" | custom-call | tf_op jit(solution)/shard_map/decode/pallas_call | solution.py:336
  117.1 0.0 copy-done.13
  117.1 0.0 copy-done.14
  117.1 4.0 %broadcast_select_fusion = (bf16[2,8,128,8,128]{4,3,2,1,0:T(8,128)(2,1)}, bf16[2,8,128,8,128]{4,3,2,1,0:T(8,128)(2,1)}) fusion(bf16[2,8,128,8,128]{4,3,2,1,0:T(8,128)(2,1)S(1)} %copy-done.14, pred[8,128]{1,0:T(8,128)(4,1)S(1)} %iota_compare_fusion, bf16[2,8,8,128]{3,2,1,0:T(8,128)(2,1)S(1)} %bitcast.5, bf16[2,8,128,8,128]{4,3,2,1,0:T(8,128)(2,1)S(1)} %copy-done.13, ...), kind=kLoop, calls=%fused_computation | loop fusion | flops 4194304 | bytes 16843776 | tf_op jit(solution)/shard_map/jit(_where)/select_n | solution.py:347
  121.1 0.6 copy.19
Async XLA Ops:
  1.4 1.1 copy-start
  2.5 1.1 copy-start.1
  3.6 1.1 copy-start.2
  4.8 1.0 copy-start.3
  5.8 1.0 copy-start.4
  6.8 0.9 copy-start.5
  7.8 0.9 copy-start.6
  8.7 0.7 copy-start.7
  9.5 0.7 copy-start.8
  10.2 0.7 copy-start.9
  10.8 0.7 copy-start.10
  11.5 0.7 copy-start.11
  12.1 0.7 copy-start.12
  12.8 104.3 %copy-start.13 = (bf16[2,8,128,8,128]{4,3,2,1,0:T(8,128)(2,1)S(1)}, bf16[2,8,128,8,128]{4,3,2,1,0:T(8,128)(2,1)}, u32[]{:S(2)}) copy-start(bf16[2,8,128,8,128]{4,3,2,1,0:T(8,128)(2,1)} %param.17) | copy-start | bytes 12582916
  12.8 104.3 %copy-start.14 = (bf16[2,8,128,8,128]{4,3,2,1,0:T(8,128)(2,1)S(1)}, bf16[2,8,128,8,128]{4,3,2,1,0:T(8,128)(2,1)}, u32[]{:S(2)}) copy-start(bf16[2,8,128,8,128]{4,3,2,1,0:T(8,128)(2,1)} %param.18) | copy-start | bytes 12582916

commit v2 on v1

--- a/solution.py
+++ b/solution.py
@@ -12,6 +12,7 @@
 RMS_EPS = 1e-6
 ROPE_THETA = 1000000.0
 POOL_MAX = 2
+VMEM_LIMIT = 67043328
 MESH = pl.DeviceIdType.MESH
 F32 = jnp.float32
 BF16 = jnp.bfloat16
@@ -22,13 +23,13 @@
     return values * lax.rsqrt(jnp.sum(values * values, axis=-1, keepdims=True) * (1.0 / width) + RMS_EPS)
 
 
-def decode_kernel(cfg, pos_ref, x_ref, an_ref, qn_ref, kn_ref, mn_ref, wq_hbm, wk_hbm, wv_hbm, wo_hbm, wg_hbm, wu_hbm, wd_hbm, kc_hbm, vc_hbm,
+def decode_kernel(cfg, pos_hbm, x_hbm, an_hbm, qn_hbm, kn_hbm, mn_hbm, wq_hbm, wk_hbm, wv_hbm, wo_hbm, wg_hbm, wu_hbm, wd_hbm, kc_hbm, vc_hbm,
                   y_ref, krow_ref, vrow_ref,
-                  wqkv, wo, wgu, wd, kc, vc, xg, qkvs, qkvi, og, x1g, pbuf, ybuf, x1f, qs, ks, vs, os_, kro, vro, cs, sn,
-                  z_send, z_recv, d_send, d_recv, y_send, y_recv, a_send, a_recv, down_send, down_recv, loc_sem, down_loc):
+                  wqkv, wo, wgu, wd, kc, vc, xg, qkvs, qkvi, og, x1g, pbuf, ybuf, x1f, qs, ks, vs, os_, kro, vro, cs, sn, pos_ref, an_ref, qn_ref, kn_ref, mn_ref,
+                  z_send, z_recv, d_send, d_recv, y_send, y_recv, a_send, a_recv, down_send, down_recv, loc_sem, down_loc, in_sem):
     layers, zn, pool, tok = cfg["layers"], cfg["zn"], cfg["pool"], cfg["tok"]
     qh, kh = cfg["qh"], cfg["kh"]
-    dm = x_ref.shape[1]
+    dm = x_hbm.shape[1]
     nq = zn * tok
     ctile = dm // zn
     idx = lax.axis_index("dp")
@@ -133,6 +134,10 @@
     def arrived(buf, l, ph):
         wait_bytes(buf.at[l, 0:zn - 1], a_recv.at[l, ph])
 
+    smalls = [(x_hbm, xg.at[0, z]), (pos_hbm, pos_ref), (an_hbm, an_ref), (qn_hbm, qn_ref), (kn_hbm, kn_ref), (mn_hbm, mn_ref)]
+    small_copies = [pltpu.make_async_copy(s, d, in_sem.at[i]) for i, (s, d) in enumerate(smalls)]
+    for cp in small_copies:
+        cp.start()
     for l in range(layers):
         pltpu.make_async_copy(wd_hbm.at[l], wd.at[l, c], down_loc.at[l, 0]).start()
         for name in ("qkv", "o", "gu"):
@@ -140,15 +145,16 @@
         pltpu.make_async_copy(kc_hbm.at[l], kc.at[l], down_loc.at[l, 1]).start()
         pltpu.make_async_copy(vc_hbm.at[l], vc.at[l], down_loc.at[l, 2]).start()
 
-    xg[0, z] = x_ref[...]
-
     pl.semaphore_wait(barrier, zn + pool - 1)
 
-    spread(lambda zt: x_ref, xg.at[0, z], 0, 0)
+    small_copies[0].wait()
+    spread(lambda zt: xg.at[0, z], xg.at[0, z], 0, 0)
     w_send(0, "qkv")
     for l in range(layers):
         rcopy(wd_hbm.at[l], wd.at[l, c], down_send.at[l], down_recv.at[l], sib).start()
 
+    for cp in small_copies[1:]:
+        cp.wait()
     row_id = lax.broadcasted_iota(jnp.int32, (tok, HEAD_DIM), 0)
     lane_id = lax.broadcasted_iota(jnp.int32, (tok, HEAD_DIM), 1)
     pos = jnp.zeros((tok, HEAD_DIM), jnp.int32)
@@ -303,8 +309,7 @@
         qkvc = (qw + 2 * kw) // zn
         cfg = dict(layers=layers, zn=zn, pool=pool, tok=tok, qh=qh, kh=kh)
         vm = pl.BlockSpec(memory_space=pltpu.VMEM)
-        hb = pl.BlockSpec(memory_space=pl.ANY)
-        sm = pl.BlockSpec(memory_space=pltpu.SMEM)
+        hb = pl.BlockSpec(memory_space=pltpu.HBM)
         dma = pltpu.SemaphoreType.DMA
         flat = (layers, tok, slots * kh, hd)
         scratch = [
@@ -330,17 +335,22 @@
             pltpu.VMEM((tok * kh, hd), F32),
             pltpu.VMEM((tok, hd), F32),
             pltpu.VMEM((tok, hd), F32),
+            pltpu.SMEM((tok,), jnp.int32),
+            pltpu.VMEM((layers, dm), BF16),
+            pltpu.VMEM((layers, hd), BF16),
+            pltpu.VMEM((layers, hd), BF16),
+            pltpu.VMEM((layers, dm), BF16),
             dma((layers, 3)), dma((layers, 3)), dma((layers, 3, 2)), dma((layers, 3, 2)), dma((layers, 3)), dma((layers, 3)),
-            dma((layers, 5)), dma((layers, 5)), dma((layers,)), dma((layers,)), dma((layers, 3)), dma((layers, 3)),
+            dma((layers, 5)), dma((layers, 5)), dma((layers,)), dma((layers,)), dma((layers, 3)), dma((layers, 3)), dma((6,)),
         ]
         y, krow, vrow = pl.pallas_call(
             functools.partial(decode_kernel, cfg),
             name="decode",
             out_shape=(jax.ShapeDtypeStruct((tok, dm), BF16), jax.ShapeDtypeStruct((layers, tok * kh, hd), BF16), jax.ShapeDtypeStruct((layers, tok * kh, hd), BF16)),
-            in_specs=[sm, vm, vm, vm, vm, vm] + [hb] * 9,
+            in_specs=[hb] * 15,
             out_specs=(vm, vm, vm),
             scratch_shapes=scratch,
-            compiler_params=pltpu.CompilerParams(collective_id=0, has_side_effects=True, vmem_limit_bytes=48 * 1024 * 1024),
+            compiler_params=pltpu.CompilerParams(collective_id=0, has_side_effects=True, vmem_limit_bytes=VMEM_LIMIT),
         )(positions, x, attn_norm, q_norm, k_norm, mlp_norm, w_q, w_k, w_v, w_o, w_gate, w_up, w_down, k_cache.reshape(flat), v_cache.reshape(flat))
         slot_hit = (jnp.arange(slots)[None, :] == positions[:, None])[None, :, :, None, None]
         k_out = jnp.where(slot_hit, krow.reshape(layers, tok, 1, kh, hd), k_cache)

time: 122 us -> 113 us (0.926)
  the two profiles are of different devices: /device:TPU:22 before, /device:TPU:21 now
where the time goes in v2:
time: 113 us
  Pallas kernels  103 us (91%)
  other arithmetic  8.75 us (8%)
    pallas_call x1, Pallas kernels, device_fn(): pl.pallas_call(functools.partial(decode_kernel, cfg), name='decode', out_...  103 us
    select_n x1, other arithmetic, device_fn(): v_out = jnp.where(slot_hit, vrow.reshape(layers, tok, 1, kh, hd), v_cache)  7.46 us

profile of v2, /device:TPU:21, one launch (start us, length us, event | category | flops | bytes accessed | tf_op | source)
XLA Modules:
  0.0 113.4 jit_solution(16510803791691478912)
XLA Ops:
  0.6 1.3 %iota_compare_fusion = pred[8,128]{1,0:T(8,128)(4,1)} fusion(s32[8]{0:T(128)} %pos_hbm.1), kind=kLoop, calls=%fused_computation.2 | loop fusion | flops 1024 | bytes 1056 | tf_op jit(solution)/shard_map/eq | solution.py:355
  1.9 103.4 %decode.1 = (bf16[8,1024]{1,0:T(8,128)(2,1)}, bf16[2,64,128]{2,1,0:T(8,128)(2,1)}, bf16[2,64,128]{2,1,0:T(8,128)(2,1)}) custom-call(s32[8]{0:T(128)} %pos_hbm.1, bf16[8,1024]{1,0:T(8,128)(2,1)} %x_hbm.1, bf16[2,1024]{1,0:T(2,128)(2,1)} %an_hbm.1, bf16[2,128]{1,0:T(2,128)(2,1)} %qn_hbm.1, bf16[2,128]{1,0:T(2,128)(2,1)} %kn_hbm.1, bf16[2,1024]{1,0:T(2,128)(2,1)} %mn_hbm.1, ...), custom_call_target="tpu_custom_call" | custom-call | tf_op jit(solution)/shard_map/decode/pallas_call | solution.py:346
  105.3 0.0 copy-start
  105.3 7.5 %broadcast_select_fusion = (bf16[2,8,128,8,128]{4,3,2,1,0:T(8,128)(2,1)}, bf16[2,8,128,8,128]{4,3,2,1,0:T(8,128)(2,1)}) fusion(bf16[2,8,128,8,128]{4,3,2,1,0:T(8,128)(2,1)} %param.18, pred[8,128]{1,0:T(8,128)(4,1)} %iota_compare_fusion, bf16[2,8,8,128]{3,2,1,0:T(8,128)(2,1)} %bitcast.7, bf16[2,8,128,8,128]{4,3,2,1,0:T(8,128)(2,1)} %param.17, ...), kind=kLoop, calls=%fused_computation | loop fusion | flops 4194304 | bytes 16843776 | tf_op jit(solution)/shard_map/jit(_where)/select_n | solution.py:357
  112.8 0.0 copy-done
  112.8 0.6 copy.19
Async XLA Ops:
  105.3 7.5 %copy-start = (bf16[8,1024]{1,0:T(8,128)(2,1)S(1)}, bf16[8,1024]{1,0:T(8,128)(2,1)}, u32[]{:S(2)}) copy-start(bf16[8,1024]{1,0:T(8,128)(2,1)} %get-tuple-element.14) | copy-start | bytes 49156

commit v3 on v2

--- a/solution.py
+++ b/solution.py
@@ -11,8 +11,7 @@
 HEAD_DIM = 128
 RMS_EPS = 1e-6
 ROPE_THETA = 1000000.0
-POOL_MAX = 2
-VMEM_LIMIT = 67043328
+VMEM_LIMIT = 58400000
 MESH = pl.DeviceIdType.MESH
 F32 = jnp.float32
 BF16 = jnp.bfloat16
@@ -26,21 +25,28 @@
 def decode_kernel(cfg, pos_hbm, x_hbm, an_hbm, qn_hbm, kn_hbm, mn_hbm, wq_hbm, wk_hbm, wv_hbm, wo_hbm, wg_hbm, wu_hbm, wd_hbm, kc_hbm, vc_hbm,
                   y_ref, krow_ref, vrow_ref,
                   wqkv, wo, wgu, wd, kc, vc, xg, qkvs, qkvi, og, x1g, pbuf, ybuf, x1f, qs, ks, vs, os_, kro, vro, cs, sn, pos_ref, an_ref, qn_ref, kn_ref, mn_ref,
-                  z_send, z_recv, d_send, d_recv, y_send, y_recv, a_send, a_recv, down_send, down_recv, loc_sem, down_loc, in_sem):
+                  z_send, z_recv, d_send, d_recv, p_send, p_recv, a_send, a_recv, down_send, down_recv, loc_sem, down_loc, in_sem):
     layers, zn, pool, tok = cfg["layers"], cfg["zn"], cfg["pool"], cfg["tok"]
-    qh, kh = cfg["qh"], cfg["kh"]
+    qh, kh, ny = cfg["qh"], cfg["kh"], cfg["ny"]
     dm = x_hbm.shape[1]
     nq = zn * tok
     ctile = dm // zn
+    zh = zn // 2
     idx = lax.axis_index("dp")
     z, c = idx // 2, idx % 2
     part = lax.axis_index("part")
-    yi = part % pool
-    mate = part + 1 - 2 * yi
     sib = {"dp": 2 * z + (1 - c)}
-    nei = {"part": mate}
-    qmine = c * pool + yi
-    qother = c * pool + (pool - 1 - yi)
+    if pool == 4:
+        px, py = (part // ny) % 2, (part % ny) % 2
+        xnei = {"part": part + ny * (1 - 2 * px)}
+        ynei = {"part": part + 1 - 2 * py}
+    else:
+        px, py = 0, 0
+    quarter = px * 2 + py
+    sub = c * pool + quarter
+    subx = c * pool + (1 - px) * 2 + py
+    suby = c * pool + px * 2 + 1 - py
+    subd = c * pool + (1 - px) * 2 + 1 - py
 
     order = []
     for r in range(zn // 2, 0, -1):
@@ -58,8 +64,9 @@
     for r in order:
         pl.semaphore_signal(barrier, inc=1, device_id=peer_id(peer(r)), device_id_type=MESH)
     pl.semaphore_signal(barrier, inc=1, device_id=sib, device_id_type=MESH)
-    if pool == 2:
-        pl.semaphore_signal(barrier, inc=1, device_id=nei, device_id_type=MESH)
+    if pool == 4:
+        pl.semaphore_signal(barrier, inc=1, device_id=xnei, device_id_type=MESH)
+        pl.semaphore_signal(barrier, inc=1, device_id=ynei, device_id_type=MESH)
 
     def rcopy(src, dst, ss, rs, dev):
         return pltpu.make_async_remote_copy(src_ref=src, dst_ref=dst, send_sem=ss, recv_sem=rs, device_id=dev, device_id_type=MESH)
@@ -79,8 +86,8 @@
         out = []
         for src, off in srcs:
             width = src.shape[2] // zn
-            s = src.at[l, pl.ds(pl.multiple_of(yi * rows, rows), rows), pl.ds(pl.multiple_of(zt * width, 128), width)]
-            d = buf.at[l, z, qmine, :, pl.ds(off, width)]
+            s = src.at[l, pl.ds(pl.multiple_of(quarter * rows, rows), rows), pl.ds(pl.multiple_of(zt * width, 128), width)]
+            d = buf.at[l, z, sub, :, pl.ds(off, width)]
             out.append((s, d))
         return out, gi
 
@@ -96,35 +103,49 @@
             for s, d in ps:
                 rcopy(s, d, z_send.at[l, gi], z_recv.at[l, gi], peer_id(zt)).start()
 
-    def w_fwd1(l, name):
+    def w_s1(l, name):
         buf, gi, _ = groups[name]
         wait_bytes(buf.at[l, 0:zn - 1, 0], z_recv.at[l, gi])
         wait_bytes(buf.at[l, 0, 0], loc_sem.at[l, gi])
-        q = buf.at[l, :, qmine]
-        if pool == 2:
-            rcopy(q, q, y_send.at[l, gi], y_recv.at[l, gi], nei).start()
+        q = buf.at[l, :, sub]
+        if pool == 4:
+            rcopy(q, q, p_send.at[l, gi, 0], p_recv.at[l, gi, 0], xnei).start()
+            rcopy(q, q, p_send.at[l, gi, 1], p_recv.at[l, gi, 1], ynei).start()
         rcopy(q, q, d_send.at[l, gi, 0], d_recv.at[l, gi, 0], sib).start()
 
-    def w_fwd2(l, name):
-        if pool == 2:
+    def w_s2(l, name):
+        if pool == 4:
             buf, gi, _ = groups[name]
-            q = buf.at[l, :, qother]
-            wait_bytes(q, y_recv.at[l, gi])
-            rcopy(q, q, d_send.at[l, gi, 1], d_recv.at[l, gi, 1], sib).start()
+            qx, qy = buf.at[l, :, subx], buf.at[l, :, suby]
+            hx, hy = buf.at[l, 0:zh, subx], buf.at[l, zh:zn, suby]
+            wait_bytes(qx, p_recv.at[l, gi, 0])
+            rcopy(hx, hx, p_send.at[l, gi, 2], p_recv.at[l, gi, 2], ynei).start()
+            rcopy(qx, qx, d_send.at[l, gi, 1], d_recv.at[l, gi, 1], sib).start()
+            wait_bytes(qy, p_recv.at[l, gi, 1])
+            rcopy(hy, hy, p_send.at[l, gi, 3], p_recv.at[l, gi, 3], xnei).start()
+            rcopy(qy, qy, d_send.at[l, gi, 2], d_recv.at[l, gi, 2], sib).start()
+
+    def w_s3(l, name):
+        if pool == 4:
+            buf, gi, _ = groups[name]
+            q = buf.at[l, :, subd]
+            wait_bytes(buf.at[l, 0:zh, subd], p_recv.at[l, gi, 2])
+            wait_bytes(buf.at[l, zh:zn, subd], p_recv.at[l, gi, 3])
+            rcopy(q, q, d_send.at[l, gi, 3], d_recv.at[l, gi, 3], sib).start()
 
     def w_fin(l, name):
         buf, gi, _ = groups[name]
-        wait_bytes(buf.at[l, :, 0], d_recv.at[l, gi, 0])
-        if pool == 2:
-            wait_bytes(buf.at[l, :, 0], d_recv.at[l, gi, 1])
+        for i in range(pool):
+            wait_bytes(buf.at[l, :, 0], d_recv.at[l, gi, i])
 
     def w_drain(l, name):
         buf, gi, _ = groups[name]
         wait_bytes(buf.at[l, 0:zn - 1, 0], z_send.at[l, gi])
-        wait_bytes(buf.at[l, :, 0], d_send.at[l, gi, 0])
-        if pool == 2:
-            wait_bytes(buf.at[l, :, 0], y_send.at[l, gi])
-            wait_bytes(buf.at[l, :, 0], d_send.at[l, gi, 1])
+        for i in range(pool):
+            wait_bytes(buf.at[l, :, 0], d_send.at[l, gi, i])
+        if pool == 4:
+            for i in range(4):
+                wait_bytes(buf.at[l, :, 0] if i < 2 else buf.at[l, 0:zh, 0], p_send.at[l, gi, i])
 
     def spread(src_of, dst, l, ph):
         for r in order:
@@ -133,6 +154,24 @@
 
     def arrived(buf, l, ph):
         wait_bytes(buf.at[l, 0:zn - 1], a_recv.at[l, ph])
+
+    plan = {
+        (0, "x_sent"): [(w_send, 0, "qkv")],
+        (0, "x_in"): [(w_s1, 0, "qkv"), (w_send, 0, "o"), (w_send, 0, "gu"), (w_s2, 0, "qkv"), (w_send, 1, "qkv"), (w_s3, 0, "qkv")],
+        (0, "qkv_sent"): [(w_s1, 0, "o")],
+        (0, "qkv_in"): [(w_send, 1, "o"), (w_send, 1, "gu"), (w_s1, 0, "gu"), (w_s2, 0, "o")],
+        (0, "o_sent"): [(w_s3, 0, "o"), (w_s2, 0, "gu"), (w_s1, 1, "qkv")],
+        (0, "x1_sent"): [(w_s3, 0, "gu")],
+        (0, "x1_in"): [(w_s2, 1, "qkv")],
+        (0, "y_sent"): [(w_s3, 1, "qkv"), (w_s1, 1, "o")],
+        (1, "x_sent"): [(w_s2, 1, "o"), (w_s1, 1, "gu")],
+        (1, "qkv_sent"): [(w_s3, 1, "o"), (w_s2, 1, "gu")],
+        (1, "qkv_in"): [(w_s3, 1, "gu")],
+    }
+
+    def background(l, point):
+        for fn, wl, name in plan.get((l, point), ()):
+            fn(wl, name)
 
     smalls = [(x_hbm, xg.at[0, z]), (pos_hbm, pos_ref), (an_hbm, an_ref), (qn_hbm, qn_ref), (kn_hbm, kn_ref), (mn_hbm, mn_ref)]
     small_copies = [pltpu.make_async_copy(s, d, in_sem.at[i]) for i, (s, d) in enumerate(smalls)]
@@ -145,11 +184,11 @@
         pltpu.make_async_copy(kc_hbm.at[l], kc.at[l], down_loc.at[l, 1]).start()
         pltpu.make_async_copy(vc_hbm.at[l], vc.at[l], down_loc.at[l, 2]).start()
 
-    pl.semaphore_wait(barrier, zn + pool - 1)
+    pl.semaphore_wait(barrier, zn + (2 if pool == 4 else 0))
 
     small_copies[0].wait()
     spread(lambda zt: xg.at[0, z], xg.at[0, z], 0, 0)
-    w_send(0, "qkv")
+    background(0, "x_sent")
     for l in range(layers):
         rcopy(wd_hbm.at[l], wd.at[l, c], down_send.at[l], down_recv.at[l], sib).start()
 
@@ -167,8 +206,6 @@
     cs[...] = jnp.cos(ang)
     sin_tab = jnp.sin(ang)
     sn[...] = jnp.where(lane_id >= half, sin_tab, -sin_tab)
-
-    w_send(0, "o")
 
     def head_norm(v, gain):
         v = rms(v, HEAD_DIM) * gain
@@ -199,48 +236,44 @@
         mine = lax.rem(lane, kh) == lax.shift_right_logical(row, 1)
         slot = jnp.where(mine, lax.div(lane, kh), cols)
         scale = HEAD_DIM ** -0.5
-        for n in range(tok):
-            q = qs[n * qh:(n + 1) * qh, :]
-            s_new = jnp.sum(q * ks[n * qh:(n + 1) * qh, :], axis=-1, keepdims=True) * scale
-            s = lax.dot_general(q.astype(BF16), kc[l, n], (((1,), (1,)), ((), ())), preferred_element_type=F32) * scale
-            s = jnp.where(slot < pos_ref[n], s, NEG)
-            m = jnp.maximum(jnp.max(s, axis=-1, keepdims=True), s_new)
-            e = jnp.exp(s - m)
-            e_new = jnp.exp(s_new - m)
-            den = jnp.sum(e, axis=-1, keepdims=True) + e_new
-            p = (e / den).astype(BF16)
-            p_new = (e_new / den).astype(BF16).astype(F32)
-            o = jnp.dot(p, vc[l, n], preferred_element_type=F32) + p_new * vs[n * qh:(n + 1) * qh, :]
-            os_[n * qh:(n + 1) * qh, :] = o
+        for n0 in range(0, tok, 4):
+            seqs = range(n0, n0 + 4)
+            rows = [slice(n * qh, (n + 1) * qh) for n in seqs]
+            q = [qs[r, :] for r in rows]
+            s = [lax.dot_general(a.astype(BF16), kc[l, n], (((1,), (1,)), ((), ())), preferred_element_type=F32) * scale for a, n in zip(q, seqs)]
+            s_new = [jnp.sum(a * ks[r, :], axis=-1, keepdims=True) * scale for a, r in zip(q, rows)]
+            s = [jnp.where(slot < pos_ref[n], a, NEG) for a, n in zip(s, seqs)]
+            m = [jnp.maximum(jnp.max(a, axis=-1, keepdims=True), b) for a, b in zip(s, s_new)]
+            e = [jnp.exp(a - b) for a, b in zip(s, m)]
+            e_new = [jnp.exp(a - b) for a, b in zip(s_new, m)]
+            inv = [1.0 / (jnp.sum(a, axis=-1, keepdims=True) + b) for a, b in zip(e, e_new)]
+            p = [(a * b).astype(BF16) for a, b in zip(e, inv)]
+            p_new = [(a * b).astype(BF16).astype(F32) for a, b in zip(e_new, inv)]
+            for a, b, r, n in zip(p, p_new, rows, seqs):
+                os_[r, :] = jnp.dot(a, vc[l, n], preferred_element_type=F32) + b * vs[r, :]
         for h in range(qh):
             og[l, z, :, h * HEAD_DIM:(h + 1) * HEAD_DIM] = os_[pl.ds(h, tok, stride=qh), :].astype(BF16)
 
     for l in range(layers):
         last = l == layers - 1
-        if l == 0:
-            w_send(0, "gu")
         arrived(xg, l, 0)
         h = (rms(gathered_x(l), dm) * an_ref[l:l + 1, :].astype(F32)).astype(BF16)
-        if l == 0:
-            w_fwd1(l, "qkv")
-            w_fwd2(l, "qkv")
+        background(l, "x_in")
         w_fin(l, "qkv")
         r = jnp.dot(h, wqkv[l].reshape(dm, wqkv.shape[-1]), preferred_element_type=F32)
         qkvs[l] = r.reshape(zn, tok, wqkv.shape[-1]).astype(BF16)
+        spread(lambda zt: qkvs.at[l, zt], qkvi.at[l, z], l, 1)
         qkvi[l, z] = qkvs[l, z]
-        spread(lambda zt: qkvs.at[l, zt], qkvi.at[l, z], l, 1)
-        w_fwd1(l, "o")
+        background(l, "qkv_sent")
         if l == 0:
             for k in range(layers):
                 wait_bytes(kc.at[k], down_loc.at[k, 1])
                 wait_bytes(vc.at[k], down_loc.at[k, 2])
         arrived(qkvi, l, 1)
+        background(l, "qkv_in")
         attention(l)
         spread(lambda zt: og.at[l, z], og.at[l, z], l, 2)
-        if not last:
-            w_send(l + 1, "qkv")
-        w_fwd2(l, "o")
-        w_fwd1(l, "gu")
+        background(l, "o_sent")
         w_fin(l, "o")
         arrived(og, l, 2)
         o_all = og[l].astype(F32).reshape(nq, og.shape[-1]).astype(BF16)
@@ -248,13 +281,12 @@
         xc = xg[l, :, :, pl.ds(pl.multiple_of(z * ctile, ctile), ctile)].astype(F32).reshape(nq, ctile)
         x1g[l, z] = (xc + r).astype(BF16)
         spread(lambda zt: x1g.at[l, z], x1g.at[l, z], l, 3)
-        if not last:
-            w_send(l + 1, "o")
-        w_fwd2(l, "gu")
+        background(l, "x1_sent")
         wait_bytes(wd.at[l, 0], down_loc.at[l, 0])
         wait_bytes(wd.at[l, 0], down_recv.at[l])
         w_fin(l, "gu")
         arrived(x1g, l, 3)
+        background(l, "x1_in")
         x1 = jnp.concatenate([x1g[l, zz].astype(F32) for zz in range(zn)], axis=-1)
         x1f[...] = x1
         h2 = (rms(x1, dm) * mn_ref[l:l + 1, :].astype(F32)).astype(BF16)
@@ -264,12 +296,9 @@
         a = (g * jax.nn.sigmoid(g) * gu[:, ffc:]).astype(BF16)
         pr = jnp.dot(a, wd[l].reshape(ffc, dm), preferred_element_type=F32)
         pbuf[l] = pr.reshape(zn, tok, dm)
+        spread(lambda zt: pbuf.at[l, zt], ybuf.at[l, z], l, 4)
         ybuf[l, z] = pbuf[l, z]
-        spread(lambda zt: pbuf.at[l, zt], ybuf.at[l, z], l, 4)
-        if not last:
-            w_send(l + 1, "gu")
-            w_fwd1(l + 1, "qkv")
-            w_fwd2(l + 1, "qkv")
+        background(l, "y_sent")
         arrived(ybuf, l, 4)
         total = ybuf[l, 0]
         for zz in range(1, zn):
@@ -280,6 +309,7 @@
         else:
             xg[l + 1, z] = y
             spread(lambda zt: xg.at[l + 1, z], xg.at[l + 1, z], l + 1, 0)
+            background(l + 1, "x_sent")
 
     for l in range(layers):
         for name in ("qkv", "o", "gu"):
@@ -298,7 +328,8 @@
     in_specs = (act_spec, P(batch_axes), cache_spec, cache_spec, gain_spec, mat_spec, mat_spec, mat_spec, gain_spec, gain_spec, mat_spec, gain_spec, mat_spec, mat_spec, mat_spec)
     out_specs = (act_spec, cache_spec, cache_spec)
     zn = mesh.shape["dp"] // 2
-    pool = POOL_MAX if mesh.shape["part"] % POOL_MAX == 0 else 1
+    ny = math.isqrt(mesh.shape["part"])
+    pool = 4 if ny * ny == mesh.shape["part"] and ny % 2 == 0 else 1
 
     def device_fn(x, positions, k_cache, v_cache, attn_norm, w_q, w_k, w_v, q_norm, k_norm, w_o, mlp_norm, w_gate, w_up, w_down):
         layers, tok, slots, kh, hd = k_cache.shape
@@ -307,7 +338,7 @@
         qh = qw // hd
         nq = 2 * pool
         qkvc = (qw + 2 * kw) // zn
-        cfg = dict(layers=layers, zn=zn, pool=pool, tok=tok, qh=qh, kh=kh)
+        cfg = dict(layers=layers, zn=zn, pool=pool, ny=ny, tok=tok, qh=qh, kh=kh)
         vm = pl.BlockSpec(memory_space=pltpu.VMEM)
         hb = pl.BlockSpec(memory_space=pltpu.HBM)
         dma = pltpu.SemaphoreType.DMA
@@ -340,7 +371,7 @@
             pltpu.VMEM((layers, hd), BF16),
             pltpu.VMEM((layers, hd), BF16),
             pltpu.VMEM((layers, dm), BF16),
-            dma((layers, 3)), dma((layers, 3)), dma((layers, 3, 2)), dma((layers, 3, 2)), dma((layers, 3)), dma((layers, 3)),
+            dma((layers, 3)), dma((layers, 3)), dma((layers, 3, pool)), dma((layers, 3, pool)), dma((layers, 3, 4)), dma((layers, 3, 4)),
             dma((layers, 5)), dma((layers, 5)), dma((layers,)), dma((layers,)), dma((layers, 3)), dma((layers, 3)), dma((6,)),
         ]
         y, krow, vrow = pl.pallas_call(

time: 113 us -> 100 us (0.88); the launches traced: 113 us -> 99 us
  Pallas kernels: 103 us -> 92.2 us
  other arithmetic: 8.75 us -> 5.53 us
    pallas_call x1, Pallas kernels: 103 us -> 92.2 us  [device_fn(): pl.pallas_call(functools.partial(decode_kernel, cfg), name='decode', out_...]
    select_n x1, other arithmetic: 7.46 us -> 4.81 us  [device_fn(): v_out = jnp.where(slot_hit, vrow.reshape(layers, tok, 1, kh, hd), v_cache)]
where the time goes in v3:
time: 100 us; the launch traced here: 99 us
  Pallas kernels  92.2 us (92%)
  other arithmetic  5.53 us (6%)
    pallas_call x1, Pallas kernels, device_fn(): pl.pallas_call(functools.partial(decode_kernel, cfg), name='decode', out_...  92.2 us
    select_n x1, other arithmetic, device_fn(): v_out = jnp.where(slot_hit, vrow.reshape(layers, tok, 1, kh, hd), v_cache)  4.81 us

profile of v3, /device:TPU:21, one launch (start us, length us, event | category | flops | bytes accessed | tf_op | source)
XLA Modules:
  0.0 99.0 jit_solution(16031737845837641284)
XLA Ops:
  0.6 0.7 iota_compare_fusion
  1.4 0.0 copy-start
  1.4 0.0 copy-start.1
  1.4 92.2 %decode.1 = (bf16[8,1024]{1,0:T(8,128)(2,1)}, bf16[2,64,128]{2,1,0:T(8,128)(2,1)}, bf16[2,64,128]{2,1,0:T(8,128)(2,1)}) custom-call(s32[8]{0:T(128)} %pos_hbm.1, bf16[8,1024]{1,0:T(8,128)(2,1)} %x_hbm.1, bf16[2,1024]{1,0:T(2,128)(2,1)} %an_hbm.1, bf16[2,128]{1,0:T(2,128)(2,1)} %qn_hbm.1, bf16[2,128]{1,0:T(2,128)(2,1)} %kn_hbm.1, bf16[2,1024]{1,0:T(2,128)(2,1)} %mn_hbm.1, ...), custom_call_target="tpu_custom_call" | custom-call | tf_op jit(solution)/shard_map/decode/pallas_call | solution.py:377
  93.5 0.0 copy-done
  93.6 0.0 copy-done.1
  93.6 0.0 copy-start.2
  93.6 4.8 %broadcast_select_fusion = (bf16[2,8,128,8,128]{4,3,2,1,0:T(8,128)(2,1)}, bf16[2,8,128,8,128]{4,3,2,1,0:T(8,128)(2,1)}) fusion(bf16[2,8,128,8,128]{4,3,2,1,0:T(8,128)(2,1)S(1)} %copy-done.1, pred[8,128]{1,0:T(8,128)(4,1)S(1)} %iota_compare_fusion, bf16[2,8,8,128]{3,2,1,0:T(8,128)(2,1)} %bitcast.7, bf16[2,8,128,8,128]{4,3,2,1,0:T(8,128)(2,1)S(1)} %copy-done, ...), kind=kLoop, calls=%fused_computation | loop fusion | flops 4194304 | bytes 16843776 | tf_op jit(solution)/shard_map/jit(_where)/select_n | solution.py:388
  98.4 0.0 copy-done.2
  98.4 0.6 copy.19
Async XLA Ops:
  1.4 92.2 %copy-start = (bf16[2,8,128,8,128]{4,3,2,1,0:T(8,128)(2,1)S(1)}, bf16[2,8,128,8,128]{4,3,2,1,0:T(8,128)(2,1)}, u32[]{:S(2)}) copy-start(bf16[2,8,128,8,128]{4,3,2,1,0:T(8,128)(2,1)} %param.17) | copy-start | bytes 12582916
  1.4 92.2 %copy-start.1 = (bf16[2,8,128,8,128]{4,3,2,1,0:T(8,128)(2,1)S(1)}, bf16[2,8,128,8,128]{4,3,2,1,0:T(8,128)(2,1)}, u32[]{:S(2)}) copy-start(bf16[2,8,128,8,128]{4,3,2,1,0:T(8,128)(2,1)} %param.18) | copy-start | bytes 12582916
  93.6 4.8 %copy-start.2 = (bf16[8,1024]{1,0:T(8,128)(2,1)S(1)}, bf16[8,1024]{1,0:T(8,128)(2,1)}, u32[]{:S(2)}) copy-start(bf16[8,1024]{1,0:T(8,128)(2,1)} %get-tuple-element.14) | copy-start | bytes 49156

commit v4 on v3

--- a/solution.py
+++ b/solution.py
@@ -12,6 +12,9 @@
 RMS_EPS = 1e-6
 ROPE_THETA = 1000000.0
 VMEM_LIMIT = 58400000
+PLACE_LIMIT = 8 * 1024 * 1024
+RES_BLOCKS = 4096
+
 MESH = pl.DeviceIdType.MESH
 F32 = jnp.float32
 BF16 = jnp.bfloat16
@@ -23,9 +26,9 @@
 
 
 def decode_kernel(cfg, pos_hbm, x_hbm, an_hbm, qn_hbm, kn_hbm, mn_hbm, wq_hbm, wk_hbm, wv_hbm, wo_hbm, wg_hbm, wu_hbm, wd_hbm, kc_hbm, vc_hbm,
-                  y_ref, krow_ref, vrow_ref,
-                  wqkv, wo, wgu, wd, kc, vc, xg, qkvs, qkvi, og, x1g, pbuf, ybuf, x1f, qs, ks, vs, os_, kro, vro, cs, sn, pos_ref, an_ref, qn_ref, kn_ref, mn_ref,
-                  z_send, z_recv, d_send, d_recv, p_send, p_recv, a_send, a_recv, down_send, down_recv, loc_sem, down_loc, in_sem):
+                  res_hbm,
+                  wq, wkv, wo, wgu, wd, kc, vc, xg, qkvs, qkvi, og, x1g, pbuf, ybuf, x1f, qs, ks, vs, os_, kro, vro, cs, sn, pos_ref, an_ref, qn_ref, kn_ref, mn_ref, y_ref, krow_ref, vrow_ref,
+                  z_send, z_recv, d_send, d_recv, p_send, p_recv, a_send, a_recv, down_send, down_recv, loc_sem, down_loc, in_sem, out_sem):
     layers, zn, pool, tok = cfg["layers"], cfg["zn"], cfg["pool"], cfg["tok"]
     qh, kh, ny = cfg["qh"], cfg["kh"], cfg["ny"]
     dm = x_hbm.shape[1]
@@ -75,9 +78,10 @@
         pltpu.make_async_copy(ref, ref, sem).wait()
 
     groups = {
-        "qkv": (wqkv, 0, [(wq_hbm, 0), (wk_hbm, 2 * HEAD_DIM), (wv_hbm, 3 * HEAD_DIM)]),
-        "o": (wo, 1, [(wo_hbm, 0)]),
-        "gu": (wgu, 2, [(wg_hbm, 0), (wu_hbm, wgu.shape[-1] // 2)]),
+        "q": (wq, 0, [(wq_hbm, 0)]),
+        "kv": (wkv, 1, [(wk_hbm, 0), (wv_hbm, wkv.shape[-1] // 2)]),
+        "o": (wo, 2, [(wo_hbm, 0)]),
+        "gu": (wgu, 3, [(wg_hbm, 0), (wu_hbm, wgu.shape[-1] // 2)]),
     }
 
     def pieces(l, name, zt):
@@ -156,17 +160,17 @@
         wait_bytes(buf.at[l, 0:zn - 1], a_recv.at[l, ph])
 
     plan = {
-        (0, "x_sent"): [(w_send, 0, "qkv")],
-        (0, "x_in"): [(w_s1, 0, "qkv"), (w_send, 0, "o"), (w_send, 0, "gu"), (w_s2, 0, "qkv"), (w_send, 1, "qkv"), (w_s3, 0, "qkv")],
-        (0, "qkv_sent"): [(w_s1, 0, "o")],
-        (0, "qkv_in"): [(w_send, 1, "o"), (w_send, 1, "gu"), (w_s1, 0, "gu"), (w_s2, 0, "o")],
-        (0, "o_sent"): [(w_s3, 0, "o"), (w_s2, 0, "gu"), (w_s1, 1, "qkv")],
-        (0, "x1_sent"): [(w_s3, 0, "gu")],
-        (0, "x1_in"): [(w_s2, 1, "qkv")],
-        (0, "y_sent"): [(w_s3, 1, "qkv"), (w_s1, 1, "o")],
-        (1, "x_sent"): [(w_s2, 1, "o"), (w_s1, 1, "gu")],
-        (1, "qkv_sent"): [(w_s3, 1, "o"), (w_s2, 1, "gu")],
-        (1, "qkv_in"): [(w_s3, 1, "gu")],
+        (0, "entry"): [(w_send, 0, "q"), (w_send, 0, "kv")],
+        (0, "x_in"): [(w_s1, 0, "q"), (w_send, 0, "o"), (w_s1, 0, "kv"), (w_send, 0, "gu"), (w_s2, 0, "q"), (w_s2, 0, "kv"), (w_s3, 0, "q"), (w_s3, 0, "kv")],
+        (0, "qkv_sent"): [(w_send, 1, "q"), (w_send, 1, "kv"), (w_send, 1, "o"), (w_s1, 0, "o")],
+        (0, "qkv_in"): [(w_s1, 0, "gu"), (w_s2, 0, "o")],
+        (0, "o_sent"): [(w_s3, 0, "o"), (w_s2, 0, "gu"), (w_s1, 1, "q"), (w_s1, 1, "kv")],
+        (0, "x1_sent"): [(w_send, 1, "gu"), (w_s3, 0, "gu")],
+        (0, "x1_in"): [(w_s2, 1, "q"), (w_s2, 1, "kv"), (w_s1, 1, "o")],
+        (0, "y_sent"): [(w_s3, 1, "q"), (w_s3, 1, "kv"), (w_s2, 1, "o")],
+        (1, "x_sent"): [(w_s3, 1, "o"), (w_s1, 1, "gu")],
+        (1, "qkv_sent"): [(w_s2, 1, "gu")],
+        (1, "o_sent"): [(w_s3, 1, "gu")],
     }
 
     def background(l, point):
@@ -179,16 +183,16 @@
         cp.start()
     for l in range(layers):
         pltpu.make_async_copy(wd_hbm.at[l], wd.at[l, c], down_loc.at[l, 0]).start()
-        for name in ("qkv", "o", "gu"):
+        for name in groups:
             w_local(l, name)
         pltpu.make_async_copy(kc_hbm.at[l], kc.at[l], down_loc.at[l, 1]).start()
         pltpu.make_async_copy(vc_hbm.at[l], vc.at[l], down_loc.at[l, 2]).start()
 
     pl.semaphore_wait(barrier, zn + (2 if pool == 4 else 0))
 
+    background(0, "entry")
     small_copies[0].wait()
     spread(lambda zt: xg.at[0, z], xg.at[0, z], 0, 0)
-    background(0, "x_sent")
     for l in range(layers):
         rcopy(wd_hbm.at[l], wd.at[l, c], down_send.at[l], down_recv.at[l], sib).start()
 
@@ -206,6 +210,8 @@
     cs[...] = jnp.cos(ang)
     sin_tab = jnp.sin(ang)
     sn[...] = jnp.where(lane_id >= half, sin_tab, -sin_tab)
+
+    outs = []
 
     def head_norm(v, gain):
         v = rms(v, HEAD_DIM) * gain
@@ -230,6 +236,10 @@
             vro[pl.ds(h, tok, stride=kh), :] = v
         krow_ref[l] = kro[...].astype(BF16)
         vrow_ref[l] = vro[...].astype(BF16)
+        outs.append(pltpu.make_async_copy(krow_ref.at[l], res_hbm.at[1 + 2 * l], out_sem.at[1 + 2 * l]))
+        outs.append(pltpu.make_async_copy(vrow_ref.at[l], res_hbm.at[2 + 2 * l], out_sem.at[2 + 2 * l]))
+        outs[-2].start()
+        outs[-1].start()
         cols = kc.shape[2]
         lane = lax.broadcasted_iota(jnp.int32, (qh, cols), 1)
         row = lax.broadcasted_iota(jnp.int32, (qh, cols), 0)
@@ -259,9 +269,12 @@
         arrived(xg, l, 0)
         h = (rms(gathered_x(l), dm) * an_ref[l:l + 1, :].astype(F32)).astype(BF16)
         background(l, "x_in")
-        w_fin(l, "qkv")
-        r = jnp.dot(h, wqkv[l].reshape(dm, wqkv.shape[-1]), preferred_element_type=F32)
-        qkvs[l] = r.reshape(zn, tok, wqkv.shape[-1]).astype(BF16)
+        for name, lo in (("q", 0), ("kv", wq.shape[-1])):
+            w_fin(l, name)
+            buf = groups[name][0]
+            cols = buf.shape[-1]
+            r = jnp.dot(h, buf[l].reshape(dm, cols), preferred_element_type=F32)
+            qkvs[l, :, :, lo:lo + cols] = r.reshape(zn, tok, cols).astype(BF16)
         spread(lambda zt: qkvs.at[l, zt], qkvi.at[l, z], l, 1)
         qkvi[l, z] = qkvs[l, z]
         background(l, "qkv_sent")
@@ -303,20 +316,51 @@
         total = ybuf[l, 0]
         for zz in range(1, zn):
             total = total + ybuf[l, zz]
-        y = (x1f[pl.ds(pl.multiple_of(z * tok, tok), tok), :] + total).astype(BF16)
+        y = x1f[pl.ds(pl.multiple_of(z * tok, tok), tok), :] + total
         if last:
-            y_ref[...] = y
+            y_ref[...] = jnp.concatenate([y[:, t * HEAD_DIM:(t + 1) * HEAD_DIM] for t in range(dm // HEAD_DIM)], axis=0).astype(BF16)
+            outs.append(pltpu.make_async_copy(y_ref, res_hbm.at[0], out_sem.at[0]))
+            outs[-1].start()
         else:
-            xg[l + 1, z] = y
+            xg[l + 1, z] = y.astype(BF16)
             spread(lambda zt: xg.at[l + 1, z], xg.at[l + 1, z], l + 1, 0)
             background(l + 1, "x_sent")
 
     for l in range(layers):
-        for name in ("qkv", "o", "gu"):
+        for name in groups:
             w_drain(l, name)
         wait_bytes(wd.at[l, 0], down_send.at[l])
         for ph, buf in enumerate((xg, qkvi, og, x1g, ybuf)):
             wait_bytes(buf.at[l, 0:zn - 1], a_send.at[l, ph])
+    for cp in outs:
+        cp.wait()
+
+
+def place_rows(layers, tok, kh, pos_hbm, res_hbm, kin, vin, y_out, kout, vout, pos_ref, res, in_sem, y_sem, bulk_sem, row_sem):
+    small = [pltpu.make_async_copy(pos_hbm, pos_ref, in_sem.at[0]), pltpu.make_async_copy(res_hbm.at[0:1 + 2 * layers], res, in_sem.at[1])]
+    for cp in small:
+        cp.start()
+    pairs = ((kin, kout), (vin, vout))
+    bulk = [[[pltpu.make_async_copy(src.at[l, n], dst.at[l, n], bulk_sem.at[i, l, n]) for n in range(tok)] for l in range(layers)] for i, (src, dst) in enumerate(pairs)]
+    for l in range(layers):
+        for n in range(tok):
+            for i in range(2):
+                bulk[i][l][n].start()
+    for cp in small:
+        cp.wait()
+    done = [pltpu.make_async_copy(res.at[0, pl.ds(t * tok, tok)], y_out.at[:, pl.ds(t * HEAD_DIM, HEAD_DIM)], y_sem.at[t]) for t in range(y_out.shape[1] // HEAD_DIM)]
+    for cp in done:
+        cp.start()
+    for l in range(layers):
+        for n in range(tok):
+            at = pl.ds(pl.multiple_of(pos_ref[n] * kh, kh), kh)
+            for i, (_, dst) in enumerate(pairs):
+                bulk[i][l][n].wait()
+                cp = pltpu.make_async_copy(res.at[1 + 2 * l + i, pl.ds(n * kh, kh)], dst.at[l, n, at], row_sem.at[i, l, n])
+                cp.start()
+                done.append(cp)
+    for cp in done:
+        cp.wait()
 
 
 def solution(mesh):
@@ -339,12 +383,12 @@
         nq = 2 * pool
         qkvc = (qw + 2 * kw) // zn
         cfg = dict(layers=layers, zn=zn, pool=pool, ny=ny, tok=tok, qh=qh, kh=kh)
-        vm = pl.BlockSpec(memory_space=pltpu.VMEM)
         hb = pl.BlockSpec(memory_space=pltpu.HBM)
         dma = pltpu.SemaphoreType.DMA
         flat = (layers, tok, slots * kh, hd)
         scratch = [
-            pltpu.VMEM((layers, zn, nq, w_q.shape[1] // pool, qkvc), BF16),
+            pltpu.VMEM((layers, zn, nq, w_q.shape[1] // pool, qw // zn), BF16),
+            pltpu.VMEM((layers, zn, nq, w_k.shape[1] // pool, 2 * kw // zn), BF16),
             pltpu.VMEM((layers, zn, nq, w_o.shape[1] // pool, dm // zn), BF16),
             pltpu.VMEM((layers, zn, nq, w_gate.shape[1] // pool, 2 * ff // zn), BF16),
             pltpu.VMEM((layers, 2, w_down.shape[1], dm), BF16),
@@ -371,21 +415,34 @@
             pltpu.VMEM((layers, hd), BF16),
             pltpu.VMEM((layers, hd), BF16),
             pltpu.VMEM((layers, dm), BF16),
-            dma((layers, 3)), dma((layers, 3)), dma((layers, 3, pool)), dma((layers, 3, pool)), dma((layers, 3, 4)), dma((layers, 3, 4)),
-            dma((layers, 5)), dma((layers, 5)), dma((layers,)), dma((layers,)), dma((layers, 3)), dma((layers, 3)), dma((6,)),
+            pltpu.VMEM((tok * kh, hd), BF16),
+            pltpu.VMEM((layers, tok * kh, hd), BF16),
+            pltpu.VMEM((layers, tok * kh, hd), BF16),
+            dma((layers, 4)), dma((layers, 4)), dma((layers, 4, pool)), dma((layers, 4, pool)), dma((layers, 4, 4)), dma((layers, 4, 4)),
+            dma((layers, 5)), dma((layers, 5)), dma((layers,)), dma((layers,)), dma((layers, 4)), dma((layers, 3)), dma((6,)), dma((1 + 2 * layers,)),
         ]
-        y, krow, vrow = pl.pallas_call(
+        res = pl.pallas_call(
             functools.partial(decode_kernel, cfg),
             name="decode",
-            out_shape=(jax.ShapeDtypeStruct((tok, dm), BF16), jax.ShapeDtypeStruct((layers, tok * kh, hd), BF16), jax.ShapeDtypeStruct((layers, tok * kh, hd), BF16)),
+            out_shape=jax.ShapeDtypeStruct((RES_BLOCKS, tok * kh, hd), BF16),
             in_specs=[hb] * 15,
-            out_specs=(vm, vm, vm),
+            out_specs=hb,
             scratch_shapes=scratch,
             compiler_params=pltpu.CompilerParams(collective_id=0, has_side_effects=True, vmem_limit_bytes=VMEM_LIMIT),
         )(positions, x, attn_norm, q_norm, k_norm, mlp_norm, w_q, w_k, w_v, w_o, w_gate, w_up, w_down, k_cache.reshape(flat), v_cache.reshape(flat))
-        slot_hit = (jnp.arange(slots)[None, :] == positions[:, None])[None, :, :, None, None]
-        k_out = jnp.where(slot_hit, krow.reshape(layers, tok, 1, kh, hd), k_cache)
-        v_out = jnp.where(slot_hit, vrow.reshape(layers, tok, 1, kh, hd), v_cache)
+        anys = pl.BlockSpec(memory_space=pl.ANY)
+        rows = (1 + 2 * layers, tok * kh, hd)
+        y, k_out, v_out = pl.pallas_call(
+            functools.partial(place_rows, layers, tok, kh),
+            name="place",
+            out_shape=(jax.ShapeDtypeStruct((tok, dm), BF16), jax.ShapeDtypeStruct(flat, BF16), jax.ShapeDtypeStruct(flat, BF16)),
+            in_specs=[anys] * 4,
+            out_specs=(anys,) * 3,
+            scratch_shapes=[pltpu.SMEM((tok,), jnp.int32), pltpu.VMEM(rows, BF16), dma((2,)), dma((dm // hd,)), dma((2, layers, tok)), dma((2, layers, tok))],
+            compiler_params=pltpu.CompilerParams(vmem_limit_bytes=PLACE_LIMIT),
+        )(positions, res, k_cache.reshape(flat), v_cache.reshape(flat))
+        k_out = k_out.reshape(k_cache.shape)
+        v_out = v_out.reshape(v_cache.shape)
         return y, k_out, v_out
 
     return jax.shard_map(device_fn, mesh=mesh, in_specs=in_specs, out_specs=out_specs, check_vma=False)

time: 100 us -> 95.5 us (0.955)
  other arithmetic: 5.53 us -> 0 us
  Pallas kernels: 92.2 us -> 94.3 us
    select_n x1 -> x0, other arithmetic: 4.81 us -> none  [device_fn(): v_out = jnp.where(slot_hit, vrow.reshape(layers, tok, 1, kh, hd), v_cache)]
    pallas_call x0 -> x1, Pallas kernels: none -> 4.49 us  [device_fn(): pl.pallas_call(functools.partial(place_rows, layers, tok, kh), name='plac...]
    pallas_call x1, Pallas kernels: 92.2 us -> 89.8 us  [device_fn(): pl.pallas_call(functools.partial(decode_kernel, cfg), name='decode', out_...]
where the time goes in v4:
time: 95.5 us; the launch traced here: 95 us
  Pallas kernels  94.3 us (99%)
    pallas_call x1, Pallas kernels, device_fn(): pl.pallas_call(functools.partial(decode_kernel, cfg), name='decode', out_...  89.8 us
    pallas_call x1, Pallas kernels, device_fn(): pl.pallas_call(functools.partial(place_rows, layers, tok, kh), name='plac...  4.49 us

profile of v4, /device:TPU:21, one launch (start us, length us, event | category | flops | bytes accessed | tf_op | source)
XLA Modules:
  0.0 95.0 jit_solution(1756701143348688864)
XLA Ops:
  0.6 0.0 copy-start
  0.6 0.0 copy-start.1
  0.7 0.0 copy-start.2
  0.7 89.8 %decode.1.res_hbm = bf16[4096,64,128]{2,1,0:T(8,128)(2,1)} custom-call(s32[8]{0:T(128)} %pos_hbm.3, bf16[8,1024]{1,0:T(8,128)(2,1)} %x_hbm.1, bf16[2,1024]{1,0:T(2,128)(2,1)} %an_hbm.1, bf16[2,128]{1,0:T(2,128)(2,1)} %qn_hbm.1, bf16[2,128]{1,0:T(2,128)(2,1)} %kn_hbm.1, bf16[2,1024]{1,0:T(2,128)(2,1)} %mn_hbm.1, bf16[2,64,2048]{2,1,0:T(8,128)(2,1)} %wq_hbm.1, ...), custom_call_target="tpu_custom_call" | custom-call | tf_op jit(solution)/shard_map/decode/pallas_call | solution.py:424
  90.5 0.0 copy-done
  90.5 0.0 copy-done.1
  90.5 0.0 copy-done.2
  90.5 4.5 %place.1 = (bf16[8,1024]{1,0:T(8,128)(2,1)}, bf16[2,8,1024,128]{3,2,1,0:T(8,128)(2,1)}, bf16[2,8,1024,128]{3,2,1,0:T(8,128)(2,1)}) custom-call(s32[8]{0:T(128)S(1)} %copy-done.2, bf16[4096,64,128]{2,1,0:T(8,128)(2,1)} %decode.1.res_hbm, bf16[2,8,1024,128]{3,2,1,0:T(8,128)(2,1)S(1)} %bitcast.5, bf16[2,8,1024,128]{3,2,1,0:T(8,128)(2,1)S(1)} %bitcast.7), custom_call_target="tpu_custom_call" | custom-call | tf_op jit(solution)/shard_map/place/pallas_call | solution.py:435
Async XLA Ops:
  0.6 89.9 %copy-start = (bf16[2,8,128,8,128]{4,3,2,1,0:T(8,128)(2,1)S(1)}, bf16[2,8,128,8,128]{4,3,2,1,0:T(8,128)(2,1)}, u32[]{:S(2)}) copy-start(bf16[2,8,128,8,128]{4,3,2,1,0:T(8,128)(2,1)} %param.17) | copy-start | bytes 12582916
  0.6 89.9 %copy-start.1 = (bf16[2,8,128,8,128]{4,3,2,1,0:T(8,128)(2,1)S(1)}, bf16[2,8,128,8,128]{4,3,2,1,0:T(8,128)(2,1)}, u32[]{:S(2)}) copy-start(bf16[2,8,128,8,128]{4,3,2,1,0:T(8,128)(2,1)} %param.18) | copy-start | bytes 12582916
  0.7 89.9 %copy-start.2 = (s32[8]{0:T(128)S(1)}, s32[8]{0:T(128)}, u32[]{:S(2)}) copy-start(s32[8]{0:T(128)} %pos_hbm.3) | copy-start | bytes 100

commit v5 on v4

--- a/solution.py
+++ b/solution.py
@@ -28,7 +28,7 @@
 def decode_kernel(cfg, pos_hbm, x_hbm, an_hbm, qn_hbm, kn_hbm, mn_hbm, wq_hbm, wk_hbm, wv_hbm, wo_hbm, wg_hbm, wu_hbm, wd_hbm, kc_hbm, vc_hbm,
                   res_hbm,
                   wq, wkv, wo, wgu, wd, kc, vc, xg, qkvs, qkvi, og, x1g, pbuf, ybuf, x1f, qs, ks, vs, os_, kro, vro, cs, sn, pos_ref, an_ref, qn_ref, kn_ref, mn_ref, y_ref, krow_ref, vrow_ref,
-                  z_send, z_recv, d_send, d_recv, p_send, p_recv, a_send, a_recv, down_send, down_recv, loc_sem, down_loc, in_sem, out_sem):
+                  z_send, z_recv, d_send, d_recv, p_send, p_recv, a_send, a_recv, down_send, down_recv, loc_sem, down_loc, in_sem, out_sem, diag_send, diag_recv, diag_loc):
     layers, zn, pool, tok = cfg["layers"], cfg["zn"], cfg["pool"], cfg["tok"]
     qh, kh, ny = cfg["qh"], cfg["kh"], cfg["ny"]
     dm = x_hbm.shape[1]
@@ -84,14 +84,17 @@
         "gu": (wgu, 3, [(wg_hbm, 0), (wu_hbm, wgu.shape[-1] // 2)]),
     }
 
-    def pieces(l, name, zt):
+    direct = {(0, "q"), (0, "kv")} if pool == 4 else set()
+
+    def pieces(l, name, zt, diag=False):
         buf, gi, srcs = groups[name]
+        quart, to = (3 - quarter, subd) if diag else (quarter, sub)
         rows = buf.shape[3]
         out = []
         for src, off in srcs:
             width = src.shape[2] // zn
-            s = src.at[l, pl.ds(pl.multiple_of(quarter * rows, rows), rows), pl.ds(pl.multiple_of(zt * width, 128), width)]
-            d = buf.at[l, z, sub, :, pl.ds(off, width)]
+            s = src.at[l, pl.ds(pl.multiple_of(quart * rows, rows), rows), pl.ds(pl.multiple_of(zt * width, 128), width)]
+            d = buf.at[l, z, to, :, pl.ds(off, width)]
             out.append((s, d))
         return out, gi
 
@@ -99,6 +102,9 @@
         ps, gi = pieces(l, name, z)
         for s, d in ps:
             pltpu.make_async_copy(s, d, loc_sem.at[l, gi]).start()
+        if (l, name) in direct:
+            for s, d in pieces(l, name, z, True)[0]:
+                pltpu.make_async_copy(s, d, diag_loc.at[gi]).start()
 
     def w_send(l, name):
         for r in order:
@@ -106,6 +112,14 @@
             ps, gi = pieces(l, name, zt)
             for s, d in ps:
                 rcopy(s, d, z_send.at[l, gi], z_recv.at[l, gi], peer_id(zt)).start()
+
+    def w_diag(l, name):
+        if (l, name) in direct:
+            for r in order:
+                zt = peer(r)
+                ps, gi = pieces(l, name, zt, True)
+                for s, d in ps:
+                    rcopy(s, d, diag_send.at[gi], diag_recv.at[gi], peer_id(zt)).start()
 
     def w_s1(l, name):
         buf, gi, _ = groups[name]
@@ -123,18 +137,24 @@
             qx, qy = buf.at[l, :, subx], buf.at[l, :, suby]
             hx, hy = buf.at[l, 0:zh, subx], buf.at[l, zh:zn, suby]
             wait_bytes(qx, p_recv.at[l, gi, 0])
-            rcopy(hx, hx, p_send.at[l, gi, 2], p_recv.at[l, gi, 2], ynei).start()
+            if (l, name) not in direct:
+                rcopy(hx, hx, p_send.at[l, gi, 2], p_recv.at[l, gi, 2], ynei).start()
             rcopy(qx, qx, d_send.at[l, gi, 1], d_recv.at[l, gi, 1], sib).start()
             wait_bytes(qy, p_recv.at[l, gi, 1])
-            rcopy(hy, hy, p_send.at[l, gi, 3], p_recv.at[l, gi, 3], xnei).start()
+            if (l, name) not in direct:
+                rcopy(hy, hy, p_send.at[l, gi, 3], p_recv.at[l, gi, 3], xnei).start()
             rcopy(qy, qy, d_send.at[l, gi, 2], d_recv.at[l, gi, 2], sib).start()
 
     def w_s3(l, name):
         if pool == 4:
             buf, gi, _ = groups[name]
             q = buf.at[l, :, subd]
-            wait_bytes(buf.at[l, 0:zh, subd], p_recv.at[l, gi, 2])
-            wait_bytes(buf.at[l, zh:zn, subd], p_recv.at[l, gi, 3])
+            if (l, name) in direct:
+                wait_bytes(buf.at[l, 0:zn - 1, 0], diag_recv.at[gi])
+                wait_bytes(buf.at[l, 0, 0], diag_loc.at[gi])
+            else:
+                wait_bytes(buf.at[l, 0:zh, subd], p_recv.at[l, gi, 2])
+                wait_bytes(buf.at[l, zh:zn, subd], p_recv.at[l, gi, 3])
             rcopy(q, q, d_send.at[l, gi, 3], d_recv.at[l, gi, 3], sib).start()
 
     def w_fin(l, name):
@@ -147,8 +167,10 @@
         wait_bytes(buf.at[l, 0:zn - 1, 0], z_send.at[l, gi])
         for i in range(pool):
             wait_bytes(buf.at[l, :, 0], d_send.at[l, gi, i])
+        if (l, name) in direct:
+            wait_bytes(buf.at[l, 0:zn - 1, 0], diag_send.at[gi])
         if pool == 4:
-            for i in range(4):
+            for i in range(2 if (l, name) in direct else 4):
                 wait_bytes(buf.at[l, :, 0] if i < 2 else buf.at[l, 0:zh, 0], p_send.at[l, gi, i])
 
     def spread(src_of, dst, l, ph):
@@ -160,8 +182,8 @@
         wait_bytes(buf.at[l, 0:zn - 1], a_recv.at[l, ph])
 
     plan = {
-        (0, "entry"): [(w_send, 0, "q"), (w_send, 0, "kv")],
-        (0, "x_in"): [(w_s1, 0, "q"), (w_send, 0, "o"), (w_s1, 0, "kv"), (w_send, 0, "gu"), (w_s2, 0, "q"), (w_s2, 0, "kv"), (w_s3, 0, "q"), (w_s3, 0, "kv")],
+        (0, "entry"): [(w_send, 0, "q"), (w_send, 0, "kv"), (w_diag, 0, "q"), (w_diag, 0, "kv")],
+        (0, "x_wait"): [(w_s1, 0, "q"), (w_s1, 0, "kv"), (w_send, 0, "o"), (w_send, 0, "gu"), (w_s2, 0, "q"), (w_s3, 0, "q"), (w_s2, 0, "kv"), (w_s3, 0, "kv")],
         (0, "qkv_sent"): [(w_send, 1, "q"), (w_send, 1, "kv"), (w_send, 1, "o"), (w_s1, 0, "o")],
         (0, "qkv_in"): [(w_s1, 0, "gu"), (w_s2, 0, "o")],
         (0, "o_sent"): [(w_s3, 0, "o"), (w_s2, 0, "gu"), (w_s1, 1, "q"), (w_s1, 1, "kv")],
@@ -266,11 +288,13 @@
 
     for l in range(layers):
         last = l == layers - 1
+        background(l, "x_wait")
         arrived(xg, l, 0)
         h = (rms(gathered_x(l), dm) * an_ref[l:l + 1, :].astype(F32)).astype(BF16)
         background(l, "x_in")
+        w_fin(l, "q")
+        w_fin(l, "kv")
         for name, lo in (("q", 0), ("kv", wq.shape[-1])):
-            w_fin(l, name)
             buf = groups[name][0]
             cols = buf.shape[-1]
             r = jnp.dot(h, buf[l].reshape(dm, cols), preferred_element_type=F32)
@@ -419,7 +443,7 @@
             pltpu.VMEM((layers, tok * kh, hd), BF16),
             pltpu.VMEM((layers, tok * kh, hd), BF16),
             dma((layers, 4)), dma((layers, 4)), dma((layers, 4, pool)), dma((layers, 4, pool)), dma((layers, 4, 4)), dma((layers, 4, 4)),
-            dma((layers, 5)), dma((layers, 5)), dma((layers,)), dma((layers,)), dma((layers, 4)), dma((layers, 3)), dma((6,)), dma((1 + 2 * layers,)),
+            dma((layers, 5)), dma((layers, 5)), dma((layers,)), dma((layers,)), dma((layers, 4)), dma((layers, 3)), dma((6,)), dma((1 + 2 * layers,)), dma((2,)), dma((2,)), dma((2,)),
         ]
         res = pl.pallas_call(
             functools.partial(decode_kernel, cfg),

time: 95.5 us -> 92.5 us (0.969)
  Pallas kernels: 94.3 us -> 91.7 us
    pallas_call x1, Pallas kernels: 89.8 us -> 87.2 us  [device_fn(): pl.pallas_call(functools.partial(decode_kernel, cfg), name='decode', out_...]
where the time goes in v5:
time: 92.5 us; the launch traced here: 92.4 us
  Pallas kernels  91.7 us (99%)
    pallas_call x1, Pallas kernels, device_fn(): pl.pallas_call(functools.partial(decode_kernel, cfg), name='decode', out_...  87.2 us
    pallas_call x1, Pallas kernels, device_fn(): pl.pallas_call(functools.partial(place_rows, layers, tok, kh), name='plac...  4.49 us

profile of v5, /device:TPU:21, one launch (start us, length us, event | category | flops | bytes accessed | tf_op | source)
XLA Modules:
  0.0 92.4 jit_solution(1351291263998621653)
XLA Ops:
  0.6 0.0 copy-start
  0.6 0.0 copy-start.1
  0.7 0.0 copy-start.2
  0.7 87.2 %decode.1.res_hbm = bf16[4096,64,128]{2,1,0:T(8,128)(2,1)} custom-call(s32[8]{0:T(128)} %pos_hbm.3, bf16[8,1024]{1,0:T(8,128)(2,1)} %x_hbm.1, bf16[2,1024]{1,0:T(2,128)(2,1)} %an_hbm.1, bf16[2,128]{1,0:T(2,128)(2,1)} %qn_hbm.1, bf16[2,128]{1,0:T(2,128)(2,1)} %kn_hbm.1, bf16[2,1024]{1,0:T(2,128)(2,1)} %mn_hbm.1, bf16[2,64,2048]{2,1,0:T(8,128)(2,1)} %wq_hbm.1, ...), custom_call_target="tpu_custom_call" | custom-call | tf_op jit(solution)/shard_map/decode/pallas_call | solution.py:448
  87.8 0.0 copy-done
  87.8 0.0 copy-done.1
  87.9 0.0 copy-done.2
  87.9 4.5 %place.1 = (bf16[8,1024]{1,0:T(8,128)(2,1)}, bf16[2,8,1024,128]{3,2,1,0:T(8,128)(2,1)}, bf16[2,8,1024,128]{3,2,1,0:T(8,128)(2,1)}) custom-call(s32[8]{0:T(128)S(1)} %copy-done.2, bf16[4096,64,128]{2,1,0:T(8,128)(2,1)} %decode.1.res_hbm, bf16[2,8,1024,128]{3,2,1,0:T(8,128)(2,1)S(1)} %bitcast.5, bf16[2,8,1024,128]{3,2,1,0:T(8,128)(2,1)S(1)} %bitcast.7), custom_call_target="tpu_custom_call" | custom-call | tf_op jit(solution)/shard_map/place/pallas_call | solution.py:459
Async XLA Ops:
  0.6 87.2 %copy-start = (bf16[2,8,128,8,128]{4,3,2,1,0:T(8,128)(2,1)S(1)}, bf16[2,8,128,8,128]{4,3,2,1,0:T(8,128)(2,1)}, u32[]{:S(2)}) copy-start(bf16[2,8,128,8,128]{4,3,2,1,0:T(8,128)(2,1)} %param.17) | copy-start | bytes 12582916
  0.6 87.2 %copy-start.1 = (bf16[2,8,128,8,128]{4,3,2,1,0:T(8,128)(2,1)S(1)}, bf16[2,8,128,8,128]{4,3,2,1,0:T(8,128)(2,1)}, u32[]{:S(2)}) copy-start(bf16[2,8,128,8,128]{4,3,2,1,0:T(8,128)(2,1)} %param.18) | copy-start | bytes 12582916
  0.7 87.2 %copy-start.2 = (s32[8]{0:T(128)S(1)}, s32[8]{0:T(128)}, u32[]{:S(2)}) copy-start(s32[8]{0:T(128)} %pos_hbm.3) | copy-start | bytes 100

commit v6 on v5

--- a/solution.py
+++ b/solution.py
@@ -27,8 +27,8 @@
 
 def decode_kernel(cfg, pos_hbm, x_hbm, an_hbm, qn_hbm, kn_hbm, mn_hbm, wq_hbm, wk_hbm, wv_hbm, wo_hbm, wg_hbm, wu_hbm, wd_hbm, kc_hbm, vc_hbm,
                   res_hbm,
-                  wq, wkv, wo, wgu, wd, kc, vc, xg, qkvs, qkvi, og, x1g, pbuf, ybuf, x1f, qs, ks, vs, os_, kro, vro, cs, sn, pos_ref, an_ref, qn_ref, kn_ref, mn_ref, y_ref, krow_ref, vrow_ref,
-                  z_send, z_recv, d_send, d_recv, p_send, p_recv, a_send, a_recv, down_send, down_recv, loc_sem, down_loc, in_sem, out_sem, diag_send, diag_recv, diag_loc):
+                  wq, wkv, wo, wof, wgu, wd, kc, vc, xg, qkvs, qkvi, og, x1g, x1r, pbuf, ybuf, x1f, qs, ks, vs, os_, kro, vro, cs, sn, pos_ref, an_ref, qn_ref, kn_ref, mn_ref, y_ref, krow_ref, vrow_ref,
+                  z_send, z_recv, d_send, d_recv, p_send, p_recv, a_send, a_recv, down_send, down_recv, loc_sem, down_loc, in_sem, out_sem, diag_send, diag_recv, diag_loc, ring_send, ring_recv, of_send, of_recv, of_sib):
     layers, zn, pool, tok = cfg["layers"], cfg["zn"], cfg["pool"], cfg["tok"]
     qh, kh, ny = cfg["qh"], cfg["kh"], cfg["ny"]
     dm = x_hbm.shape[1]
@@ -84,6 +84,80 @@
         "gu": (wgu, 3, [(wg_hbm, 0), (wu_hbm, wgu.shape[-1] // 2)]),
     }
 
+    full_o = {layers - 1} if pool == 4 else set()
+
+    def skip(l, name):
+        return l in full_o and name == "o"
+
+    half_rows = wof.shape[3] // 2
+    right, left = peer_id(peer(1)), peer_id(peer(zn - 1))
+
+    def r_block(d, which=None):
+        return wof.at[0, lax.rem(z + zn + d, zn), sub if which is None else which]
+
+    def signed(d):
+        return (d,) if d in (0, zh) else (d, -d)
+
+    def of_own(l, d):
+        if d == 0:
+            wait_bytes(r_block(0), loc_sem.at[l, 2])
+        elif d == zh:
+            ring(l, zh)
+        for b in signed(d):
+            q = r_block(b)
+            rcopy(q, q, of_send.at[0], of_recv.at[0, d], xnei).start()
+            rcopy(q, q, of_send.at[1], of_recv.at[1, d], ynei).start()
+            rcopy(q, q, of_send.at[2], of_sib.at[0], sib).start()
+
+    def of_relay(l, d):
+        for i, which, to in ((0, subx, ynei), (1, suby, xnei)):
+            wait_bytes(wof.at[0, 0:len(signed(d)), 0], of_recv.at[i, d])
+            for b in signed(d):
+                q = r_block(b, which)
+                if (b > 0 if i == 0 else b <= 0):
+                    rcopy(q, q, of_send.at[3], of_recv.at[2, d], to).start()
+                rcopy(q, q, of_send.at[4 + i], of_sib.at[1 + i], sib).start()
+
+    def of_last(l, d):
+        wait_bytes(wof.at[0, 0:len(signed(d)), 0], of_recv.at[2, d])
+        for b in signed(d):
+            q = r_block(b, subd)
+            rcopy(q, q, of_send.at[6], of_sib.at[3], sib).start()
+
+    def of_fin():
+        for i in range(4):
+            wait_bytes(wof.at[0, :, 0], of_sib.at[i])
+
+    def of_drain():
+        for i in range(7):
+            wait_bytes(wof.at[0, :, 0], of_send.at[i])
+        for i in range(2):
+            for step in range(zh):
+                wait_bytes(r_block(0) if step < zh - 1 else r_halves(0)[0], ring_send.at[i, step])
+
+    def r_halves(d):
+        blk = lax.rem(z + zn + d, zn)
+        return wof.at[0, blk, sub, 0:half_rows], wof.at[0, blk, sub, half_rows:2 * half_rows]
+
+    def ring(l, step):
+        if step == 0:
+            src = wo_hbm.at[l, pl.ds(pl.multiple_of(quarter * 2 * half_rows, 2 * half_rows), 2 * half_rows)]
+            pltpu.make_async_copy(src, r_block(0), loc_sem.at[l, 2]).start()
+            rcopy(src, r_block(0), ring_send.at[0, 0], ring_recv.at[0, 0], right).start()
+            rcopy(src, r_block(0), ring_send.at[1, 0], ring_recv.at[1, 0], left).start()
+        elif step < zh - 1:
+            for i, d, to in ((0, -step, right), (1, step, left)):
+                wait_bytes(r_block(d), ring_recv.at[i, step - 1])
+                rcopy(r_block(d), r_block(d), ring_send.at[i, step], ring_recv.at[i, step], to).start()
+        elif step == zh - 1:
+            for i, d, to in ((0, -step, right), (1, step, left)):
+                wait_bytes(r_block(d), ring_recv.at[i, step - 1])
+                h = r_halves(d)[i]
+                rcopy(h, h, ring_send.at[i, step], ring_recv.at[i, step], to).start()
+        else:
+            for i in range(2):
+                wait_bytes(r_halves(zh)[i], ring_recv.at[i, zh - 1])
+
     direct = {(0, "q"), (0, "kv")} if pool == 4 else set()
 
     def pieces(l, name, zt, diag=False):
@@ -123,9 +197,10 @@
 
     def w_s1(l, name):
         buf, gi, _ = groups[name]
-        wait_bytes(buf.at[l, 0:zn - 1, 0], z_recv.at[l, gi])
-        wait_bytes(buf.at[l, 0, 0], loc_sem.at[l, gi])
-        q = buf.at[l, :, sub]
+        buf = buf.at[l]
+        wait_bytes(buf.at[0:zn - 1, 0], z_recv.at[l, gi])
+        wait_bytes(buf.at[0, 0], loc_sem.at[l, gi])
+        q = buf.at[:, sub]
         if pool == 4:
             rcopy(q, q, p_send.at[l, gi, 0], p_recv.at[l, gi, 0], xnei).start()
             rcopy(q, q, p_send.at[l, gi, 1], p_recv.at[l, gi, 1], ynei).start()
@@ -134,8 +209,9 @@
     def w_s2(l, name):
         if pool == 4:
             buf, gi, _ = groups[name]
-            qx, qy = buf.at[l, :, subx], buf.at[l, :, suby]
-            hx, hy = buf.at[l, 0:zh, subx], buf.at[l, zh:zn, suby]
+            buf = buf.at[l]
+            qx, qy = buf.at[:, subx], buf.at[:, suby]
+            hx, hy = buf.at[0:zh, subx], buf.at[zh:zn, suby]
             wait_bytes(qx, p_recv.at[l, gi, 0])
             if (l, name) not in direct:
                 rcopy(hx, hx, p_send.at[l, gi, 2], p_recv.at[l, gi, 2], ynei).start()
@@ -148,30 +224,33 @@
     def w_s3(l, name):
         if pool == 4:
             buf, gi, _ = groups[name]
-            q = buf.at[l, :, subd]
+            buf = buf.at[l]
+            q = buf.at[:, subd]
             if (l, name) in direct:
-                wait_bytes(buf.at[l, 0:zn - 1, 0], diag_recv.at[gi])
-                wait_bytes(buf.at[l, 0, 0], diag_loc.at[gi])
+                wait_bytes(buf.at[0:zn - 1, 0], diag_recv.at[gi])
+                wait_bytes(buf.at[0, 0], diag_loc.at[gi])
             else:
-                wait_bytes(buf.at[l, 0:zh, subd], p_recv.at[l, gi, 2])
-                wait_bytes(buf.at[l, zh:zn, subd], p_recv.at[l, gi, 3])
+                wait_bytes(buf.at[0:zh, subd], p_recv.at[l, gi, 2])
+                wait_bytes(buf.at[zh:zn, subd], p_recv.at[l, gi, 3])
             rcopy(q, q, d_send.at[l, gi, 3], d_recv.at[l, gi, 3], sib).start()
 
     def w_fin(l, name):
         buf, gi, _ = groups[name]
+        buf = buf.at[l]
         for i in range(pool):
-            wait_bytes(buf.at[l, :, 0], d_recv.at[l, gi, i])
+            wait_bytes(buf.at[:, 0], d_recv.at[l, gi, i])
 
     def w_drain(l, name):
         buf, gi, _ = groups[name]
-        wait_bytes(buf.at[l, 0:zn - 1, 0], z_send.at[l, gi])
+        buf = buf.at[l]
+        wait_bytes(buf.at[0:zn - 1, 0], z_send.at[l, gi])
         for i in range(pool):
-            wait_bytes(buf.at[l, :, 0], d_send.at[l, gi, i])
+            wait_bytes(buf.at[:, 0], d_send.at[l, gi, i])
         if (l, name) in direct:
-            wait_bytes(buf.at[l, 0:zn - 1, 0], diag_send.at[gi])
+            wait_bytes(buf.at[0:zn - 1, 0], diag_send.at[gi])
         if pool == 4:
             for i in range(2 if (l, name) in direct else 4):
-                wait_bytes(buf.at[l, :, 0] if i < 2 else buf.at[l, 0:zh, 0], p_send.at[l, gi, i])
+                wait_bytes(buf.at[:, 0] if i < 2 else buf.at[0:zh, 0], p_send.at[l, gi, i])
 
     def spread(src_of, dst, l, ph):
         for r in order:
@@ -179,20 +258,32 @@
             rcopy(src_of(zt), dst, a_send.at[l, ph], a_recv.at[l, ph], peer_id(zt)).start()
 
     def arrived(buf, l, ph):
-        wait_bytes(buf.at[l, 0:zn - 1], a_recv.at[l, ph])
-
+        if l is None:
+            wait_bytes(buf.at[0:zn - 1], a_recv.at[layers - 1, ph])
+        else:
+            wait_bytes(buf.at[l, 0:zn - 1], a_recv.at[l, ph])
+
+    end = layers - 1
     plan = {
         (0, "entry"): [(w_send, 0, "q"), (w_send, 0, "kv"), (w_diag, 0, "q"), (w_diag, 0, "kv")],
-        (0, "x_wait"): [(w_s1, 0, "q"), (w_s1, 0, "kv"), (w_send, 0, "o"), (w_send, 0, "gu"), (w_s2, 0, "q"), (w_s3, 0, "q"), (w_s2, 0, "kv"), (w_s3, 0, "kv")],
-        (0, "qkv_sent"): [(w_send, 1, "q"), (w_send, 1, "kv"), (w_send, 1, "o"), (w_s1, 0, "o")],
-        (0, "qkv_in"): [(w_s1, 0, "gu"), (w_s2, 0, "o")],
-        (0, "o_sent"): [(w_s3, 0, "o"), (w_s2, 0, "gu"), (w_s1, 1, "q"), (w_s1, 1, "kv")],
-        (0, "x1_sent"): [(w_send, 1, "gu"), (w_s3, 0, "gu")],
-        (0, "x1_in"): [(w_s2, 1, "q"), (w_s2, 1, "kv"), (w_s1, 1, "o")],
-        (0, "y_sent"): [(w_s3, 1, "q"), (w_s3, 1, "kv"), (w_s2, 1, "o")],
-        (1, "x_sent"): [(w_s3, 1, "o"), (w_s1, 1, "gu")],
-        (1, "qkv_sent"): [(w_s2, 1, "gu")],
-        (1, "o_sent"): [(w_s3, 1, "gu")],
+        (0, "x_wait"): [(ring, end, 0), (w_s1, 0, "q"), (w_s1, 0, "kv"), (w_send, 0, "o"), (w_send, 0, "gu"), (w_s2, 0, "q"), (w_s3, 0, "q"), (w_s2, 0, "kv"), (w_s3, 0, "kv")],
+        (0, "qkv_sent"): [(ring, end, 1), (w_send, 1, "q"), (w_send, 1, "kv"), (w_s1, 0, "o"), (of_own, end, 0), (of_own, end, 1)],
+        (0, "qkv_in"): [(w_s2, 0, "o"), (w_s1, 0, "gu")],
+        (0, "o_sent"): [(ring, end, 2), (w_s3, 0, "o"), (w_s2, 0, "gu"), (w_s1, 1, "q"), (w_s1, 1, "kv"), (of_relay, end, 0), (of_own, end, 2)],
+        (0, "x1_sent"): [(ring, end, 3), (w_send, 1, "gu"), (w_s3, 0, "gu"), (of_own, end, 3)],
+        (0, "x1_in"): [(w_s2, 1, "q"), (w_s2, 1, "kv")],
+        (0, "y_sent"): [(of_relay, end, 1), (of_relay, end, 2), (w_s1, 1, "gu"), (w_s3, 1, "q"), (w_s3, 1, "kv"), (of_own, end, zh)],
+        (1, "x_sent"): [(of_relay, end, 3), (of_relay, end, zh), (of_last, end, 0), (of_last, end, 1), (of_last, end, 2)],
+        (1, "qkv_sent"): [(w_s2, 1, "gu"), (of_last, end, 3), (of_last, end, zh)],
+        (1, "x1_sent"): [(w_s3, 1, "gu")],
+    } if full_o else {
+        (0, "entry"): [(w_send, 0, "q"), (w_send, 0, "kv"), (w_send, 0, "o"), (w_send, 0, "gu")],
+        (0, "x_wait"): [(w_s1, 0, "q"), (w_s1, 0, "kv")],
+        (0, "qkv_sent"): [(w_s1, 0, "o"), (w_send, 1, "q"), (w_send, 1, "kv"), (w_send, 1, "o")],
+        (0, "o_sent"): [(w_s1, 0, "gu")],
+        (0, "x1_sent"): [(w_send, 1, "gu"), (w_s1, 1, "q"), (w_s1, 1, "kv")],
+        (0, "y_sent"): [(w_s1, 1, "o")],
+        (1, "qkv_sent"): [(w_s1, 1, "gu")],
     }
 
     def background(l, point):
@@ -205,8 +296,9 @@
         cp.start()
     for l in range(layers):
         pltpu.make_async_copy(wd_hbm.at[l], wd.at[l, c], down_loc.at[l, 0]).start()
-        for name in groups:
-            w_local(l, name)
+        for name in ("q", "kv", "o", "gu"):
+            if not skip(l, name):
+                w_local(l, name)
         pltpu.make_async_copy(kc_hbm.at[l], kc.at[l], down_loc.at[l, 1]).start()
         pltpu.make_async_copy(vc_hbm.at[l], vc.at[l], down_loc.at[l, 2]).start()
 
@@ -286,6 +378,36 @@
         for h in range(qh):
             og[l, z, :, h * HEAD_DIM:(h + 1) * HEAD_DIM] = os_[pl.ds(h, tok, stride=qh), :].astype(BF16)
 
+    def own_rows(l):
+        of_fin()
+        r = jnp.dot(og[l, z], wof[0].reshape(og.shape[-1], dm), preferred_element_type=F32)
+        x1r[z] = (xg[l, z].astype(F32) + r).astype(BF16)
+        spread(lambda zt: x1r.at[z], x1r.at[z], l, 3)
+        background(l, "x1_sent")
+        wait_bytes(wd.at[l, 0], down_loc.at[l, 0])
+        wait_bytes(wd.at[l, 0], down_recv.at[l])
+        w_fin(l, "gu")
+        arrived(x1r, None, 3)
+        return x1r[...].astype(F32).reshape(nq, dm)
+
+    def gathered_rows(l):
+        spread(lambda zt: og.at[l, z], og.at[l, z], l, 2)
+        background(l, "o_sent")
+        w_fin(l, "o")
+        arrived(og, l, 2)
+        o_all = og[l].astype(F32).reshape(nq, og.shape[-1]).astype(BF16)
+        r = jnp.dot(o_all, wo[l].reshape(og.shape[-1], ctile), preferred_element_type=F32)
+        xc = xg[l, :, :, pl.ds(pl.multiple_of(z * ctile, ctile), ctile)].astype(F32).reshape(nq, ctile)
+        x1g[l, z] = (xc + r).astype(BF16)
+        spread(lambda zt: x1g.at[l, z], x1g.at[l, z], l, 3)
+        background(l, "x1_sent")
+        wait_bytes(wd.at[l, 0], down_loc.at[l, 0])
+        wait_bytes(wd.at[l, 0], down_recv.at[l])
+        w_fin(l, "gu")
+        arrived(x1g, l, 3)
+        background(l, "x1_in")
+        return jnp.concatenate([x1g[l, zz].astype(F32) for zz in range(zn)], axis=-1)
+
     for l in range(layers):
         last = l == layers - 1
         background(l, "x_wait")
@@ -309,22 +431,7 @@
         arrived(qkvi, l, 1)
         background(l, "qkv_in")
         attention(l)
-        spread(lambda zt: og.at[l, z], og.at[l, z], l, 2)
-        background(l, "o_sent")
-        w_fin(l, "o")
-        arrived(og, l, 2)
-        o_all = og[l].astype(F32).reshape(nq, og.shape[-1]).astype(BF16)
-        r = jnp.dot(o_all, wo[l].reshape(og.shape[-1], ctile), preferred_element_type=F32)
-        xc = xg[l, :, :, pl.ds(pl.multiple_of(z * ctile, ctile), ctile)].astype(F32).reshape(nq, ctile)
-        x1g[l, z] = (xc + r).astype(BF16)
-        spread(lambda zt: x1g.at[l, z], x1g.at[l, z], l, 3)
-        background(l, "x1_sent")
-        wait_bytes(wd.at[l, 0], down_loc.at[l, 0])
-        wait_bytes(wd.at[l, 0], down_recv.at[l])
-        w_fin(l, "gu")
-        arrived(x1g, l, 3)
-        background(l, "x1_in")
-        x1 = jnp.concatenate([x1g[l, zz].astype(F32) for zz in range(zn)], axis=-1)
+        x1 = own_rows(l) if l in full_o else gathered_rows(l)
         x1f[...] = x1
         h2 = (rms(x1, dm) * mn_ref[l:l + 1, :].astype(F32)).astype(BF16)
         gu = jnp.dot(h2, wgu[l].reshape(dm, wgu.shape[-1]), preferred_element_type=F32)
@@ -352,10 +459,14 @@
 
     for l in range(layers):
         for name in groups:
-            w_drain(l, name)
+            if not skip(l, name):
+                w_drain(l, name)
+        if l in full_o:
+            of_drain()
         wait_bytes(wd.at[l, 0], down_send.at[l])
         for ph, buf in enumerate((xg, qkvi, og, x1g, ybuf)):
-            wait_bytes(buf.at[l, 0:zn - 1], a_send.at[l, ph])
+            if ph != 2 or l not in full_o:
+                wait_bytes(buf.at[l, 0:zn - 1], a_send.at[l, ph])
     for cp in outs:
         cp.wait()
 
@@ -414,6 +525,7 @@
             pltpu.VMEM((layers, zn, nq, w_q.shape[1] // pool, qw // zn), BF16),
             pltpu.VMEM((layers, zn, nq, w_k.shape[1] // pool, 2 * kw // zn), BF16),
             pltpu.VMEM((layers, zn, nq, w_o.shape[1] // pool, dm // zn), BF16),
+            pltpu.VMEM((1, zn, nq, w_o.shape[1] // pool, dm), BF16),
             pltpu.VMEM((layers, zn, nq, w_gate.shape[1] // pool, 2 * ff // zn), BF16),
             pltpu.VMEM((layers, 2, w_down.shape[1], dm), BF16),
             pltpu.VMEM(flat, BF16),
@@ -423,6 +535,7 @@
             pltpu.VMEM((layers, zn, tok, qkvc), BF16),
             pltpu.VMEM((layers, zn, tok, qw), BF16),
             pltpu.VMEM((layers, zn, zn * tok, dm // zn), BF16),
+            pltpu.VMEM((zn, tok, dm), BF16),
             pltpu.VMEM((layers, zn, tok, dm), F32),
             pltpu.VMEM((layers, zn, tok, dm), F32),
             pltpu.VMEM((zn * tok, dm), F32),
@@ -443,7 +556,7 @@
             pltpu.VMEM((layers, tok * kh, hd), BF16),
             pltpu.VMEM((layers, tok * kh, hd), BF16),
             dma((layers, 4)), dma((layers, 4)), dma((layers, 4, pool)), dma((layers, 4, pool)), dma((layers, 4, 4)), dma((layers, 4, 4)),
-            dma((layers, 5)), dma((layers, 5)), dma((layers,)), dma((layers,)), dma((layers, 4)), dma((layers, 3)), dma((6,)), dma((1 + 2 * layers,)), dma((2,)), dma((2,)), dma((2,)),
+            dma((layers, 5)), dma((layers, 5)), dma((layers,)), dma((layers,)), dma((layers, 4)), dma((layers, 3)), dma((6,)), dma((1 + 2 * layers,)), dma((2,)), dma((2,)), dma((2,)), dma((2, zn // 2)), dma((2, zn // 2)), dma((7,)), dma((3, zn // 2 + 1)), dma((4,)),
         ]
         res = pl.pallas_call(
             functools.partial(decode_kernel, cfg),

time: 92.5 us -> 85.9 us (0.929)
  the two profiles are of different devices: /device:TPU:21 before, /device:TPU:30 now
where the time goes in v6:
time: 85.9 us; the launch traced here: 85.8 us
  Pallas kernels  85.1 us (99%)
    pallas_call x1, Pallas kernels, device_fn(): pl.pallas_call(functools.partial(decode_kernel, cfg), name='decode', out_...  80.6 us
    pallas_call x1, Pallas kernels, device_fn(): pl.pallas_call(functools.partial(place_rows, layers, tok, kh), name='plac...  4.49 us

profile of v6, /device:TPU:30, one launch (start us, length us, event | category | flops | bytes accessed | tf_op | source)
XLA Modules:
  0.0 85.8 jit_solution(10543702879744583951)
XLA Ops:
  0.6 0.0 copy-start
  0.6 0.0 copy-start.1
  0.7 0.0 copy-start.2
  0.7 80.6 %decode.1.res_hbm = bf16[4096,64,128]{2,1,0:T(8,128)(2,1)} custom-call(s32[8]{0:T(128)} %pos_hbm.3, bf16[8,1024]{1,0:T(8,128)(2,1)} %x_hbm.1, bf16[2,1024]{1,0:T(2,128)(2,1)} %an_hbm.1, bf16[2,128]{1,0:T(2,128)(2,1)} %qn_hbm.1, bf16[2,128]{1,0:T(2,128)(2,1)} %kn_hbm.1, bf16[2,1024]{1,0:T(2,128)(2,1)} %mn_hbm.1, bf16[2,64,2048]{2,1,0:T(8,128)(2,1)} %wq_hbm.1, ...), custom_call_target="tpu_custom_call" | custom-call | tf_op jit(solution)/shard_map/decode/pallas_call | solution.py:561
  81.3 0.0 copy-done
  81.3 0.0 copy-done.1
  81.3 0.0 copy-done.2
  81.3 4.5 %place.1 = (bf16[8,1024]{1,0:T(8,128)(2,1)}, bf16[2,8,1024,128]{3,2,1,0:T(8,128)(2,1)}, bf16[2,8,1024,128]{3,2,1,0:T(8,128)(2,1)}) custom-call(s32[8]{0:T(128)S(1)} %copy-done.2, bf16[4096,64,128]{2,1,0:T(8,128)(2,1)} %decode.1.res_hbm, bf16[2,8,1024,128]{3,2,1,0:T(8,128)(2,1)S(1)} %bitcast.5, bf16[2,8,1024,128]{3,2,1,0:T(8,128)(2,1)S(1)} %bitcast.7), custom_call_target="tpu_custom_call" | custom-call | tf_op jit(solution)/shard_map/place/pallas_call | solution.py:572
Async XLA Ops:
  0.6 80.6 %copy-start = (bf16[2,8,128,8,128]{4,3,2,1,0:T(8,128)(2,1)S(1)}, bf16[2,8,128,8,128]{4,3,2,1,0:T(8,128)(2,1)}, u32[]{:S(2)}) copy-start(bf16[2,8,128,8,128]{4,3,2,1,0:T(8,128)(2,1)} %param.17) | copy-start | bytes 12582916
  0.6 80.6 %copy-start.1 = (bf16[2,8,128,8,128]{4,3,2,1,0:T(8,128)(2,1)S(1)}, bf16[2,8,128,8,128]{4,3,2,1,0:T(8,128)(2,1)}, u32[]{:S(2)}) copy-start(bf16[2,8,128,8,128]{4,3,2,1,0:T(8,128)(2,1)} %param.18) | copy-start | bytes 12582916
  0.7 80.6 %copy-start.2 = (s32[8]{0:T(128)S(1)}, s32[8]{0:T(128)}, u32[]{:S(2)}) copy-start(s32[8]{0:T(128)} %pos_hbm.3) | copy-start | bytes 100

commit v7 on v6

--- a/solution.py
+++ b/solution.py
@@ -27,7 +27,7 @@
 
 def decode_kernel(cfg, pos_hbm, x_hbm, an_hbm, qn_hbm, kn_hbm, mn_hbm, wq_hbm, wk_hbm, wv_hbm, wo_hbm, wg_hbm, wu_hbm, wd_hbm, kc_hbm, vc_hbm,
                   res_hbm,
-                  wq, wkv, wo, wof, wgu, wd, kc, vc, xg, qkvs, qkvi, og, x1g, x1r, pbuf, ybuf, x1f, qs, ks, vs, os_, kro, vro, cs, sn, pos_ref, an_ref, qn_ref, kn_ref, mn_ref, y_ref, krow_ref, vrow_ref,
+                  wq, wkv, wo, wof, wg, wu, wd, kc, vc, xg, qkvs, qkvi, og, x1g, x1r, pbuf, ybuf, x1f, qs, ks, vs, os_, kro, vro, cs, sn, pos_ref, an_ref, qn_ref, kn_ref, mn_ref, y_ref, krow_ref, vrow_ref,
                   z_send, z_recv, d_send, d_recv, p_send, p_recv, a_send, a_recv, down_send, down_recv, loc_sem, down_loc, in_sem, out_sem, diag_send, diag_recv, diag_loc, ring_send, ring_recv, of_send, of_recv, of_sib):
     layers, zn, pool, tok = cfg["layers"], cfg["zn"], cfg["pool"], cfg["tok"]
     qh, kh, ny = cfg["qh"], cfg["kh"], cfg["ny"]
@@ -81,7 +81,8 @@
         "q": (wq, 0, [(wq_hbm, 0)]),
         "kv": (wkv, 1, [(wk_hbm, 0), (wv_hbm, wkv.shape[-1] // 2)]),
         "o": (wo, 2, [(wo_hbm, 0)]),
-        "gu": (wgu, 3, [(wg_hbm, 0), (wu_hbm, wgu.shape[-1] // 2)]),
+        "g": (wg, 3, [(wg_hbm, 0)]),
+        "u": (wu, 4, [(wu_hbm, 0)]),
     }
 
     full_o = {layers - 1} if pool == 4 else set()
@@ -105,9 +106,9 @@
             ring(l, zh)
         for b in signed(d):
             q = r_block(b)
-            rcopy(q, q, of_send.at[0], of_recv.at[0, d], xnei).start()
-            rcopy(q, q, of_send.at[1], of_recv.at[1, d], ynei).start()
-            rcopy(q, q, of_send.at[2], of_sib.at[0], sib).start()
+            rcopy(q, q, of_send, of_recv.at[0, d], xnei).start()
+            rcopy(q, q, of_send, of_recv.at[1, d], ynei).start()
+            rcopy(q, q, of_send, of_sib, sib).start()
 
     def of_relay(l, d):
         for i, which, to in ((0, subx, ynei), (1, suby, xnei)):
@@ -115,25 +116,21 @@
             for b in signed(d):
                 q = r_block(b, which)
                 if (b > 0 if i == 0 else b <= 0):
-                    rcopy(q, q, of_send.at[3], of_recv.at[2, d], to).start()
-                rcopy(q, q, of_send.at[4 + i], of_sib.at[1 + i], sib).start()
+                    rcopy(q, q, of_send, of_recv.at[2, d], to).start()
+                rcopy(q, q, of_send, of_sib, sib).start()
 
     def of_last(l, d):
         wait_bytes(wof.at[0, 0:len(signed(d)), 0], of_recv.at[2, d])
         for b in signed(d):
             q = r_block(b, subd)
-            rcopy(q, q, of_send.at[6], of_sib.at[3], sib).start()
+            rcopy(q, q, of_send, of_sib, sib).start()
 
     def of_fin():
-        for i in range(4):
-            wait_bytes(wof.at[0, :, 0], of_sib.at[i])
+        wait_bytes(wof.at[0, :, 0:4], of_sib)
 
     def of_drain():
-        for i in range(7):
-            wait_bytes(wof.at[0, :, 0], of_send.at[i])
-        for i in range(2):
-            for step in range(zh):
-                wait_bytes(r_block(0) if step < zh - 1 else r_halves(0)[0], ring_send.at[i, step])
+        wait_bytes(wof.at[0, :, 0:7], of_send)
+        wait_bytes(wof.at[0, 0:zn - 1, 0], ring_send)
 
     def r_halves(d):
         blk = lax.rem(z + zn + d, zn)
@@ -143,17 +140,17 @@
         if step == 0:
             src = wo_hbm.at[l, pl.ds(pl.multiple_of(quarter * 2 * half_rows, 2 * half_rows), 2 * half_rows)]
             pltpu.make_async_copy(src, r_block(0), loc_sem.at[l, 2]).start()
-            rcopy(src, r_block(0), ring_send.at[0, 0], ring_recv.at[0, 0], right).start()
-            rcopy(src, r_block(0), ring_send.at[1, 0], ring_recv.at[1, 0], left).start()
+            rcopy(src, r_block(0), ring_send, ring_recv.at[0, 0], right).start()
+            rcopy(src, r_block(0), ring_send, ring_recv.at[1, 0], left).start()
         elif step < zh - 1:
             for i, d, to in ((0, -step, right), (1, step, left)):
                 wait_bytes(r_block(d), ring_recv.at[i, step - 1])
-                rcopy(r_block(d), r_block(d), ring_send.at[i, step], ring_recv.at[i, step], to).start()
+                rcopy(r_block(d), r_block(d), ring_send, ring_recv.at[i, step], to).start()
         elif step == zh - 1:
             for i, d, to in ((0, -step, right), (1, step, left)):
                 wait_bytes(r_block(d), ring_recv.at[i, step - 1])
                 h = r_halves(d)[i]
-                rcopy(h, h, ring_send.at[i, step], ring_recv.at[i, step], to).start()
+                rcopy(h, h, ring_send, ring_recv.at[i, step], to).start()
         else:
             for i in range(2):
                 wait_bytes(r_halves(zh)[i], ring_recv.at[i, zh - 1])
@@ -178,7 +175,7 @@
             pltpu.make_async_copy(s, d, loc_sem.at[l, gi]).start()
         if (l, name) in direct:
             for s, d in pieces(l, name, z, True)[0]:
-                pltpu.make_async_copy(s, d, diag_loc.at[gi]).start()
+                pltpu.make_async_copy(s, d, diag_loc.at[l, gi]).start()
 
     def w_send(l, name):
         for r in order:
@@ -193,7 +190,7 @@
                 zt = peer(r)
                 ps, gi = pieces(l, name, zt, True)
                 for s, d in ps:
-                    rcopy(s, d, diag_send.at[gi], diag_recv.at[gi], peer_id(zt)).start()
+                    rcopy(s, d, diag_send.at[l, gi], diag_recv.at[l, gi], peer_id(zt)).start()
 
     def w_s1(l, name):
         buf, gi, _ = groups[name]
@@ -202,9 +199,9 @@
         wait_bytes(buf.at[0, 0], loc_sem.at[l, gi])
         q = buf.at[:, sub]
         if pool == 4:
-            rcopy(q, q, p_send.at[l, gi, 0], p_recv.at[l, gi, 0], xnei).start()
-            rcopy(q, q, p_send.at[l, gi, 1], p_recv.at[l, gi, 1], ynei).start()
-        rcopy(q, q, d_send.at[l, gi, 0], d_recv.at[l, gi, 0], sib).start()
+            rcopy(q, q, p_send.at[l, gi], p_recv.at[l, gi, 0], xnei).start()
+            rcopy(q, q, p_send.at[l, gi], p_recv.at[l, gi, 1], ynei).start()
+        rcopy(q, q, d_send.at[l, gi], d_recv.at[l, gi], sib).start()
 
     def w_s2(l, name):
         if pool == 4:
@@ -214,12 +211,12 @@
             hx, hy = buf.at[0:zh, subx], buf.at[zh:zn, suby]
             wait_bytes(qx, p_recv.at[l, gi, 0])
             if (l, name) not in direct:
-                rcopy(hx, hx, p_send.at[l, gi, 2], p_recv.at[l, gi, 2], ynei).start()
-            rcopy(qx, qx, d_send.at[l, gi, 1], d_recv.at[l, gi, 1], sib).start()
+                rcopy(hx, hx, p_send.at[l, gi], p_recv.at[l, gi, 2], ynei).start()
+            rcopy(qx, qx, d_send.at[l, gi], d_recv.at[l, gi], sib).start()
             wait_bytes(qy, p_recv.at[l, gi, 1])
             if (l, name) not in direct:
-                rcopy(hy, hy, p_send.at[l, gi, 3], p_recv.at[l, gi, 3], xnei).start()
-            rcopy(qy, qy, d_send.at[l, gi, 2], d_recv.at[l, gi, 2], sib).start()
+                rcopy(hy, hy, p_send.at[l, gi], p_recv.at[l, gi, 3], xnei).start()
+            rcopy(qy, qy, d_send.at[l, gi], d_recv.at[l, gi], sib).start()
 
     def w_s3(l, name):
         if pool == 4:
@@ -227,30 +224,27 @@
             buf = buf.at[l]
             q = buf.at[:, subd]
             if (l, name) in direct:
-                wait_bytes(buf.at[0:zn - 1, 0], diag_recv.at[gi])
-                wait_bytes(buf.at[0, 0], diag_loc.at[gi])
+                wait_bytes(buf.at[0:zn - 1, 0], diag_recv.at[l, gi])
+                wait_bytes(buf.at[0, 0], diag_loc.at[l, gi])
             else:
                 wait_bytes(buf.at[0:zh, subd], p_recv.at[l, gi, 2])
                 wait_bytes(buf.at[zh:zn, subd], p_recv.at[l, gi, 3])
-            rcopy(q, q, d_send.at[l, gi, 3], d_recv.at[l, gi, 3], sib).start()
+            rcopy(q, q, d_send.at[l, gi], d_recv.at[l, gi], sib).start()
 
     def w_fin(l, name):
         buf, gi, _ = groups[name]
         buf = buf.at[l]
-        for i in range(pool):
-            wait_bytes(buf.at[:, 0], d_recv.at[l, gi, i])
+        wait_bytes(buf.at[:, 0:pool], d_recv.at[l, gi])
 
     def w_drain(l, name):
         buf, gi, _ = groups[name]
         buf = buf.at[l]
         wait_bytes(buf.at[0:zn - 1, 0], z_send.at[l, gi])
-        for i in range(pool):
-            wait_bytes(buf.at[:, 0], d_send.at[l, gi, i])
+        wait_bytes(buf.at[:, 0:pool], d_send.at[l, gi])
         if (l, name) in direct:
-            wait_bytes(buf.at[0:zn - 1, 0], diag_send.at[gi])
+            wait_bytes(buf.at[0:zn - 1, 0], diag_send.at[l, gi])
         if pool == 4:
-            for i in range(2 if (l, name) in direct else 4):
-                wait_bytes(buf.at[:, 0] if i < 2 else buf.at[0:zh, 0], p_send.at[l, gi, i])
+            wait_bytes(buf.at[:, 0:2 if (l, name) in direct else 3], p_send.at[l, gi])
 
     def spread(src_of, dst, l, ph):
         for r in order:
@@ -266,24 +260,22 @@
     end = layers - 1
     plan = {
         (0, "entry"): [(w_send, 0, "q"), (w_send, 0, "kv"), (w_diag, 0, "q"), (w_diag, 0, "kv")],
-        (0, "x_wait"): [(ring, end, 0), (w_s1, 0, "q"), (w_s1, 0, "kv"), (w_send, 0, "o"), (w_send, 0, "gu"), (w_s2, 0, "q"), (w_s3, 0, "q"), (w_s2, 0, "kv"), (w_s3, 0, "kv")],
-        (0, "qkv_sent"): [(ring, end, 1), (w_send, 1, "q"), (w_send, 1, "kv"), (w_s1, 0, "o"), (of_own, end, 0), (of_own, end, 1)],
-        (0, "qkv_in"): [(w_s2, 0, "o"), (w_s1, 0, "gu")],
-        (0, "o_sent"): [(ring, end, 2), (w_s3, 0, "o"), (w_s2, 0, "gu"), (w_s1, 1, "q"), (w_s1, 1, "kv"), (of_relay, end, 0), (of_own, end, 2)],
-        (0, "x1_sent"): [(ring, end, 3), (w_send, 1, "gu"), (w_s3, 0, "gu"), (of_own, end, 3)],
-        (0, "x1_in"): [(w_s2, 1, "q"), (w_s2, 1, "kv")],
-        (0, "y_sent"): [(of_relay, end, 1), (of_relay, end, 2), (w_s1, 1, "gu"), (w_s3, 1, "q"), (w_s3, 1, "kv"), (of_own, end, zh)],
-        (1, "x_sent"): [(of_relay, end, 3), (of_relay, end, zh), (of_last, end, 0), (of_last, end, 1), (of_last, end, 2)],
-        (1, "qkv_sent"): [(w_s2, 1, "gu"), (of_last, end, 3), (of_last, end, zh)],
-        (1, "x1_sent"): [(w_s3, 1, "gu")],
+        (0, "x_wait"): [(w_s1, 0, "q"), (w_s1, 0, "kv"), (w_send, 0, "o"), (w_send, 0, "g"), (w_s2, 0, "q"), (w_s3, 0, "q"), (w_s2, 0, "kv"), (w_s3, 0, "kv")],
+        (0, "qkv_sent"): [(w_send, 0, "u"), (ring, end, 0), (w_s1, 0, "o"), (of_own, end, 0), (w_s1, 0, "g")],
+        (0, "o_sent"): [(w_s2, 0, "o"), (w_s1, 0, "u"), (ring, end, 1), (w_s3, 0, "o"), (w_s2, 0, "g"), (of_own, end, 1), (of_relay, end, 0)],
+        (0, "x1_sent"): [(w_s2, 0, "u"), (ring, end, 2), (w_send, 1, "q"), (w_send, 1, "kv"), (w_s3, 0, "g"), (of_own, end, 2), (w_s3, 0, "u"), (of_relay, end, 1)],
+        (0, "y_sent"): [(ring, end, 3), (w_send, 1, "g"), (w_s1, 1, "q"), (w_s1, 1, "kv"), (of_own, end, 3), (of_relay, end, 2)],
+        (1, "x_sent"): [(w_s2, 1, "q"), (w_s2, 1, "kv"), (w_send, 1, "u"), (of_own, end, zh), (of_relay, end, 3), (w_s3, 1, "q"), (w_s3, 1, "kv"), (of_last, end, 0), (of_last, end, 1), (w_s1, 1, "g")],
+        (1, "qkv_sent"): [(of_relay, end, zh), (w_s1, 1, "u"), (of_last, end, 2), (w_s2, 1, "g"), (of_last, end, 3), (of_last, end, zh)],
+        (1, "x1_sent"): [(w_s2, 1, "u"), (w_s3, 1, "g"), (w_s3, 1, "u")],
     } if full_o else {
-        (0, "entry"): [(w_send, 0, "q"), (w_send, 0, "kv"), (w_send, 0, "o"), (w_send, 0, "gu")],
+        (0, "entry"): [(w_send, 0, "q"), (w_send, 0, "kv"), (w_send, 0, "o"), (w_send, 0, "g"), (w_send, 0, "u")],
         (0, "x_wait"): [(w_s1, 0, "q"), (w_s1, 0, "kv")],
         (0, "qkv_sent"): [(w_s1, 0, "o"), (w_send, 1, "q"), (w_send, 1, "kv"), (w_send, 1, "o")],
-        (0, "o_sent"): [(w_s1, 0, "gu")],
-        (0, "x1_sent"): [(w_send, 1, "gu"), (w_s1, 1, "q"), (w_s1, 1, "kv")],
+        (0, "o_sent"): [(w_s1, 0, "g"), (w_s1, 0, "u")],
+        (0, "x1_sent"): [(w_send, 1, "g"), (w_send, 1, "u"), (w_s1, 1, "q"), (w_s1, 1, "kv")],
         (0, "y_sent"): [(w_s1, 1, "o")],
-        (1, "qkv_sent"): [(w_s1, 1, "gu")],
+        (1, "qkv_sent"): [(w_s1, 1, "g"), (w_s1, 1, "u")],
     }
 
     def background(l, point):
@@ -296,7 +288,7 @@
         cp.start()
     for l in range(layers):
         pltpu.make_async_copy(wd_hbm.at[l], wd.at[l, c], down_loc.at[l, 0]).start()
-        for name in ("q", "kv", "o", "gu"):
+        for name in ("q", "kv", "o", "g", "u"):
             if not skip(l, name):
                 w_local(l, name)
         pltpu.make_async_copy(kc_hbm.at[l], kc.at[l], down_loc.at[l, 1]).start()
@@ -386,7 +378,8 @@
         background(l, "x1_sent")
         wait_bytes(wd.at[l, 0], down_loc.at[l, 0])
         wait_bytes(wd.at[l, 0], down_recv.at[l])
-        w_fin(l, "gu")
+        w_fin(l, "g")
+        w_fin(l, "u")
         arrived(x1r, None, 3)
         return x1r[...].astype(F32).reshape(nq, dm)
 
@@ -403,7 +396,8 @@
         background(l, "x1_sent")
         wait_bytes(wd.at[l, 0], down_loc.at[l, 0])
         wait_bytes(wd.at[l, 0], down_recv.at[l])
-        w_fin(l, "gu")
+        w_fin(l, "g")
+        w_fin(l, "u")
         arrived(x1g, l, 3)
         background(l, "x1_in")
         return jnp.concatenate([x1g[l, zz].astype(F32) for zz in range(zn)], axis=-1)
@@ -434,10 +428,10 @@
         x1 = own_rows(l) if l in full_o else gathered_rows(l)
         x1f[...] = x1
         h2 = (rms(x1, dm) * mn_ref[l:l + 1, :].astype(F32)).astype(BF16)
-        gu = jnp.dot(h2, wgu[l].reshape(dm, wgu.shape[-1]), preferred_element_type=F32)
-        ffc = wgu.shape[-1] // 2
-        g = gu[:, :ffc]
-        a = (g * jax.nn.sigmoid(g) * gu[:, ffc:]).astype(BF16)
+        ffc = wg.shape[-1]
+        g = jnp.dot(h2, wg[l].reshape(dm, ffc), preferred_element_type=F32)
+        u = jnp.dot(h2, wu[l].reshape(dm, ffc), preferred_element_type=F32)
+        a = (g * jax.nn.sigmoid(g) * u).astype(BF16)
         pr = jnp.dot(a, wd[l].reshape(ffc, dm), preferred_element_type=F32)
         pbuf[l] = pr.reshape(zn, tok, dm)
         spread(lambda zt: pbuf.at[l, zt], ybuf.at[l, z], l, 4)
@@ -526,7 +520,8 @@
             pltpu.VMEM((layers, zn, nq, w_k.shape[1] // pool, 2 * kw // zn), BF16),
             pltpu.VMEM((layers, zn, nq, w_o.shape[1] // pool, dm // zn), BF16),
             pltpu.VMEM((1, zn, nq, w_o.shape[1] // pool, dm), BF16),
-            pltpu.VMEM((layers, zn, nq, w_gate.shape[1] // pool, 2 * ff // zn), BF16),
+            pltpu.VMEM((layers, zn, nq, w_gate.shape[1] // pool, ff // zn), BF16),
+            pltpu.VMEM((layers, zn, nq, w_up.shape[1] // pool, ff // zn), BF16),
             pltpu.VMEM((layers, 2, w_down.shape[1], dm), BF16),
             pltpu.VMEM(flat, BF16),
             pltpu.VMEM(flat, BF16),
@@ -555,8 +550,8 @@
             pltpu.VMEM((tok * kh, hd), BF16),
             pltpu.VMEM((layers, tok * kh, hd), BF16),
             pltpu.VMEM((layers, tok * kh, hd), BF16),
-            dma((layers, 4)), dma((layers, 4)), dma((layers, 4, pool)), dma((layers, 4, pool)), dma((layers, 4, 4)), dma((layers, 4, 4)),
-            dma((layers, 5)), dma((layers, 5)), dma((layers,)), dma((layers,)), dma((layers, 4)), dma((layers, 3)), dma((6,)), dma((1 + 2 * layers,)), dma((2,)), dma((2,)), dma((2,)), dma((2, zn // 2)), dma((2, zn // 2)), dma((7,)), dma((3, zn // 2 + 1)), dma((4,)),
+            dma((layers, 5)), dma((layers, 5)), dma((layers, 5)), dma((layers, 5)), dma((layers, 5)), dma((layers, 5, 4)),
+            dma((layers, 5)), dma((layers, 5)), dma((layers,)), dma((layers,)), dma((layers, 5)), dma((layers, 3)), dma((6,)), dma((1 + 2 * layers,)), dma((1, 2)), dma((1, 2)), dma((1, 2)), dma, dma((2, zn // 2)), dma, dma((3, zn // 2 + 1)), dma,
         ]
         res = pl.pallas_call(
             functools.partial(decode_kernel, cfg),

time: 85.9 us -> 85.8 us (level)
  the two profiles are of different devices: /device:TPU:30 before, /device:TPU:21 now
where the time goes in v7:
time: 85.8 us; the launch traced here: 85.6 us
  Pallas kernels  84.9 us (99%)
    pallas_call x1, Pallas kernels, device_fn(): pl.pallas_call(functools.partial(decode_kernel, cfg), name='decode', out_...  80.4 us
    pallas_call x1, Pallas kernels, device_fn(): pl.pallas_call(functools.partial(place_rows, layers, tok, kh), name='plac...  4.49 us

profile of v7, /device:TPU:21, one launch (start us, length us, event | category | flops | bytes accessed | tf_op | source)
XLA Modules:
  0.0 85.6 jit_solution(13056229148536289695)
XLA Ops:
  0.6 0.0 copy-start
  0.6 0.0 copy-start.1
  0.7 0.0 copy-start.2
  0.7 80.4 %decode.1.res_hbm = bf16[4096,64,128]{2,1,0:T(8,128)(2,1)} custom-call(s32[8]{0:T(128)} %pos_hbm.3, bf16[8,1024]{1,0:T(8,128)(2,1)} %x_hbm.1, bf16[2,1024]{1,0:T(2,128)(2,1)} %an_hbm.1, bf16[2,128]{1,0:T(2,128)(2,1)} %qn_hbm.1, bf16[2,128]{1,0:T(2,128)(2,1)} %kn_hbm.1, bf16[2,1024]{1,0:T(2,128)(2,1)} %mn_hbm.1, bf16[2,64,2048]{2,1,0:T(8,128)(2,1)} %wq_hbm.1, ...), custom_call_target="tpu_custom_call" | custom-call | tf_op jit(solution)/shard_map/decode/pallas_call | solution.py:556
  81.1 0.0 copy-done
  81.1 0.0 copy-done.1
  81.1 0.0 copy-done.2
  81.1 4.5 %place.1 = (bf16[8,1024]{1,0:T(8,128)(2,1)}, bf16[2,8,1024,128]{3,2,1,0:T(8,128)(2,1)}, bf16[2,8,1024,128]{3,2,1,0:T(8,128)(2,1)}) custom-call(s32[8]{0:T(128)S(1)} %copy-done.2, bf16[4096,64,128]{2,1,0:T(8,128)(2,1)} %decode.1.res_hbm, bf16[2,8,1024,128]{3,2,1,0:T(8,128)(2,1)S(1)} %bitcast.5, bf16[2,8,1024,128]{3,2,1,0:T(8,128)(2,1)S(1)} %bitcast.7), custom_call_target="tpu_custom_call" | custom-call | tf_op jit(solution)/shard_map/place/pallas_call | solution.py:567
Async XLA Ops:
  0.6 80.5 %copy-start = (bf16[2,8,128,8,128]{4,3,2,1,0:T(8,128)(2,1)S(1)}, bf16[2,8,128,8,128]{4,3,2,1,0:T(8,128)(2,1)}, u32[]{:S(2)}) copy-start(bf16[2,8,128,8,128]{4,3,2,1,0:T(8,128)(2,1)} %param.17) | copy-start | bytes 12582916
  0.6 80.5 %copy-start.1 = (bf16[2,8,128,8,128]{4,3,2,1,0:T(8,128)(2,1)S(1)}, bf16[2,8,128,8,128]{4,3,2,1,0:T(8,128)(2,1)}, u32[]{:S(2)}) copy-start(bf16[2,8,128,8,128]{4,3,2,1,0:T(8,128)(2,1)} %param.18) | copy-start | bytes 12582916
  0.7 80.5 %copy-start.2 = (s32[8]{0:T(128)S(1)}, s32[8]{0:T(128)}, u32[]{:S(2)}) copy-start(s32[8]{0:T(128)} %pos_hbm.3) | copy-start | bytes 100

commit v8 on v7

--- a/solution.py
+++ b/solution.py
@@ -27,8 +27,8 @@
 
 def decode_kernel(cfg, pos_hbm, x_hbm, an_hbm, qn_hbm, kn_hbm, mn_hbm, wq_hbm, wk_hbm, wv_hbm, wo_hbm, wg_hbm, wu_hbm, wd_hbm, kc_hbm, vc_hbm,
                   res_hbm,
-                  wq, wkv, wo, wof, wg, wu, wd, kc, vc, xg, qkvs, qkvi, og, x1g, x1r, pbuf, ybuf, x1f, qs, ks, vs, os_, kro, vro, cs, sn, pos_ref, an_ref, qn_ref, kn_ref, mn_ref, y_ref, krow_ref, vrow_ref,
-                  z_send, z_recv, d_send, d_recv, p_send, p_recv, a_send, a_recv, down_send, down_recv, loc_sem, down_loc, in_sem, out_sem, diag_send, diag_recv, diag_loc, ring_send, ring_recv, of_send, of_recv, of_sib):
+                  wq, wkv, wo, wof, wg, wu, wd, kc, vc, xg, qkvs, qkvi, og, x1g, x1r, pbuf, ybuf, x1f, qs, ks, vs, os_, kro, vro, cs, sn, slot_ref, pos_ref, an_ref, qn_ref, kn_ref, mn_ref, y_ref, krow_ref, vrow_ref,
+                  z_recv, d_recv, p_recv, a_recv, down_recv, loc_sem, down_loc, in_sem, out_sem, diag_recv, diag_loc, ring_recv, of_recv, of_sib, send_sem):
     layers, zn, pool, tok = cfg["layers"], cfg["zn"], cfg["pool"], cfg["tok"]
     qh, kh, ny = cfg["qh"], cfg["kh"], cfg["ny"]
     dm = x_hbm.shape[1]
@@ -71,7 +71,10 @@
         pl.semaphore_signal(barrier, inc=1, device_id=xnei, device_id_type=MESH)
         pl.semaphore_signal(barrier, inc=1, device_id=ynei, device_id_type=MESH)
 
+    sent = []
+
     def rcopy(src, dst, ss, rs, dev):
+        sent.append(math.prod(src.shape) * src.dtype.itemsize)
         return pltpu.make_async_remote_copy(src_ref=src, dst_ref=dst, send_sem=ss, recv_sem=rs, device_id=dev, device_id_type=MESH)
 
     def wait_bytes(ref, sem):
@@ -106,31 +109,27 @@
             ring(l, zh)
         for b in signed(d):
             q = r_block(b)
-            rcopy(q, q, of_send, of_recv.at[0, d], xnei).start()
-            rcopy(q, q, of_send, of_recv.at[1, d], ynei).start()
-            rcopy(q, q, of_send, of_sib, sib).start()
+            rcopy(q, q, send_sem, of_recv.at[0, d], xnei).start()
+            rcopy(q, q, send_sem, of_recv.at[0, d], ynei).start()
+            rcopy(q, q, send_sem, of_sib, sib).start()
 
     def of_relay(l, d):
+        wait_bytes(wof.at[0, 0:len(signed(d)), 0:2], of_recv.at[0, d])
         for i, which, to in ((0, subx, ynei), (1, suby, xnei)):
-            wait_bytes(wof.at[0, 0:len(signed(d)), 0], of_recv.at[i, d])
             for b in signed(d):
                 q = r_block(b, which)
                 if (b > 0 if i == 0 else b <= 0):
-                    rcopy(q, q, of_send, of_recv.at[2, d], to).start()
-                rcopy(q, q, of_send, of_sib, sib).start()
+                    rcopy(q, q, send_sem, of_recv.at[1, d], to).start()
+                rcopy(q, q, send_sem, of_sib, sib).start()
 
     def of_last(l, d):
-        wait_bytes(wof.at[0, 0:len(signed(d)), 0], of_recv.at[2, d])
+        wait_bytes(wof.at[0, 0:len(signed(d)), 0], of_recv.at[1, d])
         for b in signed(d):
             q = r_block(b, subd)
-            rcopy(q, q, of_send, of_sib, sib).start()
+            rcopy(q, q, send_sem, of_sib, sib).start()
 
     def of_fin():
         wait_bytes(wof.at[0, :, 0:4], of_sib)
-
-    def of_drain():
-        wait_bytes(wof.at[0, :, 0:7], of_send)
-        wait_bytes(wof.at[0, 0:zn - 1, 0], ring_send)
 
     def r_halves(d):
         blk = lax.rem(z + zn + d, zn)
@@ -140,17 +139,17 @@
         if step == 0:
             src = wo_hbm.at[l, pl.ds(pl.multiple_of(quarter * 2 * half_rows, 2 * half_rows), 2 * half_rows)]
             pltpu.make_async_copy(src, r_block(0), loc_sem.at[l, 2]).start()
-            rcopy(src, r_block(0), ring_send, ring_recv.at[0, 0], right).start()
-            rcopy(src, r_block(0), ring_send, ring_recv.at[1, 0], left).start()
+            rcopy(src, r_block(0), send_sem, ring_recv.at[0, 0], right).start()
+            rcopy(src, r_block(0), send_sem, ring_recv.at[1, 0], left).start()
         elif step < zh - 1:
             for i, d, to in ((0, -step, right), (1, step, left)):
                 wait_bytes(r_block(d), ring_recv.at[i, step - 1])
-                rcopy(r_block(d), r_block(d), ring_send, ring_recv.at[i, step], to).start()
+                rcopy(r_block(d), r_block(d), send_sem, ring_recv.at[i, step], to).start()
         elif step == zh - 1:
             for i, d, to in ((0, -step, right), (1, step, left)):
                 wait_bytes(r_block(d), ring_recv.at[i, step - 1])
                 h = r_halves(d)[i]
-                rcopy(h, h, ring_send, ring_recv.at[i, step], to).start()
+                rcopy(h, h, send_sem, ring_recv.at[i, step], to).start()
         else:
             for i in range(2):
                 wait_bytes(r_halves(zh)[i], ring_recv.at[i, zh - 1])
@@ -182,7 +181,7 @@
             zt = peer(r)
             ps, gi = pieces(l, name, zt)
             for s, d in ps:
-                rcopy(s, d, z_send.at[l, gi], z_recv.at[l, gi], peer_id(zt)).start()
+                rcopy(s, d, send_sem, z_recv.at[l, gi], peer_id(zt)).start()
 
     def w_diag(l, name):
         if (l, name) in direct:
@@ -190,7 +189,7 @@
                 zt = peer(r)
                 ps, gi = pieces(l, name, zt, True)
                 for s, d in ps:
-                    rcopy(s, d, diag_send.at[l, gi], diag_recv.at[l, gi], peer_id(zt)).start()
+                    rcopy(s, d, send_sem, diag_recv.at[l, gi], peer_id(zt)).start()
 
     def w_s1(l, name):
         buf, gi, _ = groups[name]
@@ -199,9 +198,9 @@
         wait_bytes(buf.at[0, 0], loc_sem.at[l, gi])
         q = buf.at[:, sub]
         if pool == 4:
-            rcopy(q, q, p_send.at[l, gi], p_recv.at[l, gi, 0], xnei).start()
-            rcopy(q, q, p_send.at[l, gi], p_recv.at[l, gi, 1], ynei).start()
-        rcopy(q, q, d_send.at[l, gi], d_recv.at[l, gi], sib).start()
+            rcopy(q, q, send_sem, p_recv.at[l, gi, 0], xnei).start()
+            rcopy(q, q, send_sem, p_recv.at[l, gi, 0], ynei).start()
+        rcopy(q, q, send_sem, d_recv.at[l, gi], sib).start()
 
     def w_s2(l, name):
         if pool == 4:
@@ -209,14 +208,12 @@
             buf = buf.at[l]
             qx, qy = buf.at[:, subx], buf.at[:, suby]
             hx, hy = buf.at[0:zh, subx], buf.at[zh:zn, suby]
-            wait_bytes(qx, p_recv.at[l, gi, 0])
+            wait_bytes(buf.at[:, 0:2], p_recv.at[l, gi, 0])
             if (l, name) not in direct:
-                rcopy(hx, hx, p_send.at[l, gi], p_recv.at[l, gi, 2], ynei).start()
-            rcopy(qx, qx, d_send.at[l, gi], d_recv.at[l, gi], sib).start()
-            wait_bytes(qy, p_recv.at[l, gi, 1])
-            if (l, name) not in direct:
-                rcopy(hy, hy, p_send.at[l, gi], p_recv.at[l, gi, 3], xnei).start()
-            rcopy(qy, qy, d_send.at[l, gi], d_recv.at[l, gi], sib).start()
+                rcopy(hx, hx, send_sem, p_recv.at[l, gi, 1], ynei).start()
+                rcopy(hy, hy, send_sem, p_recv.at[l, gi, 1], xnei).start()
+            rcopy(qx, qx, send_sem, d_recv.at[l, gi], sib).start()
+            rcopy(qy, qy, send_sem, d_recv.at[l, gi], sib).start()
 
     def w_s3(l, name):
         if pool == 4:
@@ -227,29 +224,18 @@
                 wait_bytes(buf.at[0:zn - 1, 0], diag_recv.at[l, gi])
                 wait_bytes(buf.at[0, 0], diag_loc.at[l, gi])
             else:
-                wait_bytes(buf.at[0:zh, subd], p_recv.at[l, gi, 2])
-                wait_bytes(buf.at[zh:zn, subd], p_recv.at[l, gi, 3])
-            rcopy(q, q, d_send.at[l, gi], d_recv.at[l, gi], sib).start()
+                wait_bytes(buf.at[:, subd], p_recv.at[l, gi, 1])
+            rcopy(q, q, send_sem, d_recv.at[l, gi], sib).start()
 
     def w_fin(l, name):
         buf, gi, _ = groups[name]
         buf = buf.at[l]
         wait_bytes(buf.at[:, 0:pool], d_recv.at[l, gi])
 
-    def w_drain(l, name):
-        buf, gi, _ = groups[name]
-        buf = buf.at[l]
-        wait_bytes(buf.at[0:zn - 1, 0], z_send.at[l, gi])
-        wait_bytes(buf.at[:, 0:pool], d_send.at[l, gi])
-        if (l, name) in direct:
-            wait_bytes(buf.at[0:zn - 1, 0], diag_send.at[l, gi])
-        if pool == 4:
-            wait_bytes(buf.at[:, 0:2 if (l, name) in direct else 3], p_send.at[l, gi])
-
     def spread(src_of, dst, l, ph):
         for r in order:
             zt = peer(r)
-            rcopy(src_of(zt), dst, a_send.at[l, ph], a_recv.at[l, ph], peer_id(zt)).start()
+            rcopy(src_of(zt), dst, send_sem, a_recv.at[l, ph], peer_id(zt)).start()
 
     def arrived(buf, l, ph):
         if l is None:
@@ -294,13 +280,19 @@
         pltpu.make_async_copy(kc_hbm.at[l], kc.at[l], down_loc.at[l, 1]).start()
         pltpu.make_async_copy(vc_hbm.at[l], vc.at[l], down_loc.at[l, 2]).start()
 
+    cols = kc.shape[2]
+    lane = lax.broadcasted_iota(jnp.int32, (qh, cols), 1)
+    row = lax.broadcasted_iota(jnp.int32, (qh, cols), 0)
+    mine = lax.rem(lane, kh) == lax.shift_right_logical(row, 1)
+    slot_ref[...] = jnp.where(mine, lax.div(lane, kh), cols)
+
     pl.semaphore_wait(barrier, zn + (2 if pool == 4 else 0))
 
     background(0, "entry")
     small_copies[0].wait()
     spread(lambda zt: xg.at[0, z], xg.at[0, z], 0, 0)
     for l in range(layers):
-        rcopy(wd_hbm.at[l], wd.at[l, c], down_send.at[l], down_recv.at[l], sib).start()
+        rcopy(wd_hbm.at[l], wd.at[l, c], send_sem, down_recv.at[l], sib).start()
 
     for cp in small_copies[1:]:
         cp.wait()
@@ -342,18 +334,14 @@
             vro[pl.ds(h, tok, stride=kh), :] = v
         krow_ref[l] = kro[...].astype(BF16)
         vrow_ref[l] = vro[...].astype(BF16)
-        outs.append(pltpu.make_async_copy(krow_ref.at[l], res_hbm.at[1 + 2 * l], out_sem.at[1 + 2 * l]))
-        outs.append(pltpu.make_async_copy(vrow_ref.at[l], res_hbm.at[2 + 2 * l], out_sem.at[2 + 2 * l]))
+        outs.append(pltpu.make_async_copy(krow_ref.at[l], res_hbm.at[1 + 2 * l], out_sem))
+        outs.append(pltpu.make_async_copy(vrow_ref.at[l], res_hbm.at[2 + 2 * l], out_sem))
         outs[-2].start()
         outs[-1].start()
-        cols = kc.shape[2]
-        lane = lax.broadcasted_iota(jnp.int32, (qh, cols), 1)
-        row = lax.broadcasted_iota(jnp.int32, (qh, cols), 0)
-        mine = lax.rem(lane, kh) == lax.shift_right_logical(row, 1)
-        slot = jnp.where(mine, lax.div(lane, kh), cols)
+        slot = slot_ref[...]
         scale = HEAD_DIM ** -0.5
-        for n0 in range(0, tok, 4):
-            seqs = range(n0, n0 + 4)
+        for n0 in range(0, tok, 8):
+            seqs = range(n0, n0 + 8)
             rows = [slice(n * qh, (n + 1) * qh) for n in seqs]
             q = [qs[r, :] for r in rows]
             s = [lax.dot_general(a.astype(BF16), kc[l, n], (((1,), (1,)), ((), ())), preferred_element_type=F32) * scale for a, n in zip(q, seqs)]
@@ -444,25 +432,17 @@
         y = x1f[pl.ds(pl.multiple_of(z * tok, tok), tok), :] + total
         if last:
             y_ref[...] = jnp.concatenate([y[:, t * HEAD_DIM:(t + 1) * HEAD_DIM] for t in range(dm // HEAD_DIM)], axis=0).astype(BF16)
-            outs.append(pltpu.make_async_copy(y_ref, res_hbm.at[0], out_sem.at[0]))
+            outs.append(pltpu.make_async_copy(y_ref, res_hbm.at[0], out_sem))
             outs[-1].start()
         else:
             xg[l + 1, z] = y.astype(BF16)
             spread(lambda zt: xg.at[l + 1, z], xg.at[l + 1, z], l + 1, 0)
             background(l + 1, "x_sent")
 
-    for l in range(layers):
-        for name in groups:
-            if not skip(l, name):
-                w_drain(l, name)
-        if l in full_o:
-            of_drain()
-        wait_bytes(wd.at[l, 0], down_send.at[l])
-        for ph, buf in enumerate((xg, qkvi, og, x1g, ybuf)):
-            if ph != 2 or l not in full_o:
-                wait_bytes(buf.at[l, 0:zn - 1], a_send.at[l, ph])
-    for cp in outs:
-        cp.wait()
+    rows = sum(sent) // (res_hbm.shape[2] * 2)
+    part_rows = math.gcd(rows, res_hbm.shape[1])
+    wait_bytes(res_hbm.at[0:rows // part_rows, 0:part_rows], send_sem)
+    wait_bytes(res_hbm.at[0:len(outs)], out_sem)
 
 
 def place_rows(layers, tok, kh, pos_hbm, res_hbm, kin, vin, y_out, kout, vout, pos_ref, res, in_sem, y_sem, bulk_sem, row_sem):
@@ -542,6 +522,7 @@
             pltpu.VMEM((tok * kh, hd), F32),
             pltpu.VMEM((tok, hd), F32),
             pltpu.VMEM((tok, hd), F32),
+            pltpu.VMEM((qh, slots * kh), jnp.int32),
             pltpu.SMEM((tok,), jnp.int32),
             pltpu.VMEM((layers, dm), BF16),
             pltpu.VMEM((layers, hd), BF16),
@@ -550,8 +531,8 @@
             pltpu.VMEM((tok * kh, hd), BF16),
             pltpu.VMEM((layers, tok * kh, hd), BF16),
             pltpu.VMEM((layers, tok * kh, hd), BF16),
-            dma((layers, 5)), dma((layers, 5)), dma((layers, 5)), dma((layers, 5)), dma((layers, 5)), dma((layers, 5, 4)),
-            dma((layers, 5)), dma((layers, 5)), dma((layers,)), dma((layers,)), dma((layers, 5)), dma((layers, 3)), dma((6,)), dma((1 + 2 * layers,)), dma((1, 2)), dma((1, 2)), dma((1, 2)), dma, dma((2, zn // 2)), dma, dma((3, zn // 2 + 1)), dma,
+            dma((layers, 5)), dma((layers, 5)), dma((layers, 5, 2)), dma((layers, 5)), dma((layers,)), dma((layers, 5)), dma((layers, 3)), dma((6,)), dma,
+            dma((1, 2)), dma((1, 2)), dma((2, zn // 2)), dma((2, zn // 2 + 1)), dma, dma,
         ]
         res = pl.pallas_call(
             functools.partial(decode_kernel, cfg),

time: 85.8 us -> 83.9 us (0.978)
  Pallas kernels: 84.9 us -> 83 us
    pallas_call x1, Pallas kernels: 80.4 us -> 78.5 us  [device_fn(): pl.pallas_call(functools.partial(decode_kernel, cfg), name='decode', out_...]
where the time goes in v8:
time: 83.9 us; the launch traced here: 83.7 us
  Pallas kernels  83 us (99%)
    pallas_call x1, Pallas kernels, device_fn(): pl.pallas_call(functools.partial(decode_kernel, cfg), name='decode', out_...  78.5 us
    pallas_call x1, Pallas kernels, device_fn(): pl.pallas_call(functools.partial(place_rows, layers, tok, kh), name='plac...  4.49 us

profile of v8, /device:TPU:21, one launch (start us, length us, event | category | flops | bytes accessed | tf_op | source)
XLA Modules:
  0.0 83.7 jit_solution(1133907424467700451)
XLA Ops:
  0.6 0.0 copy-start
  0.6 0.0 copy-start.1
  0.7 0.0 copy-start.2
  0.7 78.5 %decode.1.res_hbm = bf16[4096,64,128]{2,1,0:T(8,128)(2,1)} custom-call(s32[8]{0:T(128)} %pos_hbm.3, bf16[8,1024]{1,0:T(8,128)(2,1)} %x_hbm.1, bf16[2,1024]{1,0:T(2,128)(2,1)} %an_hbm.1, bf16[2,128]{1,0:T(2,128)(2,1)} %qn_hbm.1, bf16[2,128]{1,0:T(2,128)(2,1)} %kn_hbm.1, bf16[2,1024]{1,0:T(2,128)(2,1)} %mn_hbm.1, bf16[2,64,2048]{2,1,0:T(8,128)(2,1)} %wq_hbm.1, ...), custom_call_target="tpu_custom_call" | custom-call | tf_op jit(solution)/shard_map/decode/pallas_call | solution.py:537
  79.2 0.0 copy-done
  79.2 0.0 copy-done.1
  79.2 0.0 copy-done.2
  79.2 4.5 %place.1 = (bf16[8,1024]{1,0:T(8,128)(2,1)}, bf16[2,8,1024,128]{3,2,1,0:T(8,128)(2,1)}, bf16[2,8,1024,128]{3,2,1,0:T(8,128)(2,1)}) custom-call(s32[8]{0:T(128)S(1)} %copy-done.2, bf16[4096,64,128]{2,1,0:T(8,128)(2,1)} %decode.1.res_hbm, bf16[2,8,1024,128]{3,2,1,0:T(8,128)(2,1)S(1)} %bitcast.5, bf16[2,8,1024,128]{3,2,1,0:T(8,128)(2,1)S(1)} %bitcast.7), custom_call_target="tpu_custom_call" | custom-call | tf_op jit(solution)/shard_map/place/pallas_call | solution.py:548
Async XLA Ops:
  0.6 78.5 %copy-start = (bf16[2,8,128,8,128]{4,3,2,1,0:T(8,128)(2,1)S(1)}, bf16[2,8,128,8,128]{4,3,2,1,0:T(8,128)(2,1)}, u32[]{:S(2)}) copy-start(bf16[2,8,128,8,128]{4,3,2,1,0:T(8,128)(2,1)} %param.17) | copy-start | bytes 12582916
  0.6 78.5 %copy-start.1 = (bf16[2,8,128,8,128]{4,3,2,1,0:T(8,128)(2,1)S(1)}, bf16[2,8,128,8,128]{4,3,2,1,0:T(8,128)(2,1)}, u32[]{:S(2)}) copy-start(bf16[2,8,128,8,128]{4,3,2,1,0:T(8,128)(2,1)} %param.18) | copy-start | bytes 12582916
  0.7 78.5 %copy-start.2 = (s32[8]{0:T(128)S(1)}, s32[8]{0:T(128)}, u32[]{:S(2)}) copy-start(s32[8]{0:T(128)} %pos_hbm.3) | copy-start | bytes 100

commit v9 on v8

--- a/solution.py
+++ b/solution.py
@@ -28,7 +28,7 @@
 def decode_kernel(cfg, pos_hbm, x_hbm, an_hbm, qn_hbm, kn_hbm, mn_hbm, wq_hbm, wk_hbm, wv_hbm, wo_hbm, wg_hbm, wu_hbm, wd_hbm, kc_hbm, vc_hbm,
                   res_hbm,
                   wq, wkv, wo, wof, wg, wu, wd, kc, vc, xg, qkvs, qkvi, og, x1g, x1r, pbuf, ybuf, x1f, qs, ks, vs, os_, kro, vro, cs, sn, slot_ref, pos_ref, an_ref, qn_ref, kn_ref, mn_ref, y_ref, krow_ref, vrow_ref,
-                  z_recv, d_recv, p_recv, a_recv, down_recv, loc_sem, down_loc, in_sem, out_sem, diag_recv, diag_loc, ring_recv, of_recv, of_sib, send_sem):
+                  z_recv, d_recv, p_recv, a_recv, down_recv, of_loc, cache_sem, in_sem, out_sem, diag_recv, ring_recv, of_recv, of_sib, send_sem):
     layers, zn, pool, tok = cfg["layers"], cfg["zn"], cfg["pool"], cfg["tok"]
     qh, kh, ny = cfg["qh"], cfg["kh"], cfg["ny"]
     dm = x_hbm.shape[1]
@@ -104,7 +104,7 @@
 
     def of_own(l, d):
         if d == 0:
-            wait_bytes(r_block(0), loc_sem.at[l, 2])
+            wait_bytes(r_block(0), of_loc)
         elif d == zh:
             ring(l, zh)
         for b in signed(d):
@@ -138,7 +138,7 @@
     def ring(l, step):
         if step == 0:
             src = wo_hbm.at[l, pl.ds(pl.multiple_of(quarter * 2 * half_rows, 2 * half_rows), 2 * half_rows)]
-            pltpu.make_async_copy(src, r_block(0), loc_sem.at[l, 2]).start()
+            pltpu.make_async_copy(src, r_block(0), of_loc).start()
             rcopy(src, r_block(0), send_sem, ring_recv.at[0, 0], right).start()
             rcopy(src, r_block(0), send_sem, ring_recv.at[1, 0], left).start()
         elif step < zh - 1:
@@ -171,10 +171,10 @@
     def w_local(l, name):
         ps, gi = pieces(l, name, z)
         for s, d in ps:
-            pltpu.make_async_copy(s, d, loc_sem.at[l, gi]).start()
+            pltpu.make_async_copy(s, d, z_recv.at[l, gi]).start()
         if (l, name) in direct:
             for s, d in pieces(l, name, z, True)[0]:
-                pltpu.make_async_copy(s, d, diag_loc.at[l, gi]).start()
+                pltpu.make_async_copy(s, d, diag_recv.at[l, gi]).start()
 
     def w_send(l, name):
         for r in order:
@@ -194,8 +194,7 @@
     def w_s1(l, name):
         buf, gi, _ = groups[name]
         buf = buf.at[l]
-        wait_bytes(buf.at[0:zn - 1, 0], z_recv.at[l, gi])
-        wait_bytes(buf.at[0, 0], loc_sem.at[l, gi])
+        wait_bytes(buf.at[:, 0], z_recv.at[l, gi])
         q = buf.at[:, sub]
         if pool == 4:
             rcopy(q, q, send_sem, p_recv.at[l, gi, 0], xnei).start()
@@ -221,8 +220,7 @@
             buf = buf.at[l]
             q = buf.at[:, subd]
             if (l, name) in direct:
-                wait_bytes(buf.at[0:zn - 1, 0], diag_recv.at[l, gi])
-                wait_bytes(buf.at[0, 0], diag_loc.at[l, gi])
+                wait_bytes(buf.at[:, 0], diag_recv.at[l, gi])
             else:
                 wait_bytes(buf.at[:, subd], p_recv.at[l, gi, 1])
             rcopy(q, q, send_sem, d_recv.at[l, gi], sib).start()
@@ -253,7 +251,8 @@
         (0, "y_sent"): [(ring, end, 3), (w_send, 1, "g"), (w_s1, 1, "q"), (w_s1, 1, "kv"), (of_own, end, 3), (of_relay, end, 2)],
         (1, "x_sent"): [(w_s2, 1, "q"), (w_s2, 1, "kv"), (w_send, 1, "u"), (of_own, end, zh), (of_relay, end, 3), (w_s3, 1, "q"), (w_s3, 1, "kv"), (of_last, end, 0), (of_last, end, 1), (w_s1, 1, "g")],
         (1, "qkv_sent"): [(of_relay, end, zh), (w_s1, 1, "u"), (of_last, end, 2), (w_s2, 1, "g"), (of_last, end, 3), (of_last, end, zh)],
-        (1, "x1_sent"): [(w_s2, 1, "u"), (w_s3, 1, "g"), (w_s3, 1, "u")],
+        (1, "att_done"): [(w_s2, 1, "u")],
+        (1, "x1_sent"): [(w_s3, 1, "g"), (w_s3, 1, "u")],
     } if full_o else {
         (0, "entry"): [(w_send, 0, "q"), (w_send, 0, "kv"), (w_send, 0, "o"), (w_send, 0, "g"), (w_send, 0, "u")],
         (0, "x_wait"): [(w_s1, 0, "q"), (w_s1, 0, "kv")],
@@ -273,12 +272,12 @@
     for cp in small_copies:
         cp.start()
     for l in range(layers):
-        pltpu.make_async_copy(wd_hbm.at[l], wd.at[l, c], down_loc.at[l, 0]).start()
+        pltpu.make_async_copy(wd_hbm.at[l], wd.at[l, c], down_recv.at[l]).start()
         for name in ("q", "kv", "o", "g", "u"):
             if not skip(l, name):
                 w_local(l, name)
-        pltpu.make_async_copy(kc_hbm.at[l], kc.at[l], down_loc.at[l, 1]).start()
-        pltpu.make_async_copy(vc_hbm.at[l], vc.at[l], down_loc.at[l, 2]).start()
+        pltpu.make_async_copy(kc_hbm.at[l], kc.at[l], cache_sem.at[0]).start()
+        pltpu.make_async_copy(vc_hbm.at[l], vc.at[l], cache_sem.at[1]).start()
 
     cols = kc.shape[2]
     lane = lax.broadcasted_iota(jnp.int32, (qh, cols), 1)
@@ -359,13 +358,13 @@
             og[l, z, :, h * HEAD_DIM:(h + 1) * HEAD_DIM] = os_[pl.ds(h, tok, stride=qh), :].astype(BF16)
 
     def own_rows(l):
+        background(l, "att_done")
         of_fin()
         r = jnp.dot(og[l, z], wof[0].reshape(og.shape[-1], dm), preferred_element_type=F32)
         x1r[z] = (xg[l, z].astype(F32) + r).astype(BF16)
         spread(lambda zt: x1r.at[z], x1r.at[z], l, 3)
         background(l, "x1_sent")
-        wait_bytes(wd.at[l, 0], down_loc.at[l, 0])
-        wait_bytes(wd.at[l, 0], down_recv.at[l])
+        wait_bytes(wd.at[l], down_recv.at[l])
         w_fin(l, "g")
         w_fin(l, "u")
         arrived(x1r, None, 3)
@@ -382,8 +381,7 @@
         x1g[l, z] = (xc + r).astype(BF16)
         spread(lambda zt: x1g.at[l, z], x1g.at[l, z], l, 3)
         background(l, "x1_sent")
-        wait_bytes(wd.at[l, 0], down_loc.at[l, 0])
-        wait_bytes(wd.at[l, 0], down_recv.at[l])
+        wait_bytes(wd.at[l], down_recv.at[l])
         w_fin(l, "g")
         w_fin(l, "u")
         arrived(x1g, l, 3)
@@ -407,9 +405,8 @@
         qkvi[l, z] = qkvs[l, z]
         background(l, "qkv_sent")
         if l == 0:
-            for k in range(layers):
-                wait_bytes(kc.at[k], down_loc.at[k, 1])
-                wait_bytes(vc.at[k], down_loc.at[k, 2])
+            wait_bytes(kc, cache_sem.at[0])
+            wait_bytes(vc, cache_sem.at[1])
         arrived(qkvi, l, 1)
         background(l, "qkv_in")
         attention(l)
@@ -445,31 +442,28 @@
     wait_bytes(res_hbm.at[0:len(outs)], out_sem)
 
 
-def place_rows(layers, tok, kh, pos_hbm, res_hbm, kin, vin, y_out, kout, vout, pos_ref, res, in_sem, y_sem, bulk_sem, row_sem):
+def place_rows(layers, tok, kh, pos_hbm, res_hbm, kin, vin, y_out, kout, vout, pos_ref, res, in_sem, bulk_sem, out_sem):
     small = [pltpu.make_async_copy(pos_hbm, pos_ref, in_sem.at[0]), pltpu.make_async_copy(res_hbm.at[0:1 + 2 * layers], res, in_sem.at[1])]
     for cp in small:
         cp.start()
     pairs = ((kin, kout), (vin, vout))
-    bulk = [[[pltpu.make_async_copy(src.at[l, n], dst.at[l, n], bulk_sem.at[i, l, n]) for n in range(tok)] for l in range(layers)] for i, (src, dst) in enumerate(pairs)]
     for l in range(layers):
         for n in range(tok):
-            for i in range(2):
-                bulk[i][l][n].start()
+            for src, dst in pairs:
+                pltpu.make_async_copy(src.at[l, n], dst.at[l, n], bulk_sem.at[l, n // 4]).start()
     for cp in small:
         cp.wait()
-    done = [pltpu.make_async_copy(res.at[0, pl.ds(t * tok, tok)], y_out.at[:, pl.ds(t * HEAD_DIM, HEAD_DIM)], y_sem.at[t]) for t in range(y_out.shape[1] // HEAD_DIM)]
-    for cp in done:
-        cp.start()
+    for t in range(y_out.shape[1] // HEAD_DIM):
+        pltpu.make_async_copy(res.at[0, pl.ds(t * tok, tok)], y_out.at[:, pl.ds(t * HEAD_DIM, HEAD_DIM)], out_sem).start()
     for l in range(layers):
         for n in range(tok):
             at = pl.ds(pl.multiple_of(pos_ref[n] * kh, kh), kh)
+            if n % 4 == 0:
+                done = kout.at[l]
+                pltpu.make_async_copy(done, done, bulk_sem.at[l, n // 4]).wait()
             for i, (_, dst) in enumerate(pairs):
-                bulk[i][l][n].wait()
-                cp = pltpu.make_async_copy(res.at[1 + 2 * l + i, pl.ds(n * kh, kh)], dst.at[l, n, at], row_sem.at[i, l, n])
-                cp.start()
-                done.append(cp)
-    for cp in done:
-        cp.wait()
+                pltpu.make_async_copy(res.at[1 + 2 * l + i, pl.ds(n * kh, kh)], dst.at[l, n, at], out_sem).start()
+    pltpu.make_async_copy(res, res, out_sem).wait()
 
 
 def solution(mesh):
@@ -531,8 +525,8 @@
             pltpu.VMEM((tok * kh, hd), BF16),
             pltpu.VMEM((layers, tok * kh, hd), BF16),
             pltpu.VMEM((layers, tok * kh, hd), BF16),
-            dma((layers, 5)), dma((layers, 5)), dma((layers, 5, 2)), dma((layers, 5)), dma((layers,)), dma((layers, 5)), dma((layers, 3)), dma((6,)), dma,
-            dma((1, 2)), dma((1, 2)), dma((2, zn // 2)), dma((2, zn // 2 + 1)), dma, dma,
+            dma((layers, 5)), dma((layers, 5)), dma((layers, 5, 2)), dma((layers, 5)), dma((layers,)), dma, dma((2,)), dma((6,)), dma,
+            dma((1, 2)), dma((2, zn // 2)), dma((2, zn // 2 + 1)), dma, dma,
         ]
         res = pl.pallas_call(
             functools.partial(decode_kernel, cfg),
@@ -551,7 +545,7 @@
             out_shape=(jax.ShapeDtypeStruct((tok, dm), BF16), jax.ShapeDtypeStruct(flat, BF16), jax.ShapeDtypeStruct(flat, BF16)),
             in_specs=[anys] * 4,
             out_specs=(anys,) * 3,
-            scratch_shapes=[pltpu.SMEM((tok,), jnp.int32), pltpu.VMEM(rows, BF16), dma((2,)), dma((dm // hd,)), dma((2, layers, tok)), dma((2, layers, tok))],
+            scratch_shapes=[pltpu.SMEM((tok,), jnp.int32), pltpu.VMEM(rows, BF16), dma((2,)), dma((layers, tok // 4)), dma],
             compiler_params=pltpu.CompilerParams(vmem_limit_bytes=PLACE_LIMIT),
         )(positions, res, k_cache.reshape(flat), v_cache.reshape(flat))
         k_out = k_out.reshape(k_cache.shape)

time: 83.9 us -> 82.3 us (0.981)
  Pallas kernels: 83 us -> 81.4 us
    pallas_call x1, Pallas kernels: 78.5 us -> 77.5 us  [device_fn(): pl.pallas_call(functools.partial(decode_kernel, cfg), name='decode', out_...]
where the time goes in v9:
time: 82.3 us; the launch traced here: 82.1 us
  Pallas kernels  81.4 us (99%)
    pallas_call x1, Pallas kernels, device_fn(): pl.pallas_call(functools.partial(decode_kernel, cfg), name='decode', out_...  77.5 us
    pallas_call x1, Pallas kernels, device_fn(): pl.pallas_call(functools.partial(place_rows, layers, tok, kh), name='plac...  3.92 us

profile of v9, /device:TPU:21, one launch (start us, length us, event | category | flops | bytes accessed | tf_op | source)
XLA Modules:
  0.0 82.1 jit_solution(17464168441078277504)
XLA Ops:
  0.6 0.0 copy-start
  0.6 0.0 copy-start.1
  0.7 0.0 copy-start.2
  0.7 77.5 %decode.1.res_hbm = bf16[4096,64,128]{2,1,0:T(8,128)(2,1)} custom-call(s32[8]{0:T(128)} %pos_hbm.3, bf16[8,1024]{1,0:T(8,128)(2,1)} %x_hbm.1, bf16[2,1024]{1,0:T(2,128)(2,1)} %an_hbm.1, bf16[2,128]{1,0:T(2,128)(2,1)} %qn_hbm.1, bf16[2,128]{1,0:T(2,128)(2,1)} %kn_hbm.1, bf16[2,1024]{1,0:T(2,128)(2,1)} %mn_hbm.1, bf16[2,64,2048]{2,1,0:T(8,128)(2,1)} %wq_hbm.1, ...), custom_call_target="tpu_custom_call" | custom-call | tf_op jit(solution)/shard_map/decode/pallas_call | solution.py:531
  78.2 0.0 copy-done
  78.2 0.0 copy-done.1
  78.2 0.0 copy-done.2
  78.2 3.9 %place.1 = (bf16[8,1024]{1,0:T(8,128)(2,1)}, bf16[2,8,1024,128]{3,2,1,0:T(8,128)(2,1)}, bf16[2,8,1024,128]{3,2,1,0:T(8,128)(2,1)}) custom-call(s32[8]{0:T(128)S(1)} %copy-done.2, bf16[4096,64,128]{2,1,0:T(8,128)(2,1)} %decode.1.res_hbm, bf16[2,8,1024,128]{3,2,1,0:T(8,128)(2,1)S(1)} %bitcast.5, bf16[2,8,1024,128]{3,2,1,0:T(8,128)(2,1)S(1)} %bitcast.7), custom_call_target="tpu_custom_call" | custom-call | tf_op jit(solution)/shard_map/place/pallas_call | solution.py:542
Async XLA Ops:
  0.6 77.5 %copy-start = (bf16[2,8,128,8,128]{4,3,2,1,0:T(8,128)(2,1)S(1)}, bf16[2,8,128,8,128]{4,3,2,1,0:T(8,128)(2,1)}, u32[]{:S(2)}) copy-start(bf16[2,8,128,8,128]{4,3,2,1,0:T(8,128)(2,1)} %param.17) | copy-start | bytes 12582916
  0.6 77.5 %copy-start.1 = (bf16[2,8,128,8,128]{4,3,2,1,0:T(8,128)(2,1)S(1)}, bf16[2,8,128,8,128]{4,3,2,1,0:T(8,128)(2,1)}, u32[]{:S(2)}) copy-start(bf16[2,8,128,8,128]{4,3,2,1,0:T(8,128)(2,1)} %param.18) | copy-start | bytes 12582916
  0.7 77.5 %copy-start.2 = (s32[8]{0:T(128)S(1)}, s32[8]{0:T(128)}, u32[]{:S(2)}) copy-start(s32[8]{0:T(128)} %pos_hbm.3) | copy-start | bytes 100

commit v10 on v9

--- a/solution.py
+++ b/solution.py
@@ -331,12 +331,6 @@
                 vs[pl.ds(2 * h + g, tok, stride=qh), :] = v
             kro[pl.ds(h, tok, stride=kh), :] = k
             vro[pl.ds(h, tok, stride=kh), :] = v
-        krow_ref[l] = kro[...].astype(BF16)
-        vrow_ref[l] = vro[...].astype(BF16)
-        outs.append(pltpu.make_async_copy(krow_ref.at[l], res_hbm.at[1 + 2 * l], out_sem))
-        outs.append(pltpu.make_async_copy(vrow_ref.at[l], res_hbm.at[2 + 2 * l], out_sem))
-        outs[-2].start()
-        outs[-1].start()
         slot = slot_ref[...]
         scale = HEAD_DIM ** -0.5
         for n0 in range(0, tok, 8):
@@ -357,12 +351,21 @@
         for h in range(qh):
             og[l, z, :, h * HEAD_DIM:(h + 1) * HEAD_DIM] = os_[pl.ds(h, tok, stride=qh), :].astype(BF16)
 
+    def flush_rows(l):
+        krow_ref[l] = kro[...].astype(BF16)
+        vrow_ref[l] = vro[...].astype(BF16)
+        outs.append(pltpu.make_async_copy(krow_ref.at[l], res_hbm.at[1 + 2 * l], out_sem))
+        outs.append(pltpu.make_async_copy(vrow_ref.at[l], res_hbm.at[2 + 2 * l], out_sem))
+        outs[-2].start()
+        outs[-1].start()
+
     def own_rows(l):
         background(l, "att_done")
         of_fin()
         r = jnp.dot(og[l, z], wof[0].reshape(og.shape[-1], dm), preferred_element_type=F32)
         x1r[z] = (xg[l, z].astype(F32) + r).astype(BF16)
         spread(lambda zt: x1r.at[z], x1r.at[z], l, 3)
+        flush_rows(l)
         background(l, "x1_sent")
         wait_bytes(wd.at[l], down_recv.at[l])
         w_fin(l, "g")
@@ -372,6 +375,7 @@
 
     def gathered_rows(l):
         spread(lambda zt: og.at[l, z], og.at[l, z], l, 2)
+        flush_rows(l)
         background(l, "o_sent")
         w_fin(l, "o")
         arrived(og, l, 2)

time: 82.3 us -> 82.6 us (level)
  no operation moved by 1% of the time
where the time goes in v10:
time: 82.6 us; the launch traced here: 82.4 us
  Pallas kernels  81.7 us (99%)
    pallas_call x1, Pallas kernels, device_fn(): pl.pallas_call(functools.partial(decode_kernel, cfg), name='decode', out_...  77.8 us
    pallas_call x1, Pallas kernels, device_fn(): pl.pallas_call(functools.partial(place_rows, layers, tok, kh), name='plac...  3.92 us

profile of v10, /device:TPU:21, one launch (start us, length us, event | category | flops | bytes accessed | tf_op | source)
XLA Modules:
  0.0 82.4 jit_solution(6305080969153640630)
XLA Ops:
  0.6 0.0 copy-start
  0.6 0.0 copy-start.1
  0.7 0.0 copy-start.2
  0.7 77.8 %decode.1.res_hbm = bf16[4096,64,128]{2,1,0:T(8,128)(2,1)} custom-call(s32[8]{0:T(128)} %pos_hbm.3, bf16[8,1024]{1,0:T(8,128)(2,1)} %x_hbm.1, bf16[2,1024]{1,0:T(2,128)(2,1)} %an_hbm.1, bf16[2,128]{1,0:T(2,128)(2,1)} %qn_hbm.1, bf16[2,128]{1,0:T(2,128)(2,1)} %kn_hbm.1, bf16[2,1024]{1,0:T(2,128)(2,1)} %mn_hbm.1, bf16[2,64,2048]{2,1,0:T(8,128)(2,1)} %wq_hbm.1, ...), custom_call_target="tpu_custom_call" | custom-call | tf_op jit(solution)/shard_map/decode/pallas_call | solution.py:535
  78.5 0.0 copy-done
  78.5 0.0 copy-done.1
  78.5 0.0 copy-done.2
  78.5 3.9 %place.1 = (bf16[8,1024]{1,0:T(8,128)(2,1)}, bf16[2,8,1024,128]{3,2,1,0:T(8,128)(2,1)}, bf16[2,8,1024,128]{3,2,1,0:T(8,128)(2,1)}) custom-call(s32[8]{0:T(128)S(1)} %copy-done.2, bf16[4096,64,128]{2,1,0:T(8,128)(2,1)} %decode.1.res_hbm, bf16[2,8,1024,128]{3,2,1,0:T(8,128)(2,1)S(1)} %bitcast.5, bf16[2,8,1024,128]{3,2,1,0:T(8,128)(2,1)S(1)} %bitcast.7), custom_call_target="tpu_custom_call" | custom-call | tf_op jit(solution)/shard_map/place/pallas_call | solution.py:546
Async XLA Ops:
  0.6 77.9 %copy-start = (bf16[2,8,128,8,128]{4,3,2,1,0:T(8,128)(2,1)S(1)}, bf16[2,8,128,8,128]{4,3,2,1,0:T(8,128)(2,1)}, u32[]{:S(2)}) copy-start(bf16[2,8,128,8,128]{4,3,2,1,0:T(8,128)(2,1)} %param.17) | copy-start | bytes 12582916
  0.6 77.9 %copy-start.1 = (bf16[2,8,128,8,128]{4,3,2,1,0:T(8,128)(2,1)S(1)}, bf16[2,8,128,8,128]{4,3,2,1,0:T(8,128)(2,1)}, u32[]{:S(2)}) copy-start(bf16[2,8,128,8,128]{4,3,2,1,0:T(8,128)(2,1)} %param.18) | copy-start | bytes 12582916
  0.7 77.9 %copy-start.2 = (s32[8]{0:T(128)S(1)}, s32[8]{0:T(128)}, u32[]{:S(2)}) copy-start(s32[8]{0:T(128)} %pos_hbm.3) | copy-start | bytes 100
